TPU v7x, 32 devices: a whole 2x2x4 slice. The times are simulated.
32 devices in a mesh: dp: 4 (over x, y), x: 8 (over z, core).
Axes of the slice: x: 2, y: 2, z: 4, core: 2. Of those that a mesh axis runs over, the one named last changes fastest.
Arguments:
- start_pos: int32 [512], P('dp'), parts along dimension 0
- hidden_in: bfloat16 [4, 512, 2560], P(None, ('dp', 'x')), parts along dimension 1
- k_cache: bfloat16 [512, 256, 8, 128], P('dp', None, 'x'), parts along dimension 0
- v_cache: bfloat16 [512, 256, 8, 128], P('dp', None, 'x'), parts along dimension 0
- attn_norm: bfloat16 [2560], replicated
- w_q: bfloat16 [2560, 4096], replicated
- w_k: bfloat16 [2560, 1024], replicated
- w_v: bfloat16 [2560, 1024], replicated
- q_norm: bfloat16 [128], replicated
- k_norm: bfloat16 [128], replicated
- w_o: bfloat16 [4096, 2560], replicated
- mlp_norm: bfloat16 [2560], replicated
- w_gate: bfloat16 [2560, 9728], replicated
- w_up: bfloat16 [2560, 9728], replicated
- w_down: bfloat16 [9728, 2560], replicated
Outputs:
- output 1: bfloat16 [4, 512, 2560], P(None, ('dp', 'x')), parts along dimension 1
- output 2: bfloat16 [512, 256, 8, 128], P(('dp', 'x')), parts along dimension 0
- output 3: bfloat16 [512, 256, 8, 128], P(('dp', 'x')), parts along dimension 0
There are 4 independent parts. A program takes and returns all parts, laid end to end along the dimension named above; an argument that names none is the same for every part.
All inputs are finite; a program needn't handle non-finite values.
Results may differ from a plain program's by a relative error of at most 0.010418.
Values are sent between devices in bfloat16 or wider.
A program may use at most 1 GiB of HBM per device.

v0:
```python
import jax
import jax.numpy as jnp
from jax import lax
from jax.experimental import pallas as pl
from jax.experimental.pallas import tpu as pltpu
from jax.sharding import PartitionSpec as P


EPS = 1e-6
THETA = 1000000.0
N_DEV = 8
CHUNKS = ((0, 6), (6, 12), (12, 16))


def rms_norm(values, gain_vec):
    values32 = values.astype(jnp.float32)
    inv_rms = lax.rsqrt(jnp.mean(values32 * values32, axis=-1, keepdims=True) + EPS)
    return values32 * inv_rms * gain_vec.astype(jnp.float32)


def rotary(values, positions):
    head_dim = values.shape[-1]
    half_dim = head_dim // 2
    inv_freq = jnp.power(THETA, -jnp.arange(half_dim, dtype=jnp.float32) * 2.0 / head_dim)
    angles = positions.astype(jnp.float32)[..., None, None] * inv_freq
    cos_part = jnp.cos(angles)
    sin_part = jnp.sin(angles)
    first_half = values[..., :half_dim]
    second_half = values[..., half_dim:]
    return jnp.concatenate([first_half * cos_part - second_half * sin_part, second_half * cos_part + first_half * sin_part], axis=-1)


def project(hidden, positions, attn_norm, w_q, w_k, w_v, q_norm, k_norm):
    n_steps, num_rows = hidden.shape[0], hidden.shape[1]
    head_dim = q_norm.shape[0]
    normed = rms_norm(hidden, attn_norm).astype(jnp.bfloat16)
    queries = jnp.einsum('sbd,de->sbe', normed, w_q, preferred_element_type=jnp.float32).reshape(n_steps, num_rows, -1, head_dim)
    keys_new = jnp.einsum('sbd,de->sbe', normed, w_k, preferred_element_type=jnp.float32).reshape(n_steps, num_rows, -1, head_dim)
    values_new = jnp.einsum('sbd,de->sbe', normed, w_v, preferred_element_type=jnp.float32).reshape(n_steps, num_rows, -1, head_dim)
    queries = rotary(rms_norm(queries, q_norm), positions).astype(jnp.bfloat16)
    keys_new = rotary(rms_norm(keys_new, k_norm), positions).astype(jnp.bfloat16)
    return queries, keys_new, values_new.astype(jnp.bfloat16)


def finish(hidden, attended, w_o, mlp_norm, w_gate, w_up, w_down):
    n_steps, num_rows = attended.shape[0], attended.shape[1]
    flat_attn = attended.reshape(n_steps, num_rows, -1)
    attn_out = jnp.einsum('sbe,ed->sbd', flat_attn, w_o, preferred_element_type=jnp.float32)
    residual = (hidden.astype(jnp.float32) + attn_out).astype(jnp.bfloat16)
    normed = rms_norm(residual, mlp_norm).astype(jnp.bfloat16)
    gate_val = jnp.einsum('sbd,df->sbf', normed, w_gate, preferred_element_type=jnp.float32)
    up_val = jnp.einsum('sbd,df->sbf', normed, w_up, preferred_element_type=jnp.float32)
    activated = (jax.nn.silu(gate_val) * up_val).astype(jnp.bfloat16)
    down_val = jnp.einsum('sbf,fd->sbd', activated, w_down, preferred_element_type=jnp.float32)
    return (residual.astype(jnp.float32) + down_val).astype(jnp.bfloat16)


NT = (((1,), (1,)), ((), ()))
NN = (((1,), (0,)), ((), ()))


def attend_one(pack, keys, values, pos):
    q = pack[:16]
    new_keys, new_values = pack[16:20], pack[20:24]
    scale = q.shape[-1] ** -0.5
    old = lax.dot_general(q, keys, NT, preferred_element_type=jnp.float32) * scale
    new = lax.dot_general(q, new_keys, NT, preferred_element_type=jnp.float32) * scale
    slot = lax.broadcasted_iota(jnp.int32, old.shape, 1)
    old = jnp.where(slot < pos, old, -jnp.inf)
    step = lax.broadcasted_iota(jnp.int32, new.shape, 0) // 4
    new = jnp.where(lax.broadcasted_iota(jnp.int32, new.shape, 1) <= step, new, -jnp.inf)
    peak = jnp.maximum(jnp.max(old, axis=-1, keepdims=True), jnp.max(new, axis=-1, keepdims=True))
    old_w, new_w = jnp.exp(old - peak), jnp.exp(new - peak)
    total = jnp.sum(old_w, axis=-1, keepdims=True) + jnp.sum(new_w, axis=-1, keepdims=True)
    mixed = lax.dot_general(old_w.astype(jnp.bfloat16), values, NN, preferred_element_type=jnp.float32)
    mixed = mixed + lax.dot_general(new_w.astype(jnp.bfloat16), new_values, NN, preferred_element_type=jnp.float32)
    return (mixed / total).astype(jnp.bfloat16)


def remote_attend(scalars, blocks, packs, offset):
    n_seq, num_slots, head_dim = blocks[0].shape[1:]

    def body(scal_ref, *refs):
        block_refs, pack_refs, out_refs = refs[:N_DEV], refs[N_DEV:2 * N_DEV], refs[2 * N_DEV:]
        seq = pl.program_id(0)
        me = scal_ref[128]
        for k in range(N_DEV):
            pos = scal_ref[(me ^ k) * 16 + offset + seq]
            out_refs[k][0] = attend_one(pack_refs[k][0], block_refs[k][0, 0], block_refs[k][1, 0], pos)

    return pl.pallas_call(
        body,
        grid_spec=pltpu.PrefetchScalarGridSpec(
            num_scalar_prefetch=1,
            grid=(n_seq,),
            in_specs=[pl.BlockSpec((2, 1, num_slots, head_dim), lambda i, s: (0, i, 0, 0))] * N_DEV
            + [pl.BlockSpec((1, 24, head_dim), lambda i, s: (i, 0, 0))] * N_DEV,
            out_specs=[pl.BlockSpec((1, 16, head_dim), lambda i, s: (i, 0, 0))] * N_DEV,
        ),
        out_shape=[jax.ShapeDtypeStruct((n_seq, 16, head_dim), jnp.bfloat16)] * N_DEV,
        cost_estimate=pl.CostEstimate(flops=n_seq * 40_000_000, bytes_accessed=n_seq * 1_100_000, transcendentals=0),
        name="remote_attend",
    )(scalars, *blocks, *packs)


def settle(scalars, blocks, new_keys, new_values, pack, caches, offset, num_seqs):
    n_seq, num_slots, head_dim = blocks[0].shape[1:]
    with_attn, in_place = pack is not None, caches is not None
    n_steps = new_keys.shape[1]

    def body(scal_ref, *refs):
        refs = list(refs)
        block_refs = [refs.pop(0) for _ in range(N_DEV)]
        new_refs = [refs.pop(0) for _ in range(2)]
        pack_ref = refs.pop(0) if with_attn else None
        if in_place:
            refs = refs[2:]
        cache_refs = [refs.pop(0) for _ in range(2)]
        out_ref = refs.pop(0) if with_attn else None
        spread_refs = refs
        me = scal_ref[128]
        pos = scal_ref[me * 16 + offset + pl.program_id(0)]
        for kind in range(2):
            spread = spread_refs[kind]
            for k in range(N_DEV):
                spread[pl.ds(me ^ k, num_slots, stride=N_DEV), :] = block_refs[k][kind, 0].astype(jnp.float32)
            cache_refs[kind][0] = spread[...].reshape(num_slots, N_DEV, head_dim).astype(jnp.bfloat16)
            for step in range(n_steps):
                cache_refs[kind][0, pos + step] = new_refs[kind][0, step]
        if with_attn:
            for k in range(N_DEV):
                out_ref[0, me ^ k] = attend_one(pack_ref[0, me ^ k], block_refs[k][0, 0], block_refs[k][1, 0], pos)

    cache_block = pl.BlockSpec((1, num_slots, N_DEV, head_dim), lambda i, s: (offset + i, 0, 0, 0))
    in_specs = [pl.BlockSpec((2, 1, num_slots, head_dim), lambda i, s: (0, i, 0, 0))] * N_DEV
    in_specs += [pl.BlockSpec((1, n_steps, N_DEV, head_dim), lambda i, s: (i, 0, 0, 0))] * 2
    args = [scalars, *blocks, new_keys, new_values]
    if with_attn:
        in_specs.append(pl.BlockSpec((1, N_DEV, 24, head_dim), lambda i, s: (i, 0, 0, 0)))
        args.append(pack)
    aliases = {}
    if in_place:
        aliases = {len(args): 0, len(args) + 1: 1}
        in_specs += [pl.BlockSpec(memory_space=pl.ANY)] * 2
        args += list(caches)
    cache_shape = jax.ShapeDtypeStruct((num_seqs, num_slots, N_DEV, head_dim), jnp.bfloat16)
    out_specs, out_shape = [cache_block] * 2, [cache_shape] * 2
    if with_attn:
        out_specs.append(pl.BlockSpec((1, N_DEV, 16, head_dim), lambda i, s: (i, 0, 0, 0)))
        out_shape.append(jax.ShapeDtypeStruct((n_seq, N_DEV, 16, head_dim), jnp.bfloat16))
    return pl.pallas_call(
        body,
        grid_spec=pltpu.PrefetchScalarGridSpec(
            num_scalar_prefetch=1,
            grid=(n_seq,),
            in_specs=in_specs,
            out_specs=out_specs,
            scratch_shapes=[pltpu.VMEM((num_slots * N_DEV, head_dim), jnp.float32)] * 2,
        ),
        out_shape=out_shape,
        input_output_aliases=aliases,
        cost_estimate=pl.CostEstimate(flops=n_seq * 60_000_000, bytes_accessed=n_seq * 2_200_000, transcendentals=0),
        name="settle",
    )(*args)


def solution(mesh):
    row_spec = P(None, ('dp', 'x'), None)
    cache_in = P('dp', None, 'x', None)
    cache_out = P(('dp', 'x'), None, None, None)

    def swap(value, k):
        if k == 0:
            return value
        return lax.ppermute(value, 'x', [(i, i ^ k) for i in range(N_DEV)])

    order = (2, 3, 1, 4, 5, 6, 7)

    def swap_all(values):
        got = {0: values[0]}
        for k in order:
            got[k] = swap(values[k], k)
        return [got[k] for k in range(N_DEV)]

    def local_run(start_pos, hidden_in, k_heads, v_heads, attn_norm, w_q, w_k, w_v, q_norm, k_norm, w_o, mlp_norm, w_gate, w_up, w_down):
        me = lax.axis_index('x')
        n_steps, num_rows = hidden_in.shape[:2]
        num_slots, head_dim = k_heads.shape[1], k_heads.shape[3]
        my_pos = lax.dynamic_slice_in_dim(start_pos, me * num_rows, num_rows)
        scalars = jnp.concatenate([start_pos, me[None].astype(jnp.int32)])
        partners = [me ^ k for k in range(N_DEV)]
        xor_heads = jnp.stack(partners)

        def pieces(caches, chunk):
            lo, hi = chunk
            keys, values = (c.reshape(N_DEV * num_rows, num_slots, head_dim) for c in caches)
            return [
                jnp.stack([lax.dynamic_slice_in_dim(c, p * num_rows + lo, hi - lo) for c in (keys, values)])
                for p in partners
            ]

        caches = (k_heads, v_heads)
        a, b, r = CHUNKS
        got_a = swap_all(pieces(caches, a))
        positions = my_pos[None, :] + jnp.arange(n_steps)[:, None]
        queries, keys_new, values_new = project(hidden_in, positions, attn_norm, w_q, w_k, w_v, q_norm, k_norm)
        q_rows = jnp.transpose(queries.reshape(n_steps, num_rows, N_DEV, -1, head_dim), (1, 2, 0, 3, 4)).reshape(num_rows, N_DEV, -1, head_dim)
        k_rows = jnp.transpose(keys_new, (1, 2, 0, 3))
        v_rows = jnp.transpose(values_new, (1, 2, 0, 3))
        pack = jnp.concatenate([q_rows, k_rows, v_rows], axis=2)
        knat, vnat = jnp.swapaxes(keys_new, 0, 1), jnp.swapaxes(values_new, 0, 1)
        pack_r = jnp.take(jnp.swapaxes(pack[r[0]:r[1]], 0, 1), xor_heads, axis=0)
        got_q = swap_all([pack_r[k] for k in range(N_DEV)])
        *caches, pack = lax.optimization_barrier((*caches, pack))
        got_b = swap_all(pieces(caches, b))
        blocks_r = pieces(caches, r)
        o_r = remote_attend(scalars, blocks_r, got_q, r[0])
        got_o = swap_all(o_r)
        blocks_r, _ = lax.optimization_barrier((blocks_r, o_r))
        got_r = swap_all(blocks_r)
        k_out, v_out, o_a = settle(scalars, got_a, knat[a[0]:a[1]], vnat[a[0]:a[1]], pack[a[0]:a[1]], None, a[0], num_rows)
        k_out, v_out, o_b = settle(scalars, got_b, knat[b[0]:b[1]], vnat[b[0]:b[1]], pack[b[0]:b[1]], (k_out, v_out), b[0], num_rows)
        o_r = jnp.swapaxes(jnp.take(jnp.stack(got_o), xor_heads, axis=0), 0, 1)
        attended = jnp.concatenate([o_a, o_b, o_r], axis=0).reshape(num_rows, N_DEV, n_steps, -1, head_dim)
        attended = jnp.transpose(attended, (2, 0, 1, 3, 4)).reshape(n_steps, num_rows, -1)
        out_hidden = finish(hidden_in, attended, w_o, mlp_norm, w_gate, w_up, w_down)
        k_out, v_out = settle(scalars, got_r, knat[r[0]:r[1]], vnat[r[0]:r[1]], None, (k_out, v_out), r[0], num_rows)
        return out_hidden, k_out, v_out

    return jax.shard_map(local_run, mesh=mesh, in_specs=(P('dp'), row_spec, cache_in, cache_in) + (P(),) * 11, out_specs=(row_spec, cache_out, cache_out), check_vma=False)
```

profile of v0, /device:TPU:17, one launch (start us, length us, event | category | flops | bytes accessed | tf_op | source)
XLA Modules:
  0.0 510.1 jit_solution(4524105340867086235)
XLA Ops:
  2.5 3.7 fusion.47
  7.0 3.7 fusion.20
  12.0 9.2 %fusion.8 = f32[4,16,4096]{2,1,0:T(8,128)S(1)} fusion(bf16[2560,4096]{1,0:T(8,128)(2,1)} %param.20, bf16[4,16,2560]{2,1,0:T(8,128)(2,1)S(1)} %copy-done, f32[2560]{0:T(1024)S(1)} %convert_element_type.53, f32[4,16]{1,0:T(4,128)S(1)} %add_rsqrt_fusion.3), kind=kOutput, calls=%fused_computation.10 | convolution fusion | flops 1342832640 | bytes 22358272 | tf_op jit(solution)/shard_map/sbd,de->sbe/dot_general | solution.py:37
  31.1 3.5 dynamic-slice_bitcast_fusion
  42.0 4.6 dynamic-slice_bitcast_fusion.16
  64.7 11.6 %remote_attend.1 = (bf16[4,16,128]{2,1,0:T(8,128)(2,1)}, bf16[4,16,128]{2,1,0:T(8,128)(2,1)}, bf16[4,16,128]{2,1,0:T(8,128)(2,1)}, bf16[4,16,128]{2,1,0:T(8,128)...) custom-call(s32[129]{0:T(256)} %pad_add_fusion.scal_ref, ...), custom_call_target="tpu_custom_call" | custom-call | flops 160000000 | bytes 4400000 | tf_op jit(solution)/shard_map/remote_attend/pallas_call | solution.py:91
  81.3 17.2 %collective-permute-done.22 = bf16[4,16,128]{2,1,0:T(8,128)(2,1)S(1)} collective-permute-done((bf16[4,16,128]{2,1,0:T(8,128)(2,1)}, bf16[4,16,128]{2,1,0:T(8,128)(2,1)S(1)}, u32[]{:S(2)}, u32[]{:S(2)}) %collective-permute-start.22) | collective-permute-done | bytes 16416 | tf_op jit(solution)/shard_map/ppermute | solution.py:175
  118.7 5.2 %collective-permute-start.2 = (bf16[2,6,256,128]{3,2,1,0:T(8,128)(2,1)S(1)}, bf16[2,6,256,128]{3,2,1,0:T(8,128)(2,1)}, u32[]{:S(2)}, u32[]{:S(2)}) collective-permute-start(bf16[2,6,256,128]{3,2,1,0:T(8,128)(2,1)S(1)} %pad_maximum_fusion.3), channel_id=1, source_target_pairs={{0,3},{1,2},{2,1},{3,0},{4,7},{5,6},{6,5},{7,4},{8,11},{9,10},{10,... | collective-permute-start | bytes 2359304 | tf_op jit(solution)/shard_map/ppermute | solution.py:175
  128.4 29.0 %collective-permute-done.2.refs_3_ = bf16[2,6,256,128]{3,2,1,0:T(8,128)(2,1)} collective-permute-done((bf16[2,6,256,128]{3,2,1,0:T(8,128)(2,1)S(1)}, bf16[2,6,256,128]{3,2,1,0:T(8,128)(2,1)}, u32[]{:S(2)}, u32[]{:S(2)}) %collective-permute-start.2) | collective-permute-done | bytes 786464 | tf_op jit(solution)/shard_map/ppermute | solution.py:175
  159.9 47.8 %collective-permute-done.3.refs_4_ = bf16[2,6,256,128]{3,2,1,0:T(8,128)(2,1)} collective-permute-done((bf16[2,6,256,128]{3,2,1,0:T(8,128)(2,1)S(1)}, bf16[2,6,256,128]{3,2,1,0:T(8,128)(2,1)}, u32[]{:S(2)}, u32[]{:S(2)}) %collective-permute-start.3) | collective-permute-done | bytes 786464 | tf_op jit(solution)/shard_map/ppermute | solution.py:175
  207.7 3.7 collective-permute-start.10
  211.4 47.6 %collective-permute-done.4.refs_5_ = bf16[2,6,256,128]{3,2,1,0:T(8,128)(2,1)S(1)} collective-permute-done((bf16[2,6,256,128]{3,2,1,0:T(8,128)(2,1)S(1)}, bf16[2,6,256,128]{3,2,1,0:T(8,128)(2,1)S(1)}, u32[]{:S(2)}, u32[]{:S(2)}) %collective-permute-start.4) | collective-permute-done | bytes 786464 | tf_op jit(solution)/shard_map/ppermute | solution.py:175
  262.4 47.2 %collective-permute-done.5.refs_6_ = bf16[2,6,256,128]{3,2,1,0:T(8,128)(2,1)S(1)} collective-permute-done((bf16[2,6,256,128]{3,2,1,0:T(8,128)(2,1)S(1)}, bf16[2,6,256,128]{3,2,1,0:T(8,128)(2,1)S(1)}, u32[]{:S(2)}, u32[]{:S(2)}) %collective-permute-start.5) | collective-permute-done | bytes 786464 | tf_op jit(solution)/shard_map/ppermute | solution.py:175
  311.8 17.1 %collective-permute-done.6.refs_7_ = bf16[2,6,256,128]{3,2,1,0:T(8,128)(2,1)S(1)} collective-permute-done((bf16[2,6,256,128]{3,2,1,0:T(8,128)(2,1)S(1)}, bf16[2,6,256,128]{3,2,1,0:T(8,128)(2,1)S(1)}, u32[]{:S(2)}, u32[]{:S(2)}) %collective-permute-start.6) | collective-permute-done | bytes 786464 | tf_op jit(solution)/shard_map/ppermute | solution.py:175
  330.4 18.9 %settle.3 = (bf16[16,256,8,128]{3,2,1,0:T(8,128)(2,1)}, bf16[16,256,8,128]{3,2,1,0:T(8,128)(2,1)}, bf16[6,8,16,128]{3,2,1,0:T(8,128)(2,1)}) custom-call(s32[129]{0:T(256)} %pad_add_fusion.scal_ref, bf16[2,6,256,128]{3,2,1,0:T(8,128)(2,1)} %pad_maximum_fusion.refs_0_, bf16[2,6,256,128]{3,2,1,0:T(8,128)(2,1)} %collective-permute-done.refs_1_, ...), custom_call_target="tpu_custom_call" | custom-call | flops 360000000 | bytes 13200000 | tf_op jit(solution)/shard_map/settle/pallas_call | solution.py:151
  349.6 10.8 %collective-permute-done.11.refs_5_ = bf16[2,6,256,128]{3,2,1,0:T(8,128)(2,1)} collective-permute-done((bf16[2,6,256,128]{3,2,1,0:T(8,128)(2,1)}, bf16[2,6,256,128]{3,2,1,0:T(8,128)(2,1)}, u32[]{:S(2)}, u32[]{:S(2)}) %collective-permute-start.11) | collective-permute-done | bytes 786464 | tf_op jit(solution)/shard_map/ppermute | solution.py:175
  361.2 16.0 %collective-permute-done.12.refs_6_ = bf16[2,6,256,128]{3,2,1,0:T(8,128)(2,1)} collective-permute-done((bf16[2,6,256,128]{3,2,1,0:T(8,128)(2,1)}, bf16[2,6,256,128]{3,2,1,0:T(8,128)(2,1)}, u32[]{:S(2)}, u32[]{:S(2)}) %collective-permute-start.12) | collective-permute-done | bytes 786464 | tf_op jit(solution)/shard_map/ppermute | solution.py:175
  377.2 30.5 %collective-permute-done.13.refs_7_ = bf16[2,6,256,128]{3,2,1,0:T(8,128)(2,1)} collective-permute-done((bf16[2,6,256,128]{3,2,1,0:T(8,128)(2,1)}, bf16[2,6,256,128]{3,2,1,0:T(8,128)(2,1)}, u32[]{:S(2)}, u32[]{:S(2)}) %collective-permute-start.13) | collective-permute-done | bytes 786464 | tf_op jit(solution)/shard_map/ppermute | solution.py:175
  407.7 19.3 %settle.4 = (bf16[16,256,8,128]{3,2,1,0:T(8,128)(2,1)}, bf16[16,256,8,128]{3,2,1,0:T(8,128)(2,1)}, bf16[6,8,16,128]{3,2,1,0:T(8,128)(2,1)}) custom-call(s32[129]{0:T(256)} %pad_add_fusion.scal_ref, bf16[2,6,256,128]{3,2,1,0:T(8,128)(2,1)} %pad_maximum_fusion.9.refs_0_, ...), custom_call_target="tpu_custom_call", output_to_operand_aliasing={{0}: (12, {}), {1}: (13, {})} | custom-call | flops 360000000 | bytes 13200000 | tf_op jit(solution)/shard_map/settle/pallas_call | solution.py:151
  428.7 9.0 %multiply_reduce_fusion = (f32[4,16]{1,0:T(4,128)S(1)}, f32[4,16,2560]{2,1,0:T(8,128)S(1)}) fusion(bf16[4,16,4096]{2,1,0:T(8,128)(2,1)S(1)} %reshape.554, bf16[4096,2560]{1,0:T(8,128)(2,1)} %param.25, bf16[4,16,2560]{2,1,0:T(8,128)(2,1)S(1)} %copy-done), kind=kOutput, calls=%fused_computation.59 | convolution fusion | flops 1343160320 | bytes 22479104 | tf_op jit(solution)/shard_map/sbe,ed->sbd/dot_general | solution.py:48
  437.7 19.6 %fusion.4 = f32[4,16,9728]{2,1,0:T(8,128)S(1)} fusion(bf16[2560,9728]{1,0:T(8,128)(2,1)} %param.27, f32[4,16,2560]{2,1,0:T(8,128)S(1)} %get-tuple-element.128, f32[2560]{0:T(1024)S(1)} %convert_element_type.62, f32[4,16]{1,0:T(4,128)S(1)} %add_rsqrt_fusion.2), kind=kOutput, calls=%fused_computation.6 | convolution fusion | flops 3188162560 | bytes 52963584 | tf_op jit(solution)/shard_map/sbd,df->sbf/dot_general | solution.py:51
  457.6 34.9 %fusion.30 = bf16[4,16,2560]{2,1,0:T(8,128)(2,1)} fusion(f32[4,16,2560]{2,1,0:T(8,128)S(1)} %get-tuple-element.128, bf16[9728,2560]{1,0:T(8,128)(2,1)} %param.29, bf16[2560,9728]{1,0:T(8,128)(2,1)} %param.28, f32[4,16,9728]{2,1,0:T(8,128)S(1)} %fusion.4, f32[2560]{0:T(1024)S(1)} %convert_element_type.62, f32[4,16]{1,0:T(4,128)S(1)} %add_rsqrt_fusion.2), kind=kOutput, calls=%fused_computation.20 | convolution fusion | flops 6379896832 | bytes 103098624 | tf_op jit(solution)/shard_map/sbf,fd->sbd/dot_general | solution.py:54
  493.8 9.5 %collective-permute-done.34.refs_7_ = bf16[2,4,256,128]{3,2,1,0:T(8,128)(2,1)} collective-permute-done((bf16[2,4,256,128]{3,2,1,0:T(8,128)(2,1)}, bf16[2,4,256,128]{3,2,1,0:T(8,128)(2,1)}, u32[]{:S(2)}, u32[]{:S(2)}) %collective-permute-start.34) | collective-permute-done | bytes 524320 | tf_op jit(solution)/shard_map/ppermute | solution.py:175
  503.3 6.6 %settle.5 = (bf16[16,256,8,128]{3,2,1,0:T(8,128)(2,1)}, bf16[16,256,8,128]{3,2,1,0:T(8,128)(2,1)}) custom-call(s32[129]{0:T(256)} %pad_add_fusion.scal_ref, bf16[2,4,256,128]{3,2,1,0:T(8,128)(2,1)} %pad_maximum_fusion.17.refs_0_, bf16[2,4,256,128]{3,2,1,0:T(8,128)(2,1)} %collective-permute-done.28.refs_1_, ...), custom_call_target="tpu_custom_call", output_to_operand_aliasing={{0}: (11, {}), {1}: (12, {})} | custom-call | flops 240000000 | bytes 8800000 | tf_op jit(solution)/shard_map/settle/pallas_call | solution.py:151
  (182 shorter events, 82.5 us)
Async XLA Ops:
  27.1 33.1 %collective-permute-start.16 = (bf16[4,24,128]{2,1,0:T(8,128)(2,1)}, bf16[4,24,128]{2,1,0:T(8,128)(2,1)S(1)}, u32[]{:S(2)}, u32[]{:S(2)}) collective-permute-start(bf16[4,24,128]{2,1,0:T(8,128)(2,1)} %get-tuple-element.117), channel_id=1, source_target_pairs={{0,3},{1,2},{2,1},{3,0},{4,7},{5,6},{6,5},{7,4},{8,11},{9,10},{10,... | collective-permute-start | bytes 73736 | tf_op jit(solution)/shard_map/ppermute | solution.py:175
  27.5 32.8 %collective-permute-start.17 = (bf16[4,24,128]{2,1,0:T(8,128)(2,1)}, bf16[4,24,128]{2,1,0:T(8,128)(2,1)}, u32[]{:S(2)}, u32[]{:S(2)}) collective-permute-start(bf16[4,24,128]{2,1,0:T(8,128)(2,1)} %get-tuple-element.116), channel_id=1, source_target_pairs={{0,4},{1,5},{2,6},{3,7},{4,0},{5,1},{6,2},{7,3},{8,12},{9,13},{10,... | collective-permute-start | bytes 73736 | tf_op jit(solution)/shard_map/ppermute | solution.py:175
  27.5 35.9 %collective-permute-start.18 = (bf16[4,24,128]{2,1,0:T(8,128)(2,1)}, bf16[4,24,128]{2,1,0:T(8,128)(2,1)}, u32[]{:S(2)}, u32[]{:S(2)}) collective-permute-start(bf16[4,24,128]{2,1,0:T(8,128)(2,1)} %get-tuple-element.115), channel_id=1, source_target_pairs={{0,5},{1,4},{2,7},{3,6},{4,1},{5,0},{6,3},{7,2},{8,13},{9,12},{10,... | collective-permute-start | bytes 73736 | tf_op jit(solution)/shard_map/ppermute | solution.py:175
  60.2 63.7 %collective-permute-start.7 = (bf16[2,6,256,128]{3,2,1,0:T(8,128)(2,1)}, bf16[2,6,256,128]{3,2,1,0:T(8,128)(2,1)}, u32[]{:S(2)}, u32[]{:S(2)}) collective-permute-start(bf16[2,6,256,128]{3,2,1,0:T(8,128)(2,1)} %pad_maximum_fusion.10), channel_id=1, source_target_pairs={{0,1},{1,0},{2,3},{3,2},{4,5},{5,4},{6,7},{7,6},{8,9},{9,8},{10,11... | collective-permute-start | bytes 2359304 | tf_op jit(solution)/shard_map/ppermute | solution.py:175
  60.4 63.6 %collective-permute-start.8 = (bf16[2,6,256,128]{3,2,1,0:T(8,128)(2,1)}, bf16[2,6,256,128]{3,2,1,0:T(8,128)(2,1)}, u32[]{:S(2)}, u32[]{:S(2)}) collective-permute-start(bf16[2,6,256,128]{3,2,1,0:T(8,128)(2,1)} %pad_maximum_fusion.11), channel_id=1, source_target_pairs={{0,2},{1,3},{2,0},{3,1},{4,6},{5,7},{6,4},{7,5},{8,10},{9,11},{10,... | collective-permute-start | bytes 2359304 | tf_op jit(solution)/shard_map/ppermute | solution.py:175
  63.5 62.1 %collective-permute-start = (bf16[2,6,256,128]{3,2,1,0:T(8,128)(2,1)}, bf16[2,6,256,128]{3,2,1,0:T(8,128)(2,1)}, u32[]{:S(2)}, u32[]{:S(2)}) collective-permute-start(bf16[2,6,256,128]{3,2,1,0:T(8,128)(2,1)} %pad_maximum_fusion.1), channel_id=1, source_target_pairs={{0,1},{1,0},{2,3},{3,2},{4,5},{5,4},{6,7},{7,6},{8,9},{9,8},{10,11... | collective-permute-start | bytes 2359304 | tf_op jit(solution)/shard_map/ppermute | solution.py:175
  64.1 62.9 %collective-permute-start.1 = (bf16[2,6,256,128]{3,2,1,0:T(8,128)(2,1)}, bf16[2,6,256,128]{3,2,1,0:T(8,128)(2,1)}, u32[]{:S(2)}, u32[]{:S(2)}) collective-permute-start(bf16[2,6,256,128]{3,2,1,0:T(8,128)(2,1)} %pad_maximum_fusion.2), channel_id=1, source_target_pairs={{0,2},{1,3},{2,0},{3,1},{4,6},{5,7},{6,4},{7,5},{8,10},{9,11},{10,... | collective-permute-start | bytes 2359304 | tf_op jit(solution)/shard_map/ppermute | solution.py:175
  118.7 38.7 %collective-permute-start.2 = (bf16[2,6,256,128]{3,2,1,0:T(8,128)(2,1)S(1)}, bf16[2,6,256,128]{3,2,1,0:T(8,128)(2,1)}, u32[]{:S(2)}, u32[]{:S(2)}) collective-permute-start(bf16[2,6,256,128]{3,2,1,0:T(8,128)(2,1)S(1)} %pad_maximum_fusion.3), channel_id=1, source_target_pairs={{0,3},{1,2},{2,1},{3,0},{4,7},{5,6},{6,5},{7,4},{8,11},{9,10},{10,... | collective-permute-start | bytes 2359304 | tf_op jit(solution)/shard_map/ppermute | solution.py:175
  123.9 83.8 %collective-permute-start.3 = (bf16[2,6,256,128]{3,2,1,0:T(8,128)(2,1)S(1)}, bf16[2,6,256,128]{3,2,1,0:T(8,128)(2,1)}, u32[]{:S(2)}, u32[]{:S(2)}) collective-permute-start(bf16[2,6,256,128]{3,2,1,0:T(8,128)(2,1)S(1)} %pad_maximum_fusion.4), channel_id=1, source_target_pairs={{0,4},{1,5},{2,6},{3,7},{4,0},{5,1},{6,2},{7,3},{8,12},{9,13},{10,... | collective-permute-start | bytes 2359304 | tf_op jit(solution)/shard_map/ppermute | solution.py:175
  123.9 135.1 %collective-permute-start.4 = (bf16[2,6,256,128]{3,2,1,0:T(8,128)(2,1)S(1)}, bf16[2,6,256,128]{3,2,1,0:T(8,128)(2,1)S(1)}, u32[]{:S(2)}, u32[]{:S(2)}) collective-permute-start(bf16[2,6,256,128]{3,2,1,0:T(8,128)(2,1)S(1)} %pad_maximum_fusion.5), channel_id=1, source_target_pairs={{0,5},{1,4},{2,7},{3,6},{4,1},{5,0},{6,3},{7,2},{8,13},{9,12},{10,... | collective-permute-start | bytes 2359304 | tf_op jit(solution)/shard_map/ppermute | solution.py:175
  125.6 184.1 %collective-permute-start.5 = (bf16[2,6,256,128]{3,2,1,0:T(8,128)(2,1)S(1)}, bf16[2,6,256,128]{3,2,1,0:T(8,128)(2,1)S(1)}, u32[]{:S(2)}, u32[]{:S(2)}) collective-permute-start(bf16[2,6,256,128]{3,2,1,0:T(8,128)(2,1)S(1)} %pad_maximum_fusion.6), channel_id=1, source_target_pairs={{0,6},{1,7},{2,4},{3,5},{4,2},{5,3},{6,0},{7,1},{8,14},{9,15},{10,... | collective-permute-start | bytes 2359304 | tf_op jit(solution)/shard_map/ppermute | solution.py:175
  127.0 201.9 %collective-permute-start.6 = (bf16[2,6,256,128]{3,2,1,0:T(8,128)(2,1)S(1)}, bf16[2,6,256,128]{3,2,1,0:T(8,128)(2,1)S(1)}, u32[]{:S(2)}, u32[]{:S(2)}) collective-permute-start(bf16[2,6,256,128]{3,2,1,0:T(8,128)(2,1)S(1)} %pad_maximum_fusion.7), channel_id=1, source_target_pairs={{0,7},{1,6},{2,5},{3,4},{4,3},{5,2},{6,1},{7,0},{8,15},{9,14},{10,... | collective-permute-start | bytes 2359304 | tf_op jit(solution)/shard_map/ppermute | solution.py:175
  157.3 192.0 %collective-permute-start.9 = (bf16[2,6,256,128]{3,2,1,0:T(8,128)(2,1)}, bf16[2,6,256,128]{3,2,1,0:T(8,128)(2,1)S(1)}, u32[]{:S(2)}, u32[]{:S(2)}) collective-permute-start(bf16[2,6,256,128]{3,2,1,0:T(8,128)(2,1)} %pad_maximum_fusion.12), channel_id=1, source_target_pairs={{0,3},{1,2},{2,1},{3,0},{4,7},{5,6},{6,5},{7,4},{8,11},{9,10},{10,... | collective-permute-start | bytes 2359304 | tf_op jit(solution)/shard_map/ppermute | solution.py:175
  207.7 141.7 %collective-permute-start.10 = (bf16[2,6,256,128]{3,2,1,0:T(8,128)(2,1)}, bf16[2,6,256,128]{3,2,1,0:T(8,128)(2,1)S(1)}, u32[]{:S(2)}, u32[]{:S(2)}) collective-permute-start(bf16[2,6,256,128]{3,2,1,0:T(8,128)(2,1)} %pad_maximum_fusion.13), channel_id=1, source_target_pairs={{0,4},{1,5},{2,6},{3,7},{4,0},{5,1},{6,2},{7,3},{8,12},{9,13},{10,... | collective-permute-start | bytes 2359304 | tf_op jit(solution)/shard_map/ppermute | solution.py:175
  259.1 101.3 %collective-permute-start.11 = (bf16[2,6,256,128]{3,2,1,0:T(8,128)(2,1)}, bf16[2,6,256,128]{3,2,1,0:T(8,128)(2,1)}, u32[]{:S(2)}, u32[]{:S(2)}) collective-permute-start(bf16[2,6,256,128]{3,2,1,0:T(8,128)(2,1)} %pad_maximum_fusion.14), channel_id=1, source_target_pairs={{0,5},{1,4},{2,7},{3,6},{4,1},{5,0},{6,3},{7,2},{8,13},{9,12},{10,... | collective-permute-start | bytes 2359304 | tf_op jit(solution)/shard_map/ppermute | solution.py:175
  309.6 67.6 %collective-permute-start.12 = (bf16[2,6,256,128]{3,2,1,0:T(8,128)(2,1)}, bf16[2,6,256,128]{3,2,1,0:T(8,128)(2,1)}, u32[]{:S(2)}, u32[]{:S(2)}) collective-permute-start(bf16[2,6,256,128]{3,2,1,0:T(8,128)(2,1)} %pad_maximum_fusion.15), channel_id=1, source_target_pairs={{0,6},{1,7},{2,4},{3,5},{4,2},{5,3},{6,0},{7,1},{8,14},{9,15},{10,... | collective-permute-start | bytes 2359304 | tf_op jit(solution)/shard_map/ppermute | solution.py:175
  328.9 78.8 %collective-permute-start.13 = (bf16[2,6,256,128]{3,2,1,0:T(8,128)(2,1)}, bf16[2,6,256,128]{3,2,1,0:T(8,128)(2,1)}, u32[]{:S(2)}, u32[]{:S(2)}) collective-permute-start(bf16[2,6,256,128]{3,2,1,0:T(8,128)(2,1)} %pad_maximum_fusion.16), channel_id=1, source_target_pairs={{0,7},{1,6},{2,5},{3,4},{4,3},{5,2},{6,1},{7,0},{8,15},{9,14},{10,... | collective-permute-start | bytes 2359304 | tf_op jit(solution)/shard_map/ppermute | solution.py:175
  349.4 108.0 %collective-permute-start.28 = (bf16[2,4,256,128]{3,2,1,0:T(8,128)(2,1)}, bf16[2,4,256,128]{3,2,1,0:T(8,128)(2,1)}, u32[]{:S(2)}, u32[]{:S(2)}) collective-permute-start(bf16[2,4,256,128]{3,2,1,0:T(8,128)(2,1)} %pad_maximum_fusion.18.refs_1_), channel_id=1, source_target_pairs={{0,1},{1,0},{2,3},{3,2},{4,5},{5,4},{6,7},{7,6},{8,9},{9,8},{10,11... | collective-permute-start | bytes 1572872 | tf_op jit(solution)/shard_map/ppermute | solution.py:175
  349.5 108.0 %collective-permute-start.29 = (bf16[2,4,256,128]{3,2,1,0:T(8,128)(2,1)}, bf16[2,4,256,128]{3,2,1,0:T(8,128)(2,1)}, u32[]{:S(2)}, u32[]{:S(2)}) collective-permute-start(bf16[2,4,256,128]{3,2,1,0:T(8,128)(2,1)} %pad_maximum_fusion.19.refs_2_), channel_id=1, source_target_pairs={{0,2},{1,3},{2,0},{3,1},{4,6},{5,7},{6,4},{7,5},{8,10},{9,11},{10,... | collective-permute-start | bytes 1572872 | tf_op jit(solution)/shard_map/ppermute | solution.py:175
  360.3 132.1 %collective-permute-start.30 = (bf16[2,4,256,128]{3,2,1,0:T(8,128)(2,1)}, bf16[2,4,256,128]{3,2,1,0:T(8,128)(2,1)}, u32[]{:S(2)}, u32[]{:S(2)}) collective-permute-start(bf16[2,4,256,128]{3,2,1,0:T(8,128)(2,1)} %pad_maximum_fusion.20.refs_3_), channel_id=1, source_target_pairs={{0,3},{1,2},{2,1},{3,0},{4,7},{5,6},{6,5},{7,4},{8,11},{9,10},{10,... | collective-permute-start | bytes 1572872 | tf_op jit(solution)/shard_map/ppermute | solution.py:175
  377.2 115.3 %collective-permute-start.31 = (bf16[2,4,256,128]{3,2,1,0:T(8,128)(2,1)}, bf16[2,4,256,128]{3,2,1,0:T(8,128)(2,1)}, u32[]{:S(2)}, u32[]{:S(2)}) collective-permute-start(bf16[2,4,256,128]{3,2,1,0:T(8,128)(2,1)} %pad_maximum_fusion.21.refs_4_), channel_id=1, source_target_pairs={{0,4},{1,5},{2,6},{3,7},{4,0},{5,1},{6,2},{7,3},{8,12},{9,13},{10,... | collective-permute-start | bytes 1572872 | tf_op jit(solution)/shard_map/ppermute | solution.py:175
  407.7 84.8 %collective-permute-start.32 = (bf16[2,4,256,128]{3,2,1,0:T(8,128)(2,1)}, bf16[2,4,256,128]{3,2,1,0:T(8,128)(2,1)}, u32[]{:S(2)}, u32[]{:S(2)}) collective-permute-start(bf16[2,4,256,128]{3,2,1,0:T(8,128)(2,1)} %pad_maximum_fusion.22.refs_5_), channel_id=1, source_target_pairs={{0,5},{1,4},{2,7},{3,6},{4,1},{5,0},{6,3},{7,2},{8,13},{9,12},{10,... | collective-permute-start | bytes 1572872 | tf_op jit(solution)/shard_map/ppermute | solution.py:175
  457.3 36.5 %collective-permute-start.33 = (bf16[2,4,256,128]{3,2,1,0:T(8,128)(2,1)}, bf16[2,4,256,128]{3,2,1,0:T(8,128)(2,1)}, u32[]{:S(2)}, u32[]{:S(2)}) collective-permute-start(bf16[2,4,256,128]{3,2,1,0:T(8,128)(2,1)} %pad_maximum_fusion.23.refs_6_), channel_id=1, source_target_pairs={{0,6},{1,7},{2,4},{3,5},{4,2},{5,3},{6,0},{7,1},{8,14},{9,15},{10,... | collective-permute-start | bytes 1572872 | tf_op jit(solution)/shard_map/ppermute | solution.py:175
  457.5 45.9 %collective-permute-start.34 = (bf16[2,4,256,128]{3,2,1,0:T(8,128)(2,1)}, bf16[2,4,256,128]{3,2,1,0:T(8,128)(2,1)}, u32[]{:S(2)}, u32[]{:S(2)}) collective-permute-start(bf16[2,4,256,128]{3,2,1,0:T(8,128)(2,1)} %pad_maximum_fusion.24.refs_7_), channel_id=1, source_target_pairs={{0,7},{1,6},{2,5},{3,4},{4,3},{5,2},{6,1},{7,0},{8,15},{9,14},{10,... | collective-permute-start | bytes 1572872 | tf_op jit(solution)/shard_map/ppermute | solution.py:175
  (31 other events, 540.7 us)
where the time goes:
time: 512 us; the launch traced here: 510 us
  waiting for transfers between devices  279 us (54%)
  matrix products  80.1 us (16%)
  Pallas kernels  56.4 us (11%)
  starting transfers between devices  44.5 us (9%)
  other arithmetic  29.7 us (6%)
  local copies, waits for them, and re-layouts  19.1 us (4%)
    ppermute x35, waiting for transfers between devices, swap(): return lax.ppermute(value, 'x', [(i, i ^ k) for i in range(N_DEV)])  279 us
    pallas_call x3, Pallas kernels, settle(): pl.pallas_call(body, grid_spec=pltpu.PrefetchScalarGridSpec(num_scalar_pr...  44.8 us
    ppermute x35, starting transfers between devices, swap(): return lax.ppermute(value, 'x', [(i, i ^ k) for i in range(N_DEV)])  44.5 us
    dot_general x1, matrix products, finish(): jnp.einsum('sbf,fd->sbd', activated, w_down, preferred_element_type=jnp.f...  34.9 us
    another operation x24, other arithmetic, pieces(): jnp.stack([lax.dynamic_slice_in_dim(c, p * num_rows + lo, hi - lo) for c...  22.1 us
    dot_general x1, matrix products, finish(): jnp.einsum('sbd,df->sbf', normed, w_gate, preferred_element_type=jnp.floa...  19.6 us
    pallas_call x1, Pallas kernels, remote_attend(): pl.pallas_call(body, grid_spec=pltpu.PrefetchScalarGridSpec(num_scalar_pr...  11.6 us
    another operation x3, local copies, waits for them, and re-layouts, pieces(): jnp.stack([lax.dynamic_slice_in_dim(c, p * num_rows + lo, hi - lo) for c...  10.5 us
  transfers between devices with their start and end apart: 35, of which 16 were waited for; matrix products, arithmetic and copies ran while one was open for 20% of the time, Pallas kernels for 10%

commit v1 on v0

--- a/solution.py
+++ b/solution.py
@@ -9,7 +9,7 @@
 EPS = 1e-6
 THETA = 1000000.0
 N_DEV = 8
-CHUNKS = ((0, 6), (6, 12), (12, 16))
+FIRST, LOCAL, LAST = 2, 8, 14
 
 
 def rms_norm(values, gain_vec):
@@ -77,40 +77,48 @@
     return (mixed / total).astype(jnp.bfloat16)
 
 
-def remote_attend(scalars, blocks, packs, offset):
-    n_seq, num_slots, head_dim = blocks[0].shape[1:]
+def cache_specs(num_slots, head_dim, first_row):
+    return pl.BlockSpec((1, num_slots, head_dim), lambda i, s: (first_row(s) + i, 0, 0))
+
+
+def remote_attend(scalars, caches, packs, offset):
+    n_seq = packs[0].shape[0]
+    num_slots, head_dim = caches[0].shape[1:]
 
     def body(scal_ref, *refs):
-        block_refs, pack_refs, out_refs = refs[:N_DEV], refs[N_DEV:2 * N_DEV], refs[2 * N_DEV:]
+        key_refs, value_refs = refs[:N_DEV], refs[N_DEV:2 * N_DEV]
+        pack_refs, out_refs = refs[2 * N_DEV:3 * N_DEV], refs[3 * N_DEV:]
         seq = pl.program_id(0)
         me = scal_ref[128]
         for k in range(N_DEV):
             pos = scal_ref[(me ^ k) * 16 + offset + seq]
-            out_refs[k][0] = attend_one(pack_refs[k][0], block_refs[k][0, 0], block_refs[k][1, 0], pos)
-
+            out_refs[k][0] = attend_one(pack_refs[k][0], key_refs[k][0], value_refs[k][0], pos)
+
+    rows = [cache_specs(num_slots, head_dim, lambda s, k=k: (s[128] ^ k) * 16 + offset) for k in range(N_DEV)]
     return pl.pallas_call(
         body,
         grid_spec=pltpu.PrefetchScalarGridSpec(
             num_scalar_prefetch=1,
             grid=(n_seq,),
-            in_specs=[pl.BlockSpec((2, 1, num_slots, head_dim), lambda i, s: (0, i, 0, 0))] * N_DEV
-            + [pl.BlockSpec((1, 24, head_dim), lambda i, s: (i, 0, 0))] * N_DEV,
+            in_specs=rows + rows + [pl.BlockSpec((1, 24, head_dim), lambda i, s: (i, 0, 0))] * N_DEV,
             out_specs=[pl.BlockSpec((1, 16, head_dim), lambda i, s: (i, 0, 0))] * N_DEV,
         ),
         out_shape=[jax.ShapeDtypeStruct((n_seq, 16, head_dim), jnp.bfloat16)] * N_DEV,
         cost_estimate=pl.CostEstimate(flops=n_seq * 40_000_000, bytes_accessed=n_seq * 1_100_000, transcendentals=0),
         name="remote_attend",
-    )(scalars, *blocks, *packs)
-
-
-def settle(scalars, blocks, new_keys, new_values, pack, caches, offset, num_seqs):
-    n_seq, num_slots, head_dim = blocks[0].shape[1:]
+    )(scalars, *[caches[0]] * N_DEV, *[caches[1]] * N_DEV, *packs)
+
+
+def settle(scalars, own, blocks, new_keys, new_values, pack, caches, chunk, num_seqs):
+    lo, hi = chunk
+    num_slots, head_dim = own[0].shape[1:]
     with_attn, in_place = pack is not None, caches is not None
     n_steps = new_keys.shape[1]
 
     def body(scal_ref, *refs):
         refs = list(refs)
-        block_refs = [refs.pop(0) for _ in range(N_DEV)]
+        own_refs = [refs.pop(0) for _ in range(2)]
+        block_refs = [refs.pop(0) for _ in range(N_DEV - 1)]
         new_refs = [refs.pop(0) for _ in range(2)]
         pack_ref = refs.pop(0) if with_attn else None
         if in_place:
@@ -119,24 +127,32 @@
         out_ref = refs.pop(0) if with_attn else None
         spread_refs = refs
         me = scal_ref[128]
-        pos = scal_ref[me * 16 + offset + pl.program_id(0)]
+        pos = scal_ref[me * 16 + lo + pl.program_id(0)]
+
+        def block(k, kind):
+            return own_refs[kind][0] if k == 0 else block_refs[k - 1][kind, 0]
+
         for kind in range(2):
             spread = spread_refs[kind]
             for k in range(N_DEV):
-                spread[pl.ds(me ^ k, num_slots, stride=N_DEV), :] = block_refs[k][kind, 0].astype(jnp.float32)
+                spread[pl.ds(me ^ k, num_slots, stride=N_DEV), :] = block(k, kind).astype(jnp.float32)
             cache_refs[kind][0] = spread[...].reshape(num_slots, N_DEV, head_dim).astype(jnp.bfloat16)
             for step in range(n_steps):
                 cache_refs[kind][0, pos + step] = new_refs[kind][0, step]
         if with_attn:
             for k in range(N_DEV):
-                out_ref[0, me ^ k] = attend_one(pack_ref[0, me ^ k], block_refs[k][0, 0], block_refs[k][1, 0], pos)
-
-    cache_block = pl.BlockSpec((1, num_slots, N_DEV, head_dim), lambda i, s: (offset + i, 0, 0, 0))
-    in_specs = [pl.BlockSpec((2, 1, num_slots, head_dim), lambda i, s: (0, i, 0, 0))] * N_DEV
-    in_specs += [pl.BlockSpec((1, n_steps, N_DEV, head_dim), lambda i, s: (i, 0, 0, 0))] * 2
-    args = [scalars, *blocks, new_keys, new_values]
+                out_ref[0, me ^ k] = attend_one(pack_ref[0, me ^ k], block(k, 0), block(k, 1), pos)
+
+    cache_block = pl.BlockSpec((1, num_slots, N_DEV, head_dim), lambda i, s: (lo + i, 0, 0, 0))
+    in_specs = [cache_specs(num_slots, head_dim, lambda s: s[128] * 16 + lo)] * 2
+    in_specs += [
+        pl.BlockSpec((2, 1, num_slots, head_dim), lambda i, s, first=lo - first: (0, first + i, 0, 0))
+        for first, _ in blocks
+    ]
+    in_specs += [pl.BlockSpec((1, n_steps, N_DEV, head_dim), lambda i, s: (lo + i, 0, 0, 0))] * 2
+    args = [scalars, *own, *[b for _, b in blocks], new_keys, new_values]
     if with_attn:
-        in_specs.append(pl.BlockSpec((1, N_DEV, 24, head_dim), lambda i, s: (i, 0, 0, 0)))
+        in_specs.append(pl.BlockSpec((1, N_DEV, 24, head_dim), lambda i, s: (lo + i, 0, 0, 0)))
         args.append(pack)
     aliases = {}
     if in_place:
@@ -147,19 +163,19 @@
     out_specs, out_shape = [cache_block] * 2, [cache_shape] * 2
     if with_attn:
         out_specs.append(pl.BlockSpec((1, N_DEV, 16, head_dim), lambda i, s: (i, 0, 0, 0)))
-        out_shape.append(jax.ShapeDtypeStruct((n_seq, N_DEV, 16, head_dim), jnp.bfloat16))
+        out_shape.append(jax.ShapeDtypeStruct((hi - lo, N_DEV, 16, head_dim), jnp.bfloat16))
     return pl.pallas_call(
         body,
         grid_spec=pltpu.PrefetchScalarGridSpec(
             num_scalar_prefetch=1,
-            grid=(n_seq,),
+            grid=(hi - lo,),
             in_specs=in_specs,
             out_specs=out_specs,
             scratch_shapes=[pltpu.VMEM((num_slots * N_DEV, head_dim), jnp.float32)] * 2,
         ),
         out_shape=out_shape,
         input_output_aliases=aliases,
-        cost_estimate=pl.CostEstimate(flops=n_seq * 60_000_000, bytes_accessed=n_seq * 2_200_000, transcendentals=0),
+        cost_estimate=pl.CostEstimate(flops=(hi - lo) * 60_000_000, bytes_accessed=(hi - lo) * 2_200_000, transcendentals=0),
         name="settle",
     )(*args)
 
@@ -168,19 +184,10 @@
     row_spec = P(None, ('dp', 'x'), None)
     cache_in = P('dp', None, 'x', None)
     cache_out = P(('dp', 'x'), None, None, None)
+    near, far = (2, 3, 1), (4, 5, 6, 7)
 
     def swap(value, k):
-        if k == 0:
-            return value
         return lax.ppermute(value, 'x', [(i, i ^ k) for i in range(N_DEV)])
-
-    order = (2, 3, 1, 4, 5, 6, 7)
-
-    def swap_all(values):
-        got = {0: values[0]}
-        for k in order:
-            got[k] = swap(values[k], k)
-        return [got[k] for k in range(N_DEV)]
 
     def local_run(start_pos, hidden_in, k_heads, v_heads, attn_norm, w_q, w_k, w_v, q_norm, k_norm, w_o, mlp_norm, w_gate, w_up, w_down):
         me = lax.axis_index('x')
@@ -188,43 +195,50 @@
         num_slots, head_dim = k_heads.shape[1], k_heads.shape[3]
         my_pos = lax.dynamic_slice_in_dim(start_pos, me * num_rows, num_rows)
         scalars = jnp.concatenate([start_pos, me[None].astype(jnp.int32)])
-        partners = [me ^ k for k in range(N_DEV)]
-        xor_heads = jnp.stack(partners)
-
-        def pieces(caches, chunk):
-            lo, hi = chunk
-            keys, values = (c.reshape(N_DEV * num_rows, num_slots, head_dim) for c in caches)
-            return [
-                jnp.stack([lax.dynamic_slice_in_dim(c, p * num_rows + lo, hi - lo) for c in (keys, values)])
-                for p in partners
-            ]
-
-        caches = (k_heads, v_heads)
-        a, b, r = CHUNKS
-        got_a = swap_all(pieces(caches, a))
+        xor_heads = me ^ jnp.arange(N_DEV)
+        own = tuple(c.reshape(N_DEV * num_rows, num_slots, head_dim) for c in (k_heads, v_heads))
+
+        def exchange(caches, lo, hi, partners):
+            return {
+                k: (lo, swap(jnp.stack([lax.dynamic_slice_in_dim(c, (me ^ k) * num_rows + lo, hi - lo) for c in caches]), k))
+                for k in partners
+            }
+
+        def swap_small(values):
+            got = {k: swap(values[k], k) for k in near + far}
+            return [values[0]] + [got[k] for k in range(1, N_DEV)]
+
+        def chosen(*parts):
+            merged = {k: v for part in parts for k, v in part.items()}
+            return [merged[k] for k in range(1, N_DEV)]
+
+        far_first = exchange(own, 0, FIRST, far)
         positions = my_pos[None, :] + jnp.arange(n_steps)[:, None]
         queries, keys_new, values_new = project(hidden_in, positions, attn_norm, w_q, w_k, w_v, q_norm, k_norm)
         q_rows = jnp.transpose(queries.reshape(n_steps, num_rows, N_DEV, -1, head_dim), (1, 2, 0, 3, 4)).reshape(num_rows, N_DEV, -1, head_dim)
         k_rows = jnp.transpose(keys_new, (1, 2, 0, 3))
         v_rows = jnp.transpose(values_new, (1, 2, 0, 3))
         pack = jnp.concatenate([q_rows, k_rows, v_rows], axis=2)
-        knat, vnat = jnp.swapaxes(keys_new, 0, 1), jnp.swapaxes(values_new, 0, 1)
-        pack_r = jnp.take(jnp.swapaxes(pack[r[0]:r[1]], 0, 1), xor_heads, axis=0)
-        got_q = swap_all([pack_r[k] for k in range(N_DEV)])
-        *caches, pack = lax.optimization_barrier((*caches, pack))
-        got_b = swap_all(pieces(caches, b))
-        blocks_r = pieces(caches, r)
-        o_r = remote_attend(scalars, blocks_r, got_q, r[0])
-        got_o = swap_all(o_r)
-        blocks_r, _ = lax.optimization_barrier((blocks_r, o_r))
-        got_r = swap_all(blocks_r)
-        k_out, v_out, o_a = settle(scalars, got_a, knat[a[0]:a[1]], vnat[a[0]:a[1]], pack[a[0]:a[1]], None, a[0], num_rows)
-        k_out, v_out, o_b = settle(scalars, got_b, knat[b[0]:b[1]], vnat[b[0]:b[1]], pack[b[0]:b[1]], (k_out, v_out), b[0], num_rows)
+        new = jnp.swapaxes(keys_new, 0, 1), jnp.swapaxes(values_new, 0, 1)
+        pack_r = jnp.take(jnp.swapaxes(pack[LOCAL:], 0, 1), xor_heads, axis=0)
+        got_q = swap_small([pack_r[k] for k in range(N_DEV)])
+        *held, pack = lax.optimization_barrier((*own, pack))
+        near_local = exchange(held, 0, LOCAL, near)
+        far_local = exchange(held, FIRST, LOCAL, far)
+        o_r = remote_attend(scalars, own, got_q, LOCAL)
+        got_o = swap_small(o_r)
+        *held, _ = lax.optimization_barrier((*held, o_r[0]))
+        near_rest = exchange(held, LOCAL, num_rows, near)
+        far_rest = exchange(held, LOCAL, LAST, far)
+        far_last = exchange(held, LAST, num_rows, far)
+        *caches, o_a = settle(scalars, own, chosen(near_local, far_first), *new, pack, None, (0, FIRST), num_rows)
+        *caches, o_b = settle(scalars, own, chosen(near_local, far_local), *new, pack, caches, (FIRST, LOCAL), num_rows)
         o_r = jnp.swapaxes(jnp.take(jnp.stack(got_o), xor_heads, axis=0), 0, 1)
         attended = jnp.concatenate([o_a, o_b, o_r], axis=0).reshape(num_rows, N_DEV, n_steps, -1, head_dim)
         attended = jnp.transpose(attended, (2, 0, 1, 3, 4)).reshape(n_steps, num_rows, -1)
         out_hidden = finish(hidden_in, attended, w_o, mlp_norm, w_gate, w_up, w_down)
-        k_out, v_out = settle(scalars, got_r, knat[r[0]:r[1]], vnat[r[0]:r[1]], None, (k_out, v_out), r[0], num_rows)
-        return out_hidden, k_out, v_out
+        caches = settle(scalars, own, chosen(near_rest, far_rest), *new, None, caches, (LOCAL, LAST), num_rows)
+        caches = settle(scalars, own, chosen(near_rest, far_last), *new, None, caches, (LAST, num_rows), num_rows)
+        return out_hidden, *caches
 
     return jax.shard_map(local_run, mesh=mesh, in_specs=(P('dp'), row_spec, cache_in, cache_in) + (P(),) * 11, out_specs=(row_spec, cache_out, cache_out), check_vma=False)

time: 512 us -> 485 us (0.947)
  waiting for transfers between devices: 279 us -> 253 us
  starting transfers between devices: 44.5 us -> 35.5 us
  Pallas kernels: 56.4 us -> 63.1 us
    ppermute x35 -> x36, waiting for transfers between devices: 279 us -> 253 us  [swap(): return lax.ppermute(value, 'x', [(i, i ^ k) for i in range(N_DEV)])]
    pallas_call x1, Pallas kernels: 11.6 us -> 22.4 us  [remote_attend(): pl.pallas_call(body, grid_spec=pltpu.PrefetchScalarGridSpec(num_scalar_pr...]
    ppermute x35 -> x36, starting transfers between devices: 44.5 us -> 35.5 us  [swap(): return lax.ppermute(value, 'x', [(i, i ^ k) for i in range(N_DEV)])]
    pallas_call x3 -> x4, Pallas kernels: 44.8 us -> 40.8 us  [settle(): pl.pallas_call(body, grid_spec=pltpu.PrefetchScalarGridSpec(num_scalar_pr...]
    another operation x26 -> x24, other arithmetic: 22.7 us -> 20 us  [the longest x22 19.3 us: exchange(): jnp.stack([lax.dynamic_slice_in_dim(c, (me ^ k) * num_rows + lo, hi - lo)...]
    another operation x5 -> x6, local copies, waits for them, and re-layouts: 10.7 us -> 10.9 us  [exchange(): jnp.stack([lax.dynamic_slice_in_dim(c, (me ^ k) * num_rows + lo, hi - lo)...]
  transfers between devices with their start and end apart: 35 -> 36, of which waited for: 16 -> 12; matrix products, arithmetic and copies ran while one was open for 20% -> 21% of each run, Pallas kernels for 10% -> 12%
where the time goes in v1:
time: 485 us; the launch traced here: 478 us
  waiting for transfers between devices  253 us (52%)
  matrix products  80 us (16%)
  Pallas kernels  63.1 us (13%)
  starting transfers between devices  35.5 us (7%)
  other arithmetic  27 us (6%)
  local copies, waits for them, and re-layouts  17.9 us (4%)
    ppermute x36, waiting for transfers between devices, swap(): return lax.ppermute(value, 'x', [(i, i ^ k) for i in range(N_DEV)])  253 us
    pallas_call x4, Pallas kernels, settle(): pl.pallas_call(body, grid_spec=pltpu.PrefetchScalarGridSpec(num_scalar_pr...  40.8 us
    ppermute x36, starting transfers between devices, swap(): return lax.ppermute(value, 'x', [(i, i ^ k) for i in range(N_DEV)])  35.5 us
    dot_general x1, matrix products, finish(): jnp.einsum('sbf,fd->sbd', activated, w_down, preferred_element_type=jnp.f...  34.9 us
    pallas_call x1, Pallas kernels, remote_attend(): pl.pallas_call(body, grid_spec=pltpu.PrefetchScalarGridSpec(num_scalar_pr...  22.4 us
    dot_general x1, matrix products, finish(): jnp.einsum('sbd,df->sbf', normed, w_gate, preferred_element_type=jnp.floa...  19.6 us
    another operation x22, other arithmetic, exchange(): jnp.stack([lax.dynamic_slice_in_dim(c, (me ^ k) * num_rows + lo, hi - lo)...  19.3 us
    another operation x6, local copies, waits for them, and re-layouts, exchange(): jnp.stack([lax.dynamic_slice_in_dim(c, (me ^ k) * num_rows + lo, hi - lo)...  10.9 us
  transfers between devices with their start and end apart: 36, of which 12 were waited for; matrix products, arithmetic and copies ran while one was open for 21% of the time, Pallas kernels for 12%

profile of v1, /device:TPU:17, one launch (start us, length us, event | category | flops | bytes accessed | tf_op | source)
XLA Modules:
  0.0 478.1 jit_solution(7871107047197629894)
XLA Ops:
  2.5 3.7 fusion.47
  7.1 3.7 fusion.20
  12.7 9.2 %fusion.8 = f32[4,16,4096]{2,1,0:T(8,128)S(1)} fusion(bf16[2560,4096]{1,0:T(8,128)(2,1)} %param.20, bf16[4,16,2560]{2,1,0:T(8,128)(2,1)S(1)} %copy-done.1, f32[2560]{0:T(1024)S(1)} %convert_element_type.53, f32[4,16]{1,0:T(4,128)S(1)} %add_rsqrt_fusion.3), kind=kOutput, calls=%fused_computation.10 | convolution fusion | flops 1342832640 | bytes 22358272 | tf_op jit(solution)/shard_map/sbd,de->sbe/dot_general | solution.py:37
  53.4 22.4 %remote_attend.1 = (bf16[8,16,128]{2,1,0:T(8,128)(2,1)}, bf16[8,16,128]{2,1,0:T(8,128)(2,1)}, bf16[8,16,128]{2,1,0:T(8,128)(2,1)}, bf16[8,16,128]{2,1,0:T(8,128)...) custom-call(s32[129]{0:T(256)} %pad_add_fusion.scal_ref, ...), custom_call_target="tpu_custom_call" | custom-call | flops 320000000 | bytes 8800000 | tf_op jit(solution)/shard_map/remote_attend/pallas_call | solution.py:98
  99.8 9.9 %collective-permute-done.22 = bf16[8,16,128]{2,1,0:T(8,128)(2,1)S(1)} collective-permute-done((bf16[8,16,128]{2,1,0:T(8,128)(2,1)S(1)}, bf16[8,16,128]{2,1,0:T(8,128)(2,1)S(1)}, u32[]{:S(2)}, u32[]{:S(2)}) %collective-permute-start.22) | collective-permute-done | bytes 32800 | tf_op jit(solution)/shard_map/ppermute | solution.py:190
  109.7 3.4 collective-permute-start.4
  115.1 23.3 %collective-permute-done.24 = bf16[8,16,128]{2,1,0:T(8,128)(2,1)S(1)} collective-permute-done((bf16[8,16,128]{2,1,0:T(8,128)(2,1)S(1)}, bf16[8,16,128]{2,1,0:T(8,128)(2,1)S(1)}, u32[]{:S(2)}, u32[]{:S(2)}) %collective-permute-start.24) | collective-permute-done | bytes 32800 | tf_op jit(solution)/shard_map/ppermute | solution.py:190
  140.6 5.4 %collective-permute-done.5.refs_7_ = bf16[2,2,256,128]{3,2,1,0:T(8,128)(2,1)S(1)} collective-permute-done((bf16[2,2,256,128]{3,2,1,0:T(8,128)(2,1)S(1)}, bf16[2,2,256,128]{3,2,1,0:T(8,128)(2,1)S(1)}, u32[]{:S(2)}, u32[]{:S(2)}) %collective-permute-start.5) | collective-permute-done | bytes 262176 | tf_op jit(solution)/shard_map/ppermute | solution.py:190
  146.0 7.3 %collective-permute-done.6.refs_8_ = bf16[2,2,256,128]{3,2,1,0:T(8,128)(2,1)S(1)} collective-permute-done((bf16[2,2,256,128]{3,2,1,0:T(8,128)(2,1)S(1)}, bf16[2,2,256,128]{3,2,1,0:T(8,128)(2,1)S(1)}, u32[]{:S(2)}, u32[]{:S(2)}) %collective-permute-start.6) | collective-permute-done | bytes 262176 | tf_op jit(solution)/shard_map/ppermute | solution.py:190
  154.9 22.8 %collective-permute-done.2.refs_4_ = bf16[2,8,256,128]{3,2,1,0:T(8,128)(2,1)} collective-permute-done((bf16[2,8,256,128]{3,2,1,0:T(8,128)(2,1)}, bf16[2,8,256,128]{3,2,1,0:T(8,128)(2,1)}, u32[]{:S(2)}, u32[]{:S(2)}) %collective-permute-start.2) | collective-permute-done | bytes 1048608 | tf_op jit(solution)/shard_map/ppermute | solution.py:190
  178.2 8.2 %settle.4 = (bf16[16,256,8,128]{3,2,1,0:T(8,128)(2,1)}, bf16[16,256,8,128]{3,2,1,0:T(8,128)(2,1)}, bf16[2,8,16,128]{3,2,1,0:T(8,128)(2,1)}) custom-call(s32[129]{0:T(256)} %pad_add_fusion.scal_ref, bf16[128,256,128]{2,1,0:T(8,128)(2,1)} %bitcast.242, bf16[128,256,128]{2,1,0:T(8,128)(2,1)} %bitcast.259, bf16[2,8,256,128]{3,2,1,0:T(8,128)(2,1)} %copy-done.2, ...), custom_call_target="tpu_custom_call" | custom-call | flops 120000000 | bytes 4400000 | tf_op jit(solution)/shard_map/settle/pallas_call | solution.py:167
  186.4 48.1 %collective-permute-done.7.refs_5_ = bf16[2,6,256,128]{3,2,1,0:T(8,128)(2,1)} collective-permute-done((bf16[2,6,256,128]{3,2,1,0:T(8,128)(2,1)}, bf16[2,6,256,128]{3,2,1,0:T(8,128)(2,1)}, u32[]{:S(2)}, u32[]{:S(2)}) %collective-permute-start.7) | collective-permute-done | bytes 786464 | tf_op jit(solution)/shard_map/ppermute | solution.py:190
  237.1 14.3 %collective-permute-done.8.refs_6_ = bf16[2,6,256,128]{3,2,1,0:T(8,128)(2,1)} collective-permute-done((bf16[2,6,256,128]{3,2,1,0:T(8,128)(2,1)}, bf16[2,6,256,128]{3,2,1,0:T(8,128)(2,1)}, u32[]{:S(2)}, u32[]{:S(2)}) %collective-permute-start.8) | collective-permute-done | bytes 786464 | tf_op jit(solution)/shard_map/ppermute | solution.py:190
  251.4 4.5 collective-permute-start.32
  255.9 30.6 %collective-permute-done.9.refs_7_ = bf16[2,6,256,128]{3,2,1,0:T(8,128)(2,1)} collective-permute-done((bf16[2,6,256,128]{3,2,1,0:T(8,128)(2,1)}, bf16[2,6,256,128]{3,2,1,0:T(8,128)(2,1)}, u32[]{:S(2)}, u32[]{:S(2)}) %collective-permute-start.9) | collective-permute-done | bytes 786464 | tf_op jit(solution)/shard_map/ppermute | solution.py:190
  286.5 52.0 %collective-permute-done.10.refs_8_ = bf16[2,6,256,128]{3,2,1,0:T(8,128)(2,1)} collective-permute-done((bf16[2,6,256,128]{3,2,1,0:T(8,128)(2,1)}, bf16[2,6,256,128]{3,2,1,0:T(8,128)(2,1)}, u32[]{:S(2)}, u32[]{:S(2)}) %collective-permute-start.10) | collective-permute-done | bytes 786464 | tf_op jit(solution)/shard_map/ppermute | solution.py:190
  339.3 19.5 %settle.5 = (bf16[16,256,8,128]{3,2,1,0:T(8,128)(2,1)}, bf16[16,256,8,128]{3,2,1,0:T(8,128)(2,1)}, bf16[6,8,16,128]{3,2,1,0:T(8,128)(2,1)}) custom-call(s32[129]{0:T(256)} %pad_add_fusion.scal_ref, bf16[128,256,128]{2,1,0:T(8,128)(2,1)} %bitcast.243, bf16[128,256,128]{2,1,0:T(8,128)(2,1)} %bitcast.260, ...), custom_call_target="tpu_custom_call", output_to_operand_aliasing={{0}: (13, {}), {1}: (14, {})} | custom-call | flops 360000000 | bytes 13200000 | tf_op jit(solution)/shard_map/settle/pallas_call | solution.py:167
  360.3 9.0 %multiply_reduce_fusion = (f32[4,16]{1,0:T(4,128)S(1)}, f32[4,16,2560]{2,1,0:T(8,128)S(1)}) fusion(bf16[4,16,4096]{2,1,0:T(8,128)(2,1)S(1)} %reshape.148, bf16[4096,2560]{1,0:T(8,128)(2,1)} %param.25, bf16[4,16,2560]{2,1,0:T(8,128)(2,1)S(1)} %copy-done.1), kind=kOutput, calls=%fused_computation.57 | convolution fusion | flops 1343160320 | bytes 22479104 | tf_op jit(solution)/shard_map/sbe,ed->sbd/dot_general | solution.py:48
  370.2 19.6 %fusion.4 = f32[4,16,9728]{2,1,0:T(8,128)S(1)} fusion(bf16[2560,9728]{1,0:T(8,128)(2,1)} %param.27, f32[4,16,2560]{2,1,0:T(8,128)S(1)} %get-tuple-element.110, f32[2560]{0:T(1024)S(1)} %convert_element_type.62, f32[4,16]{1,0:T(4,128)S(1)} %add_rsqrt_fusion.2), kind=kOutput, calls=%fused_computation.6 | convolution fusion | flops 3188162560 | bytes 52963584 | tf_op jit(solution)/shard_map/sbd,df->sbf/dot_general | solution.py:51
  390.0 14.5 %collective-permute-done.34.refs_7_ = bf16[2,6,256,128]{3,2,1,0:T(8,128)(2,1)} collective-permute-done((bf16[2,6,256,128]{3,2,1,0:T(8,128)(2,1)}, bf16[2,6,256,128]{3,2,1,0:T(8,128)(2,1)}, u32[]{:S(2)}, u32[]{:S(2)}) %collective-permute-start.34) | collective-permute-done | bytes 786464 | tf_op jit(solution)/shard_map/ppermute | solution.py:190
  404.5 23.9 %collective-permute-done.35.refs_8_ = bf16[2,6,256,128]{3,2,1,0:T(8,128)(2,1)} collective-permute-done((bf16[2,6,256,128]{3,2,1,0:T(8,128)(2,1)}, bf16[2,6,256,128]{3,2,1,0:T(8,128)(2,1)}, u32[]{:S(2)}, u32[]{:S(2)}) %collective-permute-start.35) | collective-permute-done | bytes 786464 | tf_op jit(solution)/shard_map/ppermute | solution.py:190
  429.3 34.9 %fusion.30 = bf16[4,16,2560]{2,1,0:T(8,128)(2,1)} fusion(f32[4,16,2560]{2,1,0:T(8,128)S(1)} %get-tuple-element.110, bf16[9728,2560]{1,0:T(8,128)(2,1)} %param.29, bf16[2560,9728]{1,0:T(8,128)(2,1)} %param.28, f32[4,16,9728]{2,1,0:T(8,128)S(1)} %fusion.4, f32[2560]{0:T(1024)S(1)} %convert_element_type.62, f32[4,16]{1,0:T(4,128)S(1)} %add_rsqrt_fusion.2), kind=kOutput, calls=%fused_computation.20 | convolution fusion | flops 6379896832 | bytes 103098624 | tf_op jit(solution)/shard_map/sbf,fd->sbd/dot_general | solution.py:54
  464.2 8.8 %settle.6 = (bf16[16,256,8,128]{3,2,1,0:T(8,128)(2,1)}, bf16[16,256,8,128]{3,2,1,0:T(8,128)(2,1)}) custom-call(s32[129]{0:T(256)} %pad_add_fusion.scal_ref, bf16[128,256,128]{2,1,0:T(8,128)(2,1)} %bitcast.244, bf16[128,256,128]{2,1,0:T(8,128)(2,1)} %bitcast.261, ...), custom_call_target="tpu_custom_call", output_to_operand_aliasing={{0}: (12, {}), {1}: (13, {})} | custom-call | flops 360000000 | bytes 13200000 | tf_op jit(solution)/shard_map/settle/pallas_call | solution.py:167
  473.7 4.3 settle.7
  (195 shorter events, 73.4 us)
Async XLA Ops:
  27.6 20.8 %collective-permute-start.13 = (bf16[8,24,128]{2,1,0:T(8,128)(2,1)S(1)}, bf16[8,24,128]{2,1,0:T(8,128)(2,1)S(1)}, u32[]{:S(2)}, u32[]{:S(2)}) collective-permute-start(bf16[8,24,128]{2,1,0:T(8,128)(2,1)S(1)} %get-tuple-element.99), channel_id=1, source_target_pairs={{0,3},{1,2},{2,1},{3,0},{4,7},{5,6},{6,5},{7,4},{8,11},{9,10},{10,... | collective-permute-start | bytes 147464 | tf_op jit(solution)/shard_map/ppermute | solution.py:190
  28.0 20.8 %collective-permute-start.14 = (bf16[8,24,128]{2,1,0:T(8,128)(2,1)S(1)}, bf16[8,24,128]{2,1,0:T(8,128)(2,1)S(1)}, u32[]{:S(2)}, u32[]{:S(2)}) collective-permute-start(bf16[8,24,128]{2,1,0:T(8,128)(2,1)S(1)} %get-tuple-element.98), channel_id=1, source_target_pairs={{0,4},{1,5},{2,6},{3,7},{4,0},{5,1},{6,2},{7,3},{8,12},{9,13},{10,... | collective-permute-start | bytes 147464 | tf_op jit(solution)/shard_map/ppermute | solution.py:190
  28.0 23.9 %collective-permute-start.15 = (bf16[8,24,128]{2,1,0:T(8,128)(2,1)}, bf16[8,24,128]{2,1,0:T(8,128)(2,1)S(1)}, u32[]{:S(2)}, u32[]{:S(2)}) collective-permute-start(bf16[8,24,128]{2,1,0:T(8,128)(2,1)} %get-tuple-element.97), channel_id=1, source_target_pairs={{0,5},{1,4},{2,7},{3,6},{4,1},{5,0},{6,3},{7,2},{8,13},{9,12},{10,... | collective-permute-start | bytes 147464 | tf_op jit(solution)/shard_map/ppermute | solution.py:190
  48.5 104.9 %collective-permute-start = (bf16[2,8,256,128]{3,2,1,0:T(8,128)(2,1)}, bf16[2,8,256,128]{3,2,1,0:T(8,128)(2,1)S(1)}, u32[]{:S(2)}, u32[]{:S(2)}) collective-permute-start(bf16[2,8,256,128]{3,2,1,0:T(8,128)(2,1)} %pad_maximum_fusion), channel_id=1, source_target_pairs={{0,1},{1,0},{2,3},{3,2},{4,5},{5,4},{6,7},{7,6},{8,9},{9,8},{10,11... | collective-permute-start | bytes 3145736 | tf_op jit(solution)/shard_map/ppermute | solution.py:190
  48.8 105.4 %collective-permute-start.1 = (bf16[2,8,256,128]{3,2,1,0:T(8,128)(2,1)}, bf16[2,8,256,128]{3,2,1,0:T(8,128)(2,1)S(1)}, u32[]{:S(2)}, u32[]{:S(2)}) collective-permute-start(bf16[2,8,256,128]{3,2,1,0:T(8,128)(2,1)} %pad_maximum_fusion.1), channel_id=1, source_target_pairs={{0,2},{1,3},{2,0},{3,1},{4,6},{5,7},{6,4},{7,5},{8,10},{9,11},{10,... | collective-permute-start | bytes 3145736 | tf_op jit(solution)/shard_map/ppermute | solution.py:190
  96.7 42.5 %collective-permute-start.3 = (bf16[2,2,256,128]{3,2,1,0:T(8,128)(2,1)}, bf16[2,2,256,128]{3,2,1,0:T(8,128)(2,1)S(1)}, u32[]{:S(2)}, u32[]{:S(2)}) collective-permute-start(bf16[2,2,256,128]{3,2,1,0:T(8,128)(2,1)} %pad_maximum_fusion.16), channel_id=1, source_target_pairs={{0,4},{1,5},{2,6},{3,7},{4,0},{5,1},{6,2},{7,3},{8,12},{9,13},{10,... | collective-permute-start | bytes 786440 | tf_op jit(solution)/shard_map/ppermute | solution.py:190
  109.7 30.8 %collective-permute-start.4 = (bf16[2,2,256,128]{3,2,1,0:T(8,128)(2,1)S(1)}, bf16[2,2,256,128]{3,2,1,0:T(8,128)(2,1)S(1)}, u32[]{:S(2)}, u32[]{:S(2)}) collective-permute-start(bf16[2,2,256,128]{3,2,1,0:T(8,128)(2,1)S(1)} %copy-done.10), channel_id=1, source_target_pairs={{0,5},{1,4},{2,7},{3,6},{4,1},{5,0},{6,3},{7,2},{8,13},{9,12},{10,... | collective-permute-start | bytes 786440 | tf_op jit(solution)/shard_map/ppermute | solution.py:190
  113.1 25.3 %collective-permute-start.24 = (bf16[8,16,128]{2,1,0:T(8,128)(2,1)S(1)}, bf16[8,16,128]{2,1,0:T(8,128)(2,1)S(1)}, u32[]{:S(2)}, u32[]{:S(2)}) collective-permute-start(bf16[8,16,128]{2,1,0:T(8,128)(2,1)S(1)} %copy-done.22), channel_id=1, source_target_pairs={{0,7},{1,6},{2,5},{3,4},{4,3},{5,2},{6,1},{7,0},{8,15},{9,14},{10,... | collective-permute-start | bytes 98312 | tf_op jit(solution)/shard_map/ppermute | solution.py:190
  140.5 37.2 %collective-permute-start.2 = (bf16[2,8,256,128]{3,2,1,0:T(8,128)(2,1)}, bf16[2,8,256,128]{3,2,1,0:T(8,128)(2,1)}, u32[]{:S(2)}, u32[]{:S(2)}) collective-permute-start(bf16[2,8,256,128]{3,2,1,0:T(8,128)(2,1)} %pad_maximum_fusion.2), channel_id=1, source_target_pairs={{0,3},{1,2},{2,1},{3,0},{4,7},{5,6},{6,5},{7,4},{8,11},{9,10},{10,... | collective-permute-start | bytes 3145736 | tf_op jit(solution)/shard_map/ppermute | solution.py:190
  146.0 88.5 %collective-permute-start.7 = (bf16[2,6,256,128]{3,2,1,0:T(8,128)(2,1)}, bf16[2,6,256,128]{3,2,1,0:T(8,128)(2,1)}, u32[]{:S(2)}, u32[]{:S(2)}) collective-permute-start(bf16[2,6,256,128]{3,2,1,0:T(8,128)(2,1)} %pad_maximum_fusion.7), channel_id=1, source_target_pairs={{0,4},{1,5},{2,6},{3,7},{4,0},{5,1},{6,2},{7,3},{8,12},{9,13},{10,... | collective-permute-start | bytes 2359304 | tf_op jit(solution)/shard_map/ppermute | solution.py:190
  153.3 98.1 %collective-permute-start.8 = (bf16[2,6,256,128]{3,2,1,0:T(8,128)(2,1)}, bf16[2,6,256,128]{3,2,1,0:T(8,128)(2,1)}, u32[]{:S(2)}, u32[]{:S(2)}) collective-permute-start(bf16[2,6,256,128]{3,2,1,0:T(8,128)(2,1)} %pad_maximum_fusion.8), channel_id=1, source_target_pairs={{0,5},{1,4},{2,7},{3,6},{4,1},{5,0},{6,3},{7,2},{8,13},{9,12},{10,... | collective-permute-start | bytes 2359304 | tf_op jit(solution)/shard_map/ppermute | solution.py:190
  153.3 133.2 %collective-permute-start.9 = (bf16[2,6,256,128]{3,2,1,0:T(8,128)(2,1)}, bf16[2,6,256,128]{3,2,1,0:T(8,128)(2,1)}, u32[]{:S(2)}, u32[]{:S(2)}) collective-permute-start(bf16[2,6,256,128]{3,2,1,0:T(8,128)(2,1)} %pad_maximum_fusion.9), channel_id=1, source_target_pairs={{0,6},{1,7},{2,4},{3,5},{4,2},{5,3},{6,0},{7,1},{8,14},{9,15},{10,... | collective-permute-start | bytes 2359304 | tf_op jit(solution)/shard_map/ppermute | solution.py:190
  154.2 184.3 %collective-permute-start.10 = (bf16[2,6,256,128]{3,2,1,0:T(8,128)(2,1)}, bf16[2,6,256,128]{3,2,1,0:T(8,128)(2,1)}, u32[]{:S(2)}, u32[]{:S(2)}) collective-permute-start(bf16[2,6,256,128]{3,2,1,0:T(8,128)(2,1)} %pad_maximum_fusion.10), channel_id=1, source_target_pairs={{0,7},{1,6},{2,5},{3,4},{4,3},{5,2},{6,1},{7,0},{8,15},{9,14},{10,... | collective-permute-start | bytes 2359304 | tf_op jit(solution)/shard_map/ppermute | solution.py:190
  177.8 250.6 %collective-permute-start.25 = (bf16[2,8,256,128]{3,2,1,0:T(8,128)(2,1)}, bf16[2,8,256,128]{3,2,1,0:T(8,128)(2,1)}, u32[]{:S(2)}, u32[]{:S(2)}) collective-permute-start(bf16[2,8,256,128]{3,2,1,0:T(8,128)(2,1)} %pad_maximum_fusion.3), channel_id=1, source_target_pairs={{0,1},{1,0},{2,3},{3,2},{4,5},{5,4},{6,7},{7,6},{8,9},{9,8},{10,11... | collective-permute-start | bytes 3145736 | tf_op jit(solution)/shard_map/ppermute | solution.py:190
  234.5 194.7 %collective-permute-start.26 = (bf16[2,8,256,128]{3,2,1,0:T(8,128)(2,1)}, bf16[2,8,256,128]{3,2,1,0:T(8,128)(2,1)}, u32[]{:S(2)}, u32[]{:S(2)}) collective-permute-start(bf16[2,8,256,128]{3,2,1,0:T(8,128)(2,1)} %pad_maximum_fusion.4), channel_id=1, source_target_pairs={{0,2},{1,3},{2,0},{3,1},{4,6},{5,7},{6,4},{7,5},{8,10},{9,11},{10,... | collective-permute-start | bytes 3145736 | tf_op jit(solution)/shard_map/ppermute | solution.py:190
  251.4 117.9 %collective-permute-start.32 = (bf16[2,6,256,128]{3,2,1,0:T(8,128)(2,1)}, bf16[2,6,256,128]{3,2,1,0:T(8,128)(2,1)S(1)}, u32[]{:S(2)}, u32[]{:S(2)}) collective-permute-start(bf16[2,6,256,128]{3,2,1,0:T(8,128)(2,1)} %pad_maximum_fusion.11), channel_id=1, source_target_pairs={{0,4},{1,5},{2,6},{3,7},{4,0},{5,1},{6,2},{7,3},{8,12},{9,13},{10,... | collective-permute-start | bytes 2359304 | tf_op jit(solution)/shard_map/ppermute | solution.py:190
  286.5 103.4 %collective-permute-start.33 = (bf16[2,6,256,128]{3,2,1,0:T(8,128)(2,1)}, bf16[2,6,256,128]{3,2,1,0:T(8,128)(2,1)}, u32[]{:S(2)}, u32[]{:S(2)}) collective-permute-start(bf16[2,6,256,128]{3,2,1,0:T(8,128)(2,1)} %pad_maximum_fusion.12), channel_id=1, source_target_pairs={{0,5},{1,4},{2,7},{3,6},{4,1},{5,0},{6,3},{7,2},{8,13},{9,12},{10,... | collective-permute-start | bytes 2359304 | tf_op jit(solution)/shard_map/ppermute | solution.py:190
  338.5 66.0 %collective-permute-start.34 = (bf16[2,6,256,128]{3,2,1,0:T(8,128)(2,1)}, bf16[2,6,256,128]{3,2,1,0:T(8,128)(2,1)}, u32[]{:S(2)}, u32[]{:S(2)}) collective-permute-start(bf16[2,6,256,128]{3,2,1,0:T(8,128)(2,1)} %pad_maximum_fusion.13), channel_id=1, source_target_pairs={{0,6},{1,7},{2,4},{3,5},{4,2},{5,3},{6,0},{7,1},{8,14},{9,15},{10,... | collective-permute-start | bytes 2359304 | tf_op jit(solution)/shard_map/ppermute | solution.py:190
  369.3 59.0 %collective-permute-start.35 = (bf16[2,6,256,128]{3,2,1,0:T(8,128)(2,1)}, bf16[2,6,256,128]{3,2,1,0:T(8,128)(2,1)}, u32[]{:S(2)}, u32[]{:S(2)}) collective-permute-start(bf16[2,6,256,128]{3,2,1,0:T(8,128)(2,1)} %pad_maximum_fusion.14), channel_id=1, source_target_pairs={{0,7},{1,6},{2,5},{3,4},{4,3},{5,2},{6,1},{7,0},{8,15},{9,14},{10,... | collective-permute-start | bytes 2359304 | tf_op jit(solution)/shard_map/ppermute | solution.py:190
  389.9 74.3 %collective-permute-start.27 = (bf16[2,8,256,128]{3,2,1,0:T(8,128)(2,1)}, bf16[2,8,256,128]{3,2,1,0:T(8,128)(2,1)}, u32[]{:S(2)}, u32[]{:S(2)}) collective-permute-start(bf16[2,8,256,128]{3,2,1,0:T(8,128)(2,1)} %pad_maximum_fusion.5), channel_id=1, source_target_pairs={{0,3},{1,2},{2,1},{3,0},{4,7},{5,6},{6,5},{7,4},{8,11},{9,10},{10,... | collective-permute-start | bytes 3145736 | tf_op jit(solution)/shard_map/ppermute | solution.py:190
  404.5 68.5 %collective-permute-start.28 = (bf16[2,2,256,128]{3,2,1,0:T(8,128)(2,1)}, bf16[2,2,256,128]{3,2,1,0:T(8,128)(2,1)S(1)}, u32[]{:S(2)}, u32[]{:S(2)}) collective-permute-start(bf16[2,2,256,128]{3,2,1,0:T(8,128)(2,1)} %pad_maximum_fusion.20), channel_id=1, source_target_pairs={{0,4},{1,5},{2,6},{3,7},{4,0},{5,1},{6,2},{7,3},{8,12},{9,13},{10,... | collective-permute-start | bytes 786440 | tf_op jit(solution)/shard_map/ppermute | solution.py:190
  428.4 44.6 %collective-permute-start.29 = (bf16[2,2,256,128]{3,2,1,0:T(8,128)(2,1)}, bf16[2,2,256,128]{3,2,1,0:T(8,128)(2,1)}, u32[]{:S(2)}, u32[]{:S(2)}) collective-permute-start(bf16[2,2,256,128]{3,2,1,0:T(8,128)(2,1)} %pad_maximum_fusion.21), channel_id=1, source_target_pairs={{0,5},{1,4},{2,7},{3,6},{4,1},{5,0},{6,3},{7,2},{8,13},{9,12},{10,... | collective-permute-start | bytes 786440 | tf_op jit(solution)/shard_map/ppermute | solution.py:190
  428.4 44.6 %collective-permute-start.30 = (bf16[2,2,256,128]{3,2,1,0:T(8,128)(2,1)}, bf16[2,2,256,128]{3,2,1,0:T(8,128)(2,1)}, u32[]{:S(2)}, u32[]{:S(2)}) collective-permute-start(bf16[2,2,256,128]{3,2,1,0:T(8,128)(2,1)} %pad_maximum_fusion.22), channel_id=1, source_target_pairs={{0,6},{1,7},{2,4},{3,5},{4,2},{5,3},{6,0},{7,1},{8,14},{9,15},{10,... | collective-permute-start | bytes 786440 | tf_op jit(solution)/shard_map/ppermute | solution.py:190
  429.2 43.9 %collective-permute-start.31 = (bf16[2,2,256,128]{3,2,1,0:T(8,128)(2,1)}, bf16[2,2,256,128]{3,2,1,0:T(8,128)(2,1)}, u32[]{:S(2)}, u32[]{:S(2)}) collective-permute-start(bf16[2,2,256,128]{3,2,1,0:T(8,128)(2,1)} %pad_maximum_fusion.23), channel_id=1, source_target_pairs={{0,7},{1,6},{2,5},{3,4},{4,3},{5,2},{6,1},{7,0},{8,15},{9,14},{10,... | collective-permute-start | bytes 786440 | tf_op jit(solution)/shard_map/ppermute | solution.py:190
  (39 other events, 545.9 us)

commit v2 on v1

--- a/solution.py
+++ b/solution.py
@@ -9,7 +9,9 @@
 EPS = 1e-6
 THETA = 1000000.0
 N_DEV = 8
-FIRST, LOCAL, LAST = 2, 8, 14
+FIRST, MIDDLE, LOCAL, LAST = 3, 7, 11, 15
+N_NEW = 4
+MAIN = 248
 
 
 def rms_norm(values, gain_vec):
@@ -59,26 +61,80 @@
 NN = (((1,), (0,)), ((), ()))
 
 
-def attend_one(pack, keys, values, pos):
-    q = pack[:16]
-    new_keys, new_values = pack[16:20], pack[20:24]
+def attend_one(q, keys, values, extra_keys, extra_values, main_end, tail_end):
     scale = q.shape[-1] ** -0.5
     old = lax.dot_general(q, keys, NT, preferred_element_type=jnp.float32) * scale
-    new = lax.dot_general(q, new_keys, NT, preferred_element_type=jnp.float32) * scale
-    slot = lax.broadcasted_iota(jnp.int32, old.shape, 1)
-    old = jnp.where(slot < pos, old, -jnp.inf)
+    new = lax.dot_general(q, extra_keys, NT, preferred_element_type=jnp.float32) * scale
+    old = jnp.where(lax.broadcasted_iota(jnp.int32, old.shape, 1) < main_end, old, -jnp.inf)
+    column = lax.broadcasted_iota(jnp.int32, new.shape, 1)
     step = lax.broadcasted_iota(jnp.int32, new.shape, 0) // 4
-    new = jnp.where(lax.broadcasted_iota(jnp.int32, new.shape, 1) <= step, new, -jnp.inf)
+    open_end = jnp.where(column < N_NEW, tail_end - MAIN, step + N_NEW + 1)
+    new = jnp.where(column < open_end, new, -jnp.inf)
     peak = jnp.maximum(jnp.max(old, axis=-1, keepdims=True), jnp.max(new, axis=-1, keepdims=True))
     old_w, new_w = jnp.exp(old - peak), jnp.exp(new - peak)
     total = jnp.sum(old_w, axis=-1, keepdims=True) + jnp.sum(new_w, axis=-1, keepdims=True)
     mixed = lax.dot_general(old_w.astype(jnp.bfloat16), values, NN, preferred_element_type=jnp.float32)
-    mixed = mixed + lax.dot_general(new_w.astype(jnp.bfloat16), new_values, NN, preferred_element_type=jnp.float32)
+    mixed = mixed + lax.dot_general(new_w.astype(jnp.bfloat16), extra_values, NN, preferred_element_type=jnp.float32)
     return (mixed / total).astype(jnp.bfloat16)
+
+
+def attend_whole(pack, keys, values, pos):
+    fresh = pack[16:].astype(jnp.float32)
+    extra_keys = pltpu.roll(fresh, N_NEW, 0).astype(jnp.bfloat16)
+    return attend_one(pack[:16], keys, values, extra_keys, pack[16:], pos, 0)
+
+
+def attend_block(pack, block_ref, pos):
+    fresh = pack[16:].astype(jnp.float32)
+    tail = block_ref[2 * MAIN:, :].astype(jnp.float32)
+    upper = lax.broadcasted_iota(jnp.int32, tail.shape, 0) < N_NEW
+    extra_keys = jnp.where(upper, tail, pltpu.roll(fresh, N_NEW, 0)).astype(jnp.bfloat16)
+    extra_values = jnp.where(upper, pltpu.roll(tail, N_NEW, 0), fresh).astype(jnp.bfloat16)
+    keys, values = block_ref[:MAIN + 8, :], block_ref[MAIN:, :]
+    return attend_one(pack[:16], keys, values, extra_keys, extra_values, jnp.minimum(pos, MAIN), pos)
+
+
+def without_new(values, pos):
+    values = values.astype(jnp.float32)
+    slot = lax.broadcasted_iota(jnp.int32, values.shape, 0)
+    return jnp.where(slot < pos, values, pltpu.roll(values, values.shape[0] - N_NEW, 0))
 
 
 def cache_specs(num_slots, head_dim, first_row):
     return pl.BlockSpec((1, num_slots, head_dim), lambda i, s: (first_row(s) + i, 0, 0))
+
+
+def pack_blocks(scalars, own, chunk, partners):
+    lo, hi = chunk
+    num_slots, head_dim = own[0].shape[1:]
+    count = len(partners)
+
+    def body(scal_ref, *refs):
+        key_refs, value_refs, out_refs = refs[:count], refs[count:2 * count], refs[2 * count:]
+        me = scal_ref[128]
+        for j, k in enumerate(partners):
+            pos = scal_ref[(me ^ k) * 16 + lo + pl.program_id(0)]
+            keys, values = without_new(key_refs[j][0], pos), without_new(value_refs[j][0], pos)
+            out_refs[j][0, :MAIN] = keys[:MAIN].astype(jnp.bfloat16)
+            out_refs[j][0, MAIN:2 * MAIN] = values[:MAIN].astype(jnp.bfloat16)
+            upper = lax.broadcasted_iota(jnp.int32, (8, head_dim), 0) < N_NEW
+            tail = jnp.where(upper, keys[MAIN:], pltpu.roll(values[MAIN:], N_NEW, 0))
+            out_refs[j][0, 2 * MAIN:] = tail.astype(jnp.bfloat16)
+
+    rows = [cache_specs(num_slots, head_dim, lambda s, k=k: (s[128] ^ k) * 16 + lo) for k in partners]
+    size = 2 * (num_slots - N_NEW)
+    return pl.pallas_call(
+        body,
+        grid_spec=pltpu.PrefetchScalarGridSpec(
+            num_scalar_prefetch=1,
+            grid=(hi - lo,),
+            in_specs=rows + rows,
+            out_specs=[pl.BlockSpec((1, size, head_dim), lambda i, s: (i, 0, 0))] * count,
+        ),
+        out_shape=[jax.ShapeDtypeStruct((hi - lo, size, head_dim), jnp.bfloat16)] * count,
+        cost_estimate=pl.CostEstimate(flops=(hi - lo) * count * 1_000_000, bytes_accessed=(hi - lo) * count * 260_000, transcendentals=0),
+        name="pack_blocks",
+    )(scalars, *[own[0]] * count, *[own[1]] * count)
 
 
 def remote_attend(scalars, caches, packs, offset):
@@ -92,7 +148,7 @@
         me = scal_ref[128]
         for k in range(N_DEV):
             pos = scal_ref[(me ^ k) * 16 + offset + seq]
-            out_refs[k][0] = attend_one(pack_refs[k][0], key_refs[k][0], value_refs[k][0], pos)
+            out_refs[k][0] = attend_whole(pack_refs[k][0], key_refs[k][0], value_refs[k][0], pos)
 
     rows = [cache_specs(num_slots, head_dim, lambda s, k=k: (s[128] ^ k) * 16 + offset) for k in range(N_DEV)]
     return pl.pallas_call(
@@ -129,24 +185,40 @@
         me = scal_ref[128]
         pos = scal_ref[me * 16 + lo + pl.program_id(0)]
 
-        def block(k, kind):
-            return own_refs[kind][0] if k == 0 else block_refs[k - 1][kind, 0]
-
         for kind in range(2):
             spread = spread_refs[kind]
             for k in range(N_DEV):
-                spread[pl.ds(me ^ k, num_slots, stride=N_DEV), :] = block(k, kind).astype(jnp.float32)
-            cache_refs[kind][0] = spread[...].reshape(num_slots, N_DEV, head_dim).astype(jnp.bfloat16)
+                if k == 0:
+                    kept = without_new(own_refs[kind][0], pos)
+                    main, tail = kept[:MAIN], kept[MAIN:]
+                else:
+                    main = block_refs[k - 1][0, kind * MAIN:(kind + 1) * MAIN].astype(jnp.float32)
+                    tail = block_refs[k - 1][0, 2 * MAIN:].astype(jnp.float32)
+                    tail = tail if kind == 0 else pltpu.roll(tail, N_NEW, 0)
+                spread[pl.ds(me ^ k, MAIN, stride=N_DEV), :] = main
+                spread[pl.ds(MAIN * N_DEV + (me ^ k), N_NEW, stride=N_DEV), :] = tail[:N_NEW]
+            fixed = num_slots // 4
+            kept = spread[:fixed * N_DEV, :].reshape(fixed, N_DEV, head_dim)
+            cache_refs[kind][0, :fixed] = kept.astype(jnp.bfloat16)
+            shape = (num_slots - fixed, N_DEV, head_dim)
+            before = spread[fixed * N_DEV:, :].reshape(shape)
+            after = spread[(fixed - N_NEW) * N_DEV:(num_slots - N_NEW) * N_DEV, :].reshape(shape)
+            slot = lax.broadcasted_iota(jnp.int32, shape, 0) + fixed
+            cache_refs[kind][0, fixed:] = jnp.where(slot < pos, before, after).astype(jnp.bfloat16)
             for step in range(n_steps):
                 cache_refs[kind][0, pos + step] = new_refs[kind][0, step]
         if with_attn:
             for k in range(N_DEV):
-                out_ref[0, me ^ k] = attend_one(pack_ref[0, me ^ k], block(k, 0), block(k, 1), pos)
+                pack = pack_ref[0, me ^ k]
+                if k == 0:
+                    out_ref[0, me ^ k] = attend_whole(pack, own_refs[0][0], own_refs[1][0], pos)
+                else:
+                    out_ref[0, me ^ k] = attend_block(pack, block_refs[k - 1].at[0], pos)
 
     cache_block = pl.BlockSpec((1, num_slots, N_DEV, head_dim), lambda i, s: (lo + i, 0, 0, 0))
     in_specs = [cache_specs(num_slots, head_dim, lambda s: s[128] * 16 + lo)] * 2
     in_specs += [
-        pl.BlockSpec((2, 1, num_slots, head_dim), lambda i, s, first=lo - first: (0, first + i, 0, 0))
+        pl.BlockSpec((1, 2 * (num_slots - N_NEW), head_dim), lambda i, s, first=lo - first: (first + i, 0, 0))
         for first, _ in blocks
     ]
     in_specs += [pl.BlockSpec((1, n_steps, N_DEV, head_dim), lambda i, s: (lo + i, 0, 0, 0))] * 2
@@ -184,7 +256,7 @@
     row_spec = P(None, ('dp', 'x'), None)
     cache_in = P('dp', None, 'x', None)
     cache_out = P(('dp', 'x'), None, None, None)
-    near, far = (2, 3, 1), (4, 5, 6, 7)
+    near, far = (2, 3, 1), (6, 7, 4, 5)
 
     def swap(value, k):
         return lax.ppermute(value, 'x', [(i, i ^ k) for i in range(N_DEV)])
@@ -198,11 +270,11 @@
         xor_heads = me ^ jnp.arange(N_DEV)
         own = tuple(c.reshape(N_DEV * num_rows, num_slots, head_dim) for c in (k_heads, v_heads))
 
-        def exchange(caches, lo, hi, partners):
-            return {
-                k: (lo, swap(jnp.stack([lax.dynamic_slice_in_dim(c, (me ^ k) * num_rows + lo, hi - lo) for c in caches]), k))
-                for k in partners
-            }
+        def exchange(packed, lo):
+            return {k: (lo, swap(block, k)) for k, block in packed.items()}
+
+        def packed(caches, lo, hi, partners):
+            return dict(zip(partners, pack_blocks(scalars, caches, (lo, hi), partners)))
 
         def swap_small(values):
             got = {k: swap(values[k], k) for k in near + far}
@@ -212,7 +284,8 @@
             merged = {k: v for part in parts for k, v in part.items()}
             return [merged[k] for k in range(1, N_DEV)]
 
-        far_first = exchange(own, 0, FIRST, far)
+        blocks = packed(own, 0, FIRST, far)
+        far_first = exchange(blocks, 0)
         positions = my_pos[None, :] + jnp.arange(n_steps)[:, None]
         queries, keys_new, values_new = project(hidden_in, positions, attn_norm, w_q, w_k, w_v, q_norm, k_norm)
         q_rows = jnp.transpose(queries.reshape(n_steps, num_rows, N_DEV, -1, head_dim), (1, 2, 0, 3, 4)).reshape(num_rows, N_DEV, -1, head_dim)
@@ -222,19 +295,25 @@
         new = jnp.swapaxes(keys_new, 0, 1), jnp.swapaxes(values_new, 0, 1)
         pack_r = jnp.take(jnp.swapaxes(pack[LOCAL:], 0, 1), xor_heads, axis=0)
         got_q = swap_small([pack_r[k] for k in range(N_DEV)])
-        *held, pack = lax.optimization_barrier((*own, pack))
-        near_local = exchange(held, 0, LOCAL, near)
-        far_local = exchange(held, FIRST, LOCAL, far)
+        near_blocks = packed(own, 0, LOCAL, near)
+        middle_blocks = packed(own, FIRST, MIDDLE, far)
+        local_blocks = packed(own, MIDDLE, LOCAL, far)
+        near_local = exchange(near_blocks, 0)
+        far_middle = exchange(middle_blocks, FIRST)
+        far_local = exchange(local_blocks, MIDDLE)
         o_r = remote_attend(scalars, own, got_q, LOCAL)
         got_o = swap_small(o_r)
-        *held, _ = lax.optimization_barrier((*held, o_r[0]))
-        near_rest = exchange(held, LOCAL, num_rows, near)
-        far_rest = exchange(held, LOCAL, LAST, far)
-        far_last = exchange(held, LAST, num_rows, far)
+        near_blocks = packed(own, LOCAL, num_rows, near)
+        rest_blocks = packed(own, LOCAL, LAST, far)
+        last_blocks = packed(own, LAST, num_rows, far)
+        near_rest = exchange(near_blocks, LOCAL)
+        far_rest = exchange(rest_blocks, LOCAL)
+        far_last = exchange(last_blocks, LAST)
         *caches, o_a = settle(scalars, own, chosen(near_local, far_first), *new, pack, None, (0, FIRST), num_rows)
-        *caches, o_b = settle(scalars, own, chosen(near_local, far_local), *new, pack, caches, (FIRST, LOCAL), num_rows)
+        *caches, o_b = settle(scalars, own, chosen(near_local, far_middle), *new, pack, caches, (FIRST, MIDDLE), num_rows)
+        *caches, o_c = settle(scalars, own, chosen(near_local, far_local), *new, pack, caches, (MIDDLE, LOCAL), num_rows)
         o_r = jnp.swapaxes(jnp.take(jnp.stack(got_o), xor_heads, axis=0), 0, 1)
-        attended = jnp.concatenate([o_a, o_b, o_r], axis=0).reshape(num_rows, N_DEV, n_steps, -1, head_dim)
+        attended = jnp.concatenate([o_a, o_b, o_c, o_r], axis=0).reshape(num_rows, N_DEV, n_steps, -1, head_dim)
         attended = jnp.transpose(attended, (2, 0, 1, 3, 4)).reshape(n_steps, num_rows, -1)
         out_hidden = finish(hidden_in, attended, w_o, mlp_norm, w_gate, w_up, w_down)
         caches = settle(scalars, own, chosen(near_rest, far_rest), *new, None, caches, (LOCAL, LAST), num_rows)

time: 485 us -> 475 us (0.979)
  waiting for transfers between devices: 253 us -> 189 us
  starting transfers between devices: 35.5 us -> 82.8 us
  Pallas kernels: 63.1 us -> 102 us
  other arithmetic: 27 us -> 5.92 us
  local copies, waits for them, and re-layouts: 17.9 us -> 6.18 us
    ppermute x36 -> x40, waiting for transfers between devices: 253 us -> 189 us  [swap(): return lax.ppermute(value, 'x', [(i, i ^ k) for i in range(N_DEV)])]
    ppermute x36 -> x40, starting transfers between devices: 35.5 us -> 82.8 us  [swap(): return lax.ppermute(value, 'x', [(i, i ^ k) for i in range(N_DEV)])]
    pallas_call x0 -> x7, Pallas kernels: none -> 35.2 us  [pack_blocks(): pl.pallas_call(body, grid_spec=pltpu.PrefetchScalarGridSpec(num_scalar_pr...]
    another operation x24 -> x2, other arithmetic: 20 us -> 0.62 us  [the longest x22 19.3 us: exchange(): jnp.stack([lax.dynamic_slice_in_dim(c, (me ^ k) * num_rows + lo, hi - lo)...]
    pallas_call x4 -> x5, Pallas kernels: 40.8 us -> 51.8 us  [settle(): pl.pallas_call(body, grid_spec=pltpu.PrefetchScalarGridSpec(num_scalar_pr...]
    another operation x6 -> x0, local copies, waits for them, and re-layouts: 10.9 us -> none  [exchange(): jnp.stack([lax.dynamic_slice_in_dim(c, (me ^ k) * num_rows + lo, hi - lo)...]
    pallas_call x1, Pallas kernels: 22.4 us -> 14.8 us  [remote_attend(): pl.pallas_call(body, grid_spec=pltpu.PrefetchScalarGridSpec(num_scalar_pr...]
  transfers between devices with their start and end apart: 36 -> 40, of which waited for: 12 -> 16; matrix products, arithmetic and copies ran while one was open for 21% -> 19% of each run, Pallas kernels for 12% -> 20%
where the time goes in v2:
time: 475 us; the launch traced here: 467 us
  waiting for transfers between devices  189 us (40%)
  Pallas kernels  102 us (21%)
  starting transfers between devices  82.8 us (17%)
  matrix products  79.6 us (17%)
  local copies, waits for them, and re-layouts  6.18 us (1%)
  other arithmetic  5.92 us (1%)
    ppermute x40, waiting for transfers between devices, swap(): return lax.ppermute(value, 'x', [(i, i ^ k) for i in range(N_DEV)])  189 us
    ppermute x40, starting transfers between devices, swap(): return lax.ppermute(value, 'x', [(i, i ^ k) for i in range(N_DEV)])  82.8 us
    pallas_call x5, Pallas kernels, settle(): pl.pallas_call(body, grid_spec=pltpu.PrefetchScalarGridSpec(num_scalar_pr...  51.8 us
    pallas_call x7, Pallas kernels, pack_blocks(): pl.pallas_call(body, grid_spec=pltpu.PrefetchScalarGridSpec(num_scalar_pr...  35.2 us
    dot_general x1, matrix products, finish(): jnp.einsum('sbf,fd->sbd', activated, w_down, preferred_element_type=jnp.f...  34.9 us
    dot_general x1, matrix products, finish(): jnp.einsum('sbd,df->sbf', normed, w_gate, preferred_element_type=jnp.floa...  19.6 us
    pallas_call x1, Pallas kernels, remote_attend(): pl.pallas_call(body, grid_spec=pltpu.PrefetchScalarGridSpec(num_scalar_pr...  14.8 us
  transfers between devices with their start and end apart: 40, of which 16 were waited for; matrix products, arithmetic and copies ran while one was open for 19% of the time, Pallas kernels for 20%

profile of v2, /device:TPU:17, one launch (start us, length us, event | category | flops | bytes accessed | tf_op | source)
XLA Modules:
  0.0 466.7 jit_solution(18053969106110786030)
XLA Ops:
  1.9 4.4 pack_blocks.8
  18.9 9.0 %fusion.8 = f32[4,16,4096]{2,1,0:T(8,128)S(1)} fusion(bf16[2560,4096]{1,0:T(8,128)(2,1)} %param.20, bf16[4,16,2560]{2,1,0:T(8,128)(2,1)S(1)} %copy-done.3, f32[2560]{0:T(1024)S(1)} %convert_element_type.53, f32[4,16]{1,0:T(4,128)S(1)} %add_rsqrt_fusion.3), kind=kOutput, calls=%fused_computation.10 | convolution fusion | flops 1342832640 | bytes 22358272 | tf_op jit(solution)/shard_map/sbd,de->sbe/dot_general | solution.py:39
  48.6 14.8 %remote_attend.1 = (bf16[5,16,128]{2,1,0:T(8,128)(2,1)}, bf16[5,16,128]{2,1,0:T(8,128)(2,1)}, bf16[5,16,128]{2,1,0:T(8,128)(2,1)}, bf16[5,16,128]{2,1,0:T(8,128)...) custom-call(s32[129]{0:T(256)} %pad_add_fusion.scal_ref, ...), custom_call_target="tpu_custom_call" | custom-call | flops 200000000 | bytes 5500000 | tf_op jit(solution)/shard_map/remote_attend/pallas_call | solution.py:154
  63.5 5.4 %collective-permute-start.23 = (bf16[5,16,128]{2,1,0:T(8,128)(2,1)}, bf16[5,16,128]{2,1,0:T(8,128)(2,1)S(1)}, u32[]{:S(2)}, u32[]{:S(2)}) collective-permute-start(bf16[5,16,128]{2,1,0:T(8,128)(2,1)} %get-tuple-element.74), channel_id=1, source_target_pairs={{0,2},{1,3},{2,0},{3,1},{4,6},{5,7},{6,4},{7,5},{8,10},{9,11},{10,... | collective-permute-start | bytes 61448 | tf_op jit(solution)/shard_map/ppermute | solution.py:262
  78.6 8.8 %pack_blocks.7 = (bf16[11,504,128]{2,1,0:T(8,128)(2,1)}, bf16[11,504,128]{2,1,0:T(8,128)(2,1)}, bf16[11,504,128]{2,1,0:T(8,128)(2,1)}) custom-call(s32[129]{0:T(256)} %pad_add_fusion.scal_ref, bf16[128,256,128]{2,1,0:T(8,128)(2,1)} %bitcast.153, bf16[128,256,128]{2,1,0:T(8,128)(2,1)} %bitcast.154, bf16[128,256,128]{2,1,0:T(8,128)(2,1)} %bitcast.155, ...), custom_call_target="tpu_custom_call" | custom-call | flops 33000000 | bytes 8580000 | tf_op jit(solution)/shard_map/pack_blocks/pallas_call | solution.py:126
  94.0 5.1 %pack_blocks.11 = (bf16[5,504,128]{2,1,0:T(8,128)(2,1)}, bf16[5,504,128]{2,1,0:T(8,128)(2,1)}, bf16[5,504,128]{2,1,0:T(8,128)(2,1)}) custom-call(s32[129]{0:T(256)} %pad_add_fusion.scal_ref, bf16[128,256,128]{2,1,0:T(8,128)(2,1)} %bitcast.160, bf16[128,256,128]{2,1,0:T(8,128)(2,1)} %bitcast.161, bf16[128,256,128]{2,1,0:T(8,128)(2,1)} %bitcast.162, ...), custom_call_target="tpu_custom_call" | custom-call | flops 15000000 | bytes 3900000 | tf_op jit(solution)/shard_map/pack_blocks/pallas_call | solution.py:126
  99.2 4.7 %pack_blocks.9 = (bf16[4,504,128]{2,1,0:T(8,128)(2,1)}, bf16[4,504,128]{2,1,0:T(8,128)(2,1)}, bf16[4,504,128]{2,1,0:T(8,128)(2,1)}, bf16[4,504,128]{2,1,0:T(8,128)(2,1)}) custom-call(s32[129]{0:T(256)} %pad_add_fusion.scal_ref, bf16[128,256,128]{2,1,0:T(8,128)(2,1)} %bitcast.163, bf16[128,256,128]{2,1,0:T(8,128)(2,1)} %bitcast.164, ...), custom_call_target="tpu_custom_call" | custom-call | flops 16000000 | bytes 4160000 | tf_op jit(solution)/shard_map/pack_blocks/pallas_call | solution.py:126
  103.9 4.7 %pack_blocks.10 = (bf16[4,504,128]{2,1,0:T(8,128)(2,1)}, bf16[4,504,128]{2,1,0:T(8,128)(2,1)}, bf16[4,504,128]{2,1,0:T(8,128)(2,1)}, bf16[4,504,128]{2,1,0:T(8,128)(2,1)}) custom-call(s32[129]{0:T(256)} %pad_add_fusion.scal_ref, bf16[128,256,128]{2,1,0:T(8,128)(2,1)} %bitcast.167, bf16[128,256,128]{2,1,0:T(8,128)(2,1)} %bitcast.168, ...), custom_call_target="tpu_custom_call" | custom-call | flops 16000000 | bytes 4160000 | tf_op jit(solution)/shard_map/pack_blocks/pallas_call | solution.py:126
  108.6 4.7 %pack_blocks.13 = (bf16[4,504,128]{2,1,0:T(8,128)(2,1)}, bf16[4,504,128]{2,1,0:T(8,128)(2,1)}, bf16[4,504,128]{2,1,0:T(8,128)(2,1)}, bf16[4,504,128]{2,1,0:T(8,128)(2,1)}) custom-call(s32[129]{0:T(256)} %pad_add_fusion.scal_ref, bf16[128,256,128]{2,1,0:T(8,128)(2,1)} %bitcast.171, bf16[128,256,128]{2,1,0:T(8,128)(2,1)} %bitcast.172, ...), custom_call_target="tpu_custom_call" | custom-call | flops 16000000 | bytes 4160000 | tf_op jit(solution)/shard_map/pack_blocks/pallas_call | solution.py:126
  115.2 20.8 %collective-permute-done.6.refs_8_ = bf16[3,504,128]{2,1,0:T(8,128)(2,1)S(1)} collective-permute-done((bf16[3,504,128]{2,1,0:T(8,128)(2,1)}, bf16[3,504,128]{2,1,0:T(8,128)(2,1)S(1)}, u32[]{:S(2)}, u32[]{:S(2)}) %collective-permute-start.6) | collective-permute-done | bytes 387104 | tf_op jit(solution)/shard_map/ppermute | solution.py:262
  136.8 37.7 %collective-permute-start.7 = (bf16[4,504,128]{2,1,0:T(8,128)(2,1)}, bf16[4,504,128]{2,1,0:T(8,128)(2,1)S(1)}, u32[]{:S(2)}, u32[]{:S(2)}) collective-permute-start(bf16[4,504,128]{2,1,0:T(8,128)(2,1)} %get-tuple-element.58), channel_id=1, source_target_pairs={{0,4},{1,5},{2,6},{3,7},{4,0},{5,1},{6,2},{7,3},{8,12},{9,13},{10,... | collective-permute-start | bytes 1548296 | tf_op jit(solution)/shard_map/ppermute | solution.py:262
  174.6 32.1 %collective-permute-done.7.refs_5_ = bf16[4,504,128]{2,1,0:T(8,128)(2,1)S(1)} collective-permute-done((bf16[4,504,128]{2,1,0:T(8,128)(2,1)}, bf16[4,504,128]{2,1,0:T(8,128)(2,1)S(1)}, u32[]{:S(2)}, u32[]{:S(2)}) %collective-permute-start.7) | collective-permute-done | bytes 516128 | tf_op jit(solution)/shard_map/ppermute | solution.py:262
  207.7 21.0 %collective-permute-done.8.refs_6_ = bf16[4,504,128]{2,1,0:T(8,128)(2,1)S(1)} collective-permute-done((bf16[4,504,128]{2,1,0:T(8,128)(2,1)}, bf16[4,504,128]{2,1,0:T(8,128)(2,1)S(1)}, u32[]{:S(2)}, u32[]{:S(2)}) %collective-permute-start.8) | collective-permute-done | bytes 516128 | tf_op jit(solution)/shard_map/ppermute | solution.py:262
  234.9 11.7 %settle.5 = (bf16[16,256,8,128]{3,2,1,0:T(8,128)(2,1)}, bf16[16,256,8,128]{3,2,1,0:T(8,128)(2,1)}, bf16[3,8,16,128]{3,2,1,0:T(8,128)(2,1)}) custom-call(s32[129]{0:T(256)} %pad_add_fusion.scal_ref, bf16[128,256,128]{2,1,0:T(8,128)(2,1)} %bitcast.175, bf16[128,256,128]{2,1,0:T(8,128)(2,1)} %bitcast.214, bf16[11,504,128]{2,1,0:T(8,128)(2,1)} %copy-done.1, ...), custom_call_target="tpu_custom_call" | custom-call | flops 180000000 | bytes 6600000 | tf_op jit(solution)/shard_map/settle/pallas_call | solution.py:239
  246.6 39.3 %collective-permute-done.9.refs_7_ = bf16[4,504,128]{2,1,0:T(8,128)(2,1)} collective-permute-done((bf16[4,504,128]{2,1,0:T(8,128)(2,1)}, bf16[4,504,128]{2,1,0:T(8,128)(2,1)}, u32[]{:S(2)}, u32[]{:S(2)}) %collective-permute-start.9) | collective-permute-done | bytes 516128 | tf_op jit(solution)/shard_map/ppermute | solution.py:262
  287.1 14.9 %settle.6 = (bf16[16,256,8,128]{3,2,1,0:T(8,128)(2,1)}, bf16[16,256,8,128]{3,2,1,0:T(8,128)(2,1)}, bf16[4,8,16,128]{3,2,1,0:T(8,128)(2,1)}) custom-call(s32[129]{0:T(256)} %pad_add_fusion.scal_ref, bf16[128,256,128]{2,1,0:T(8,128)(2,1)} %bitcast.176, bf16[128,256,128]{2,1,0:T(8,128)(2,1)} %bitcast.215, ...), custom_call_target="tpu_custom_call", output_to_operand_aliasing={{0}: (13, {}), {1}: (14, {})} | custom-call | flops 240000000 | bytes 8800000 | tf_op jit(solution)/shard_map/settle/pallas_call | solution.py:239
  309.3 20.8 %collective-permute-done.13.refs_7_ = bf16[4,504,128]{2,1,0:T(8,128)(2,1)} collective-permute-done((bf16[4,504,128]{2,1,0:T(8,128)(2,1)}, bf16[4,504,128]{2,1,0:T(8,128)(2,1)}, u32[]{:S(2)}, u32[]{:S(2)}) %collective-permute-start.13) | collective-permute-done | bytes 516128 | tf_op jit(solution)/shard_map/ppermute | solution.py:262
  330.2 33.7 %collective-permute-done.14.refs_8_ = bf16[4,504,128]{2,1,0:T(8,128)(2,1)} collective-permute-done((bf16[4,504,128]{2,1,0:T(8,128)(2,1)}, bf16[4,504,128]{2,1,0:T(8,128)(2,1)}, u32[]{:S(2)}, u32[]{:S(2)}) %collective-permute-start.14) | collective-permute-done | bytes 516128 | tf_op jit(solution)/shard_map/ppermute | solution.py:262
  363.9 14.9 %settle.7 = (bf16[16,256,8,128]{3,2,1,0:T(8,128)(2,1)}, bf16[16,256,8,128]{3,2,1,0:T(8,128)(2,1)}, bf16[4,8,16,128]{3,2,1,0:T(8,128)(2,1)}) custom-call(s32[129]{0:T(256)} %pad_add_fusion.scal_ref, bf16[128,256,128]{2,1,0:T(8,128)(2,1)} %bitcast.177, bf16[128,256,128]{2,1,0:T(8,128)(2,1)} %bitcast.216, ...), custom_call_target="tpu_custom_call", output_to_operand_aliasing={{0}: (13, {}), {1}: (14, {})} | custom-call | flops 240000000 | bytes 8800000 | tf_op jit(solution)/shard_map/settle/pallas_call | solution.py:239
  380.4 9.0 %multiply_reduce_fusion = (f32[4,16]{1,0:T(4,128)S(1)}, f32[4,16,2560]{2,1,0:T(8,128)S(1)}) fusion(bf16[4,16,4096]{2,1,0:T(8,128)(2,1)S(1)} %reshape.132, bf16[4096,2560]{1,0:T(8,128)(2,1)} %param.25, bf16[4,16,2560]{2,1,0:T(8,128)(2,1)S(1)} %copy-done.4), kind=kOutput, calls=%fused_computation.43 | convolution fusion | flops 1343160320 | bytes 22479104 | tf_op jit(solution)/shard_map/sbe,ed->sbd/dot_general | solution.py:50
  390.9 19.6 %fusion.4 = f32[4,16,9728]{2,1,0:T(8,128)S(1)} fusion(bf16[2560,9728]{1,0:T(8,128)(2,1)} %param.27, f32[4,16,2560]{2,1,0:T(8,128)S(1)} %get-tuple-element.114, f32[2560]{0:T(1024)S(1)} %convert_element_type.62, f32[4,16]{1,0:T(4,128)S(1)} %add_rsqrt_fusion.2), kind=kOutput, calls=%fused_computation.6 | convolution fusion | flops 3188162560 | bytes 52963584 | tf_op jit(solution)/shard_map/sbd,df->sbf/dot_general | solution.py:53
  412.6 6.9 %collective-permute-done.39.refs_8_ = bf16[4,504,128]{2,1,0:T(8,128)(2,1)} collective-permute-done((bf16[4,504,128]{2,1,0:T(8,128)(2,1)}, bf16[4,504,128]{2,1,0:T(8,128)(2,1)}, u32[]{:S(2)}, u32[]{:S(2)}) %collective-permute-start.39) | collective-permute-done | bytes 516128 | tf_op jit(solution)/shard_map/ppermute | solution.py:262
  420.7 34.9 %fusion.30 = bf16[4,16,2560]{2,1,0:T(8,128)(2,1)} fusion(f32[4,16,2560]{2,1,0:T(8,128)S(1)} %get-tuple-element.114, bf16[9728,2560]{1,0:T(8,128)(2,1)} %param.29, bf16[2560,9728]{1,0:T(8,128)(2,1)} %param.28, f32[4,16,9728]{2,1,0:T(8,128)S(1)} %fusion.4, f32[2560]{0:T(1024)S(1)} %convert_element_type.62, f32[4,16]{1,0:T(4,128)S(1)} %add_rsqrt_fusion.2), kind=kOutput, calls=%fused_computation.20 | convolution fusion | flops 6379896832 | bytes 103098624 | tf_op jit(solution)/shard_map/sbf,fd->sbd/dot_general | solution.py:56
  455.6 6.8 %settle.8 = (bf16[16,256,8,128]{3,2,1,0:T(8,128)(2,1)}, bf16[16,256,8,128]{3,2,1,0:T(8,128)(2,1)}) custom-call(s32[129]{0:T(256)} %pad_add_fusion.scal_ref, bf16[128,256,128]{2,1,0:T(8,128)(2,1)} %bitcast.178, bf16[128,256,128]{2,1,0:T(8,128)(2,1)} %bitcast.217, ...), custom_call_target="tpu_custom_call", output_to_operand_aliasing={{0}: (12, {}), {1}: (13, {})} | custom-call | flops 240000000 | bytes 8800000 | tf_op jit(solution)/shard_map/settle/pallas_call | solution.py:239
  (188 shorter events, 79.5 us)
Async XLA Ops:
  6.3 84.0 %collective-permute-start.3 = (bf16[3,504,128]{2,1,0:T(8,128)(2,1)}, bf16[3,504,128]{2,1,0:T(8,128)(2,1)S(1)}, u32[]{:S(2)}, u32[]{:S(2)}) collective-permute-start(bf16[3,504,128]{2,1,0:T(8,128)(2,1)} %get-tuple-element.53), channel_id=1, source_target_pairs={{0,4},{1,5},{2,6},{3,7},{4,0},{5,1},{6,2},{7,3},{8,12},{9,13},{10,... | collective-permute-start | bytes 1161224 | tf_op jit(solution)/shard_map/ppermute | solution.py:262
  6.4 106.9 %collective-permute-start.4 = (bf16[3,504,128]{2,1,0:T(8,128)(2,1)}, bf16[3,504,128]{2,1,0:T(8,128)(2,1)}, u32[]{:S(2)}, u32[]{:S(2)}) collective-permute-start(bf16[3,504,128]{2,1,0:T(8,128)(2,1)} %get-tuple-element.54), channel_id=1, source_target_pairs={{0,5},{1,4},{2,7},{3,6},{4,1},{5,0},{6,3},{7,2},{8,13},{9,12},{10,... | collective-permute-start | bytes 1161224 | tf_op jit(solution)/shard_map/ppermute | solution.py:262
  45.1 68.4 %collective-permute-start.5 = (bf16[3,504,128]{2,1,0:T(8,128)(2,1)}, bf16[3,504,128]{2,1,0:T(8,128)(2,1)}, u32[]{:S(2)}, u32[]{:S(2)}) collective-permute-start(bf16[3,504,128]{2,1,0:T(8,128)(2,1)} %get-tuple-element.55), channel_id=1, source_target_pairs={{0,6},{1,7},{2,4},{3,5},{4,2},{5,3},{6,0},{7,1},{8,14},{9,15},{10,... | collective-permute-start | bytes 1161224 | tf_op jit(solution)/shard_map/ppermute | solution.py:262
  87.5 144.3 %collective-permute-start = (bf16[11,504,128]{2,1,0:T(8,128)(2,1)}, bf16[11,504,128]{2,1,0:T(8,128)(2,1)S(1)}, u32[]{:S(2)}, u32[]{:S(2)}) collective-permute-start(bf16[11,504,128]{2,1,0:T(8,128)(2,1)} %get-tuple-element.50), channel_id=1, source_target_pairs={{0,1},{1,0},{2,3},{3,2},{4,5},{5,4},{6,7},{7,6},{8,9},{9,8},{10,11... | collective-permute-start | bytes 4257800 | tf_op jit(solution)/shard_map/ppermute | solution.py:262
  87.5 144.6 %collective-permute-start.1 = (bf16[11,504,128]{2,1,0:T(8,128)(2,1)}, bf16[11,504,128]{2,1,0:T(8,128)(2,1)S(1)}, u32[]{:S(2)}, u32[]{:S(2)}) collective-permute-start(bf16[11,504,128]{2,1,0:T(8,128)(2,1)} %get-tuple-element.51), channel_id=1, source_target_pairs={{0,2},{1,3},{2,0},{3,1},{4,6},{5,7},{6,4},{7,5},{8,10},{9,11},{10,... | collective-permute-start | bytes 4257800 | tf_op jit(solution)/shard_map/ppermute | solution.py:262
  91.1 142.6 %collective-permute-start.2 = (bf16[11,504,128]{2,1,0:T(8,128)(2,1)}, bf16[11,504,128]{2,1,0:T(8,128)(2,1)}, u32[]{:S(2)}, u32[]{:S(2)}) collective-permute-start(bf16[11,504,128]{2,1,0:T(8,128)(2,1)} %get-tuple-element.52), channel_id=1, source_target_pairs={{0,3},{1,2},{2,1},{3,0},{4,7},{5,6},{6,5},{7,4},{8,11},{9,10},{10,... | collective-permute-start | bytes 4257800 | tf_op jit(solution)/shard_map/ppermute | solution.py:262
  113.3 61.2 %collective-permute-start.10 = (bf16[4,504,128]{2,1,0:T(8,128)(2,1)}, bf16[4,504,128]{2,1,0:T(8,128)(2,1)S(1)}, u32[]{:S(2)}, u32[]{:S(2)}) collective-permute-start(bf16[4,504,128]{2,1,0:T(8,128)(2,1)} %get-tuple-element.61), channel_id=1, source_target_pairs={{0,7},{1,6},{2,5},{3,4},{4,3},{5,2},{6,1},{7,0},{8,15},{9,14},{10,... | collective-permute-start | bytes 1548296 | tf_op jit(solution)/shard_map/ppermute | solution.py:262
  136.8 69.9 %collective-permute-start.7 = (bf16[4,504,128]{2,1,0:T(8,128)(2,1)}, bf16[4,504,128]{2,1,0:T(8,128)(2,1)S(1)}, u32[]{:S(2)}, u32[]{:S(2)}) collective-permute-start(bf16[4,504,128]{2,1,0:T(8,128)(2,1)} %get-tuple-element.58), channel_id=1, source_target_pairs={{0,4},{1,5},{2,6},{3,7},{4,0},{5,1},{6,2},{7,3},{8,12},{9,13},{10,... | collective-permute-start | bytes 1548296 | tf_op jit(solution)/shard_map/ppermute | solution.py:262
  174.5 54.3 %collective-permute-start.8 = (bf16[4,504,128]{2,1,0:T(8,128)(2,1)}, bf16[4,504,128]{2,1,0:T(8,128)(2,1)S(1)}, u32[]{:S(2)}, u32[]{:S(2)}) collective-permute-start(bf16[4,504,128]{2,1,0:T(8,128)(2,1)} %get-tuple-element.59), channel_id=1, source_target_pairs={{0,5},{1,4},{2,7},{3,6},{4,1},{5,0},{6,3},{7,2},{8,13},{9,12},{10,... | collective-permute-start | bytes 1548296 | tf_op jit(solution)/shard_map/ppermute | solution.py:262
  206.7 79.2 %collective-permute-start.9 = (bf16[4,504,128]{2,1,0:T(8,128)(2,1)}, bf16[4,504,128]{2,1,0:T(8,128)(2,1)}, u32[]{:S(2)}, u32[]{:S(2)}) collective-permute-start(bf16[4,504,128]{2,1,0:T(8,128)(2,1)} %get-tuple-element.60), channel_id=1, source_target_pairs={{0,6},{1,7},{2,4},{3,5},{4,2},{5,3},{6,0},{7,1},{8,14},{9,15},{10,... | collective-permute-start | bytes 1548296 | tf_op jit(solution)/shard_map/ppermute | solution.py:262
  228.8 73.2 %collective-permute-start.11 = (bf16[4,504,128]{2,1,0:T(8,128)(2,1)}, bf16[4,504,128]{2,1,0:T(8,128)(2,1)}, u32[]{:S(2)}, u32[]{:S(2)}) collective-permute-start(bf16[4,504,128]{2,1,0:T(8,128)(2,1)} %get-tuple-element.65), channel_id=1, source_target_pairs={{0,4},{1,5},{2,6},{3,7},{4,0},{5,1},{6,2},{7,3},{8,12},{9,13},{10,... | collective-permute-start | bytes 1548296 | tf_op jit(solution)/shard_map/ppermute | solution.py:262
  231.8 74.5 %collective-permute-start.12 = (bf16[4,504,128]{2,1,0:T(8,128)(2,1)}, bf16[4,504,128]{2,1,0:T(8,128)(2,1)}, u32[]{:S(2)}, u32[]{:S(2)}) collective-permute-start(bf16[4,504,128]{2,1,0:T(8,128)(2,1)} %get-tuple-element.66), channel_id=1, source_target_pairs={{0,5},{1,4},{2,7},{3,6},{4,1},{5,0},{6,3},{7,2},{8,13},{9,12},{10,... | collective-permute-start | bytes 1548296 | tf_op jit(solution)/shard_map/ppermute | solution.py:262
  232.1 98.0 %collective-permute-start.13 = (bf16[4,504,128]{2,1,0:T(8,128)(2,1)}, bf16[4,504,128]{2,1,0:T(8,128)(2,1)}, u32[]{:S(2)}, u32[]{:S(2)}) collective-permute-start(bf16[4,504,128]{2,1,0:T(8,128)(2,1)} %get-tuple-element.67), channel_id=1, source_target_pairs={{0,6},{1,7},{2,4},{3,5},{4,2},{5,3},{6,0},{7,1},{8,14},{9,15},{10,... | collective-permute-start | bytes 1548296 | tf_op jit(solution)/shard_map/ppermute | solution.py:262
  233.7 130.3 %collective-permute-start.14 = (bf16[4,504,128]{2,1,0:T(8,128)(2,1)}, bf16[4,504,128]{2,1,0:T(8,128)(2,1)}, u32[]{:S(2)}, u32[]{:S(2)}) collective-permute-start(bf16[4,504,128]{2,1,0:T(8,128)(2,1)} %get-tuple-element.68), channel_id=1, source_target_pairs={{0,7},{1,6},{2,5},{3,4},{4,3},{5,2},{6,1},{7,0},{8,15},{9,14},{10,... | collective-permute-start | bytes 1548296 | tf_op jit(solution)/shard_map/ppermute | solution.py:262
  285.9 133.6 %collective-permute-start.29 = (bf16[5,504,128]{2,1,0:T(8,128)(2,1)}, bf16[5,504,128]{2,1,0:T(8,128)(2,1)}, u32[]{:S(2)}, u32[]{:S(2)}) collective-permute-start(bf16[5,504,128]{2,1,0:T(8,128)(2,1)} %get-tuple-element.80), channel_id=1, source_target_pairs={{0,1},{1,0},{2,3},{3,2},{4,5},{5,4},{6,7},{7,6},{8,9},{9,8},{10,11... | collective-permute-start | bytes 1935368 | tf_op jit(solution)/shard_map/ppermute | solution.py:262
  302.0 117.5 %collective-permute-start.30 = (bf16[5,504,128]{2,1,0:T(8,128)(2,1)}, bf16[5,504,128]{2,1,0:T(8,128)(2,1)}, u32[]{:S(2)}, u32[]{:S(2)}) collective-permute-start(bf16[5,504,128]{2,1,0:T(8,128)(2,1)} %get-tuple-element.81), channel_id=1, source_target_pairs={{0,2},{1,3},{2,0},{3,1},{4,6},{5,7},{6,4},{7,5},{8,10},{9,11},{10,... | collective-permute-start | bytes 1935368 | tf_op jit(solution)/shard_map/ppermute | solution.py:262
  306.2 83.1 %collective-permute-start.36 = (bf16[4,504,128]{2,1,0:T(8,128)(2,1)S(1)}, bf16[4,504,128]{2,1,0:T(8,128)(2,1)S(1)}, u32[]{:S(2)}, u32[]{:S(2)}) collective-permute-start(bf16[4,504,128]{2,1,0:T(8,128)(2,1)S(1)} %copy-done.27), channel_id=1, source_target_pairs={{0,4},{1,5},{2,6},{3,7},{4,0},{5,1},{6,2},{7,3},{8,12},{9,13},{10,... | collective-permute-start | bytes 1548296 | tf_op jit(solution)/shard_map/ppermute | solution.py:262
  330.2 80.4 %collective-permute-start.37 = (bf16[4,504,128]{2,1,0:T(8,128)(2,1)}, bf16[4,504,128]{2,1,0:T(8,128)(2,1)}, u32[]{:S(2)}, u32[]{:S(2)}) collective-permute-start(bf16[4,504,128]{2,1,0:T(8,128)(2,1)} %get-tuple-element.88), channel_id=1, source_target_pairs={{0,5},{1,4},{2,7},{3,6},{4,1},{5,0},{6,3},{7,2},{8,13},{9,12},{10,... | collective-permute-start | bytes 1548296 | tf_op jit(solution)/shard_map/ppermute | solution.py:262
  363.9 46.7 %collective-permute-start.38 = (bf16[4,504,128]{2,1,0:T(8,128)(2,1)}, bf16[4,504,128]{2,1,0:T(8,128)(2,1)}, u32[]{:S(2)}, u32[]{:S(2)}) collective-permute-start(bf16[4,504,128]{2,1,0:T(8,128)(2,1)} %get-tuple-element.89), channel_id=1, source_target_pairs={{0,6},{1,7},{2,4},{3,5},{4,2},{5,3},{6,0},{7,1},{8,14},{9,15},{10,... | collective-permute-start | bytes 1548296 | tf_op jit(solution)/shard_map/ppermute | solution.py:262
  410.6 45.0 %collective-permute-start.31 = (bf16[5,504,128]{2,1,0:T(8,128)(2,1)}, bf16[5,504,128]{2,1,0:T(8,128)(2,1)}, u32[]{:S(2)}, u32[]{:S(2)}) collective-permute-start(bf16[5,504,128]{2,1,0:T(8,128)(2,1)} %get-tuple-element.82), channel_id=1, source_target_pairs={{0,3},{1,2},{2,1},{3,0},{4,7},{5,6},{6,5},{7,4},{8,11},{9,10},{10,... | collective-permute-start | bytes 1935368 | tf_op jit(solution)/shard_map/ppermute | solution.py:262
  410.7 51.7 %collective-permute-start.32 = (bf16[1,504,128]{2,1,0:T(8,128)(2,1)}, bf16[1,504,128]{2,1,0:T(8,128)(2,1)S(1)}, u32[]{:S(2)}, u32[]{:S(2)}) collective-permute-start(bf16[1,504,128]{2,1,0:T(8,128)(2,1)} %get-tuple-element.83), channel_id=1, source_target_pairs={{0,4},{1,5},{2,6},{3,7},{4,0},{5,1},{6,2},{7,3},{8,12},{9,13},{10,... | collective-permute-start | bytes 387080 | tf_op jit(solution)/shard_map/ppermute | solution.py:262
  419.5 42.9 %collective-permute-start.33 = (bf16[1,504,128]{2,1,0:T(8,128)(2,1)}, bf16[1,504,128]{2,1,0:T(8,128)(2,1)S(1)}, u32[]{:S(2)}, u32[]{:S(2)}) collective-permute-start(bf16[1,504,128]{2,1,0:T(8,128)(2,1)} %get-tuple-element.84), channel_id=1, source_target_pairs={{0,5},{1,4},{2,7},{3,6},{4,1},{5,0},{6,3},{7,2},{8,13},{9,12},{10,... | collective-permute-start | bytes 387080 | tf_op jit(solution)/shard_map/ppermute | solution.py:262
  419.5 42.9 %collective-permute-start.34 = (bf16[1,504,128]{2,1,0:T(8,128)(2,1)}, bf16[1,504,128]{2,1,0:T(8,128)(2,1)S(1)}, u32[]{:S(2)}, u32[]{:S(2)}) collective-permute-start(bf16[1,504,128]{2,1,0:T(8,128)(2,1)} %get-tuple-element.85), channel_id=1, source_target_pairs={{0,6},{1,7},{2,4},{3,5},{4,2},{5,3},{6,0},{7,1},{8,14},{9,15},{10,... | collective-permute-start | bytes 387080 | tf_op jit(solution)/shard_map/ppermute | solution.py:262
  419.5 42.9 %collective-permute-start.35 = (bf16[1,504,128]{2,1,0:T(8,128)(2,1)}, bf16[1,504,128]{2,1,0:T(8,128)(2,1)}, u32[]{:S(2)}, u32[]{:S(2)}) collective-permute-start(bf16[1,504,128]{2,1,0:T(8,128)(2,1)} %get-tuple-element.86), channel_id=1, source_target_pairs={{0,7},{1,6},{2,5},{3,4},{4,3},{5,2},{6,1},{7,0},{8,15},{9,14},{10,... | collective-permute-start | bytes 387080 | tf_op jit(solution)/shard_map/ppermute | solution.py:262
  (46 other events, 452.2 us)

commit v3 on v2

--- a/solution.py
+++ b/solution.py
@@ -9,8 +9,10 @@
 EPS = 1e-6
 THETA = 1000000.0
 N_DEV = 8
-FIRST, MIDDLE, LOCAL, LAST = 3, 7, 11, 15
+FIRST, MIDDLE, LOCAL, LAST = 3, 8, 11, 15
 N_NEW = 4
+
+
 MAIN = 248
 
 
@@ -101,7 +103,7 @@
 
 
 def cache_specs(num_slots, head_dim, first_row):
-    return pl.BlockSpec((1, num_slots, head_dim), lambda i, s: (first_row(s) + i, 0, 0))
+    return pl.BlockSpec((1, num_slots, head_dim), lambda i, s, m: (first_row(m) + i, 0, 0))
 
 
 def pack_blocks(scalars, own, chunk, partners):
@@ -109,9 +111,9 @@
     num_slots, head_dim = own[0].shape[1:]
     count = len(partners)
 
-    def body(scal_ref, *refs):
+    def body(scal_ref, me_ref, *refs):
         key_refs, value_refs, out_refs = refs[:count], refs[count:2 * count], refs[2 * count:]
-        me = scal_ref[128]
+        me = me_ref[0]
         for j, k in enumerate(partners):
             pos = scal_ref[(me ^ k) * 16 + lo + pl.program_id(0)]
             keys, values = without_new(key_refs[j][0], pos), without_new(value_refs[j][0], pos)
@@ -121,48 +123,48 @@
             tail = jnp.where(upper, keys[MAIN:], pltpu.roll(values[MAIN:], N_NEW, 0))
             out_refs[j][0, 2 * MAIN:] = tail.astype(jnp.bfloat16)
 
-    rows = [cache_specs(num_slots, head_dim, lambda s, k=k: (s[128] ^ k) * 16 + lo) for k in partners]
+    rows = [cache_specs(num_slots, head_dim, lambda m, k=k: (m[0] ^ k) * 16 + lo) for k in partners]
     size = 2 * (num_slots - N_NEW)
     return pl.pallas_call(
         body,
         grid_spec=pltpu.PrefetchScalarGridSpec(
-            num_scalar_prefetch=1,
+            num_scalar_prefetch=2,
             grid=(hi - lo,),
             in_specs=rows + rows,
-            out_specs=[pl.BlockSpec((1, size, head_dim), lambda i, s: (i, 0, 0))] * count,
+            out_specs=[pl.BlockSpec((1, size, head_dim), lambda i, s, m: (i, 0, 0))] * count,
         ),
         out_shape=[jax.ShapeDtypeStruct((hi - lo, size, head_dim), jnp.bfloat16)] * count,
         cost_estimate=pl.CostEstimate(flops=(hi - lo) * count * 1_000_000, bytes_accessed=(hi - lo) * count * 260_000, transcendentals=0),
         name="pack_blocks",
-    )(scalars, *[own[0]] * count, *[own[1]] * count)
+    )(*scalars, *[own[0]] * count, *[own[1]] * count)
 
 
 def remote_attend(scalars, caches, packs, offset):
     n_seq = packs[0].shape[0]
     num_slots, head_dim = caches[0].shape[1:]
 
-    def body(scal_ref, *refs):
+    def body(scal_ref, me_ref, *refs):
         key_refs, value_refs = refs[:N_DEV], refs[N_DEV:2 * N_DEV]
         pack_refs, out_refs = refs[2 * N_DEV:3 * N_DEV], refs[3 * N_DEV:]
         seq = pl.program_id(0)
-        me = scal_ref[128]
+        me = me_ref[0]
         for k in range(N_DEV):
             pos = scal_ref[(me ^ k) * 16 + offset + seq]
             out_refs[k][0] = attend_whole(pack_refs[k][0], key_refs[k][0], value_refs[k][0], pos)
 
-    rows = [cache_specs(num_slots, head_dim, lambda s, k=k: (s[128] ^ k) * 16 + offset) for k in range(N_DEV)]
+    rows = [cache_specs(num_slots, head_dim, lambda m, k=k: (m[0] ^ k) * 16 + offset) for k in range(N_DEV)]
     return pl.pallas_call(
         body,
         grid_spec=pltpu.PrefetchScalarGridSpec(
-            num_scalar_prefetch=1,
+            num_scalar_prefetch=2,
             grid=(n_seq,),
-            in_specs=rows + rows + [pl.BlockSpec((1, 24, head_dim), lambda i, s: (i, 0, 0))] * N_DEV,
-            out_specs=[pl.BlockSpec((1, 16, head_dim), lambda i, s: (i, 0, 0))] * N_DEV,
+            in_specs=rows + rows + [pl.BlockSpec((1, 24, head_dim), lambda i, s, m: (i, 0, 0))] * N_DEV,
+            out_specs=[pl.BlockSpec((1, 16, head_dim), lambda i, s, m: (i, 0, 0))] * N_DEV,
         ),
         out_shape=[jax.ShapeDtypeStruct((n_seq, 16, head_dim), jnp.bfloat16)] * N_DEV,
         cost_estimate=pl.CostEstimate(flops=n_seq * 40_000_000, bytes_accessed=n_seq * 1_100_000, transcendentals=0),
         name="remote_attend",
-    )(scalars, *[caches[0]] * N_DEV, *[caches[1]] * N_DEV, *packs)
+    )(*scalars, *[caches[0]] * N_DEV, *[caches[1]] * N_DEV, *packs)
 
 
 def settle(scalars, own, blocks, new_keys, new_values, pack, caches, chunk, num_seqs):
@@ -171,7 +173,7 @@
     with_attn, in_place = pack is not None, caches is not None
     n_steps = new_keys.shape[1]
 
-    def body(scal_ref, *refs):
+    def body(scal_ref, me_ref, *refs):
         refs = list(refs)
         own_refs = [refs.pop(0) for _ in range(2)]
         block_refs = [refs.pop(0) for _ in range(N_DEV - 1)]
@@ -182,7 +184,7 @@
         cache_refs = [refs.pop(0) for _ in range(2)]
         out_ref = refs.pop(0) if with_attn else None
         spread_refs = refs
-        me = scal_ref[128]
+        me = me_ref[0]
         pos = scal_ref[me * 16 + lo + pl.program_id(0)]
 
         for kind in range(2):
@@ -215,16 +217,16 @@
                 else:
                     out_ref[0, me ^ k] = attend_block(pack, block_refs[k - 1].at[0], pos)
 
-    cache_block = pl.BlockSpec((1, num_slots, N_DEV, head_dim), lambda i, s: (lo + i, 0, 0, 0))
-    in_specs = [cache_specs(num_slots, head_dim, lambda s: s[128] * 16 + lo)] * 2
+    cache_block = pl.BlockSpec((1, num_slots, N_DEV, head_dim), lambda i, s, m: (lo + i, 0, 0, 0))
+    in_specs = [cache_specs(num_slots, head_dim, lambda m: m[0] * 16 + lo)] * 2
     in_specs += [
-        pl.BlockSpec((1, 2 * (num_slots - N_NEW), head_dim), lambda i, s, first=lo - first: (first + i, 0, 0))
+        pl.BlockSpec((1, 2 * (num_slots - N_NEW), head_dim), lambda i, s, m, first=lo - first: (first + i, 0, 0))
         for first, _ in blocks
     ]
-    in_specs += [pl.BlockSpec((1, n_steps, N_DEV, head_dim), lambda i, s: (lo + i, 0, 0, 0))] * 2
-    args = [scalars, *own, *[b for _, b in blocks], new_keys, new_values]
+    in_specs += [pl.BlockSpec((1, n_steps, N_DEV, head_dim), lambda i, s, m: (lo + i, 0, 0, 0))] * 2
+    args = [*scalars, *own, *[b for _, b in blocks], new_keys, new_values]
     if with_attn:
-        in_specs.append(pl.BlockSpec((1, N_DEV, 24, head_dim), lambda i, s: (lo + i, 0, 0, 0)))
+        in_specs.append(pl.BlockSpec((1, N_DEV, 24, head_dim), lambda i, s, m: (lo + i, 0, 0, 0)))
         args.append(pack)
     aliases = {}
     if in_place:
@@ -234,12 +236,12 @@
     cache_shape = jax.ShapeDtypeStruct((num_seqs, num_slots, N_DEV, head_dim), jnp.bfloat16)
     out_specs, out_shape = [cache_block] * 2, [cache_shape] * 2
     if with_attn:
-        out_specs.append(pl.BlockSpec((1, N_DEV, 16, head_dim), lambda i, s: (i, 0, 0, 0)))
+        out_specs.append(pl.BlockSpec((1, N_DEV, 16, head_dim), lambda i, s, m: (i, 0, 0, 0)))
         out_shape.append(jax.ShapeDtypeStruct((hi - lo, N_DEV, 16, head_dim), jnp.bfloat16))
     return pl.pallas_call(
         body,
         grid_spec=pltpu.PrefetchScalarGridSpec(
-            num_scalar_prefetch=1,
+            num_scalar_prefetch=2,
             grid=(hi - lo,),
             in_specs=in_specs,
             out_specs=out_specs,
@@ -266,7 +268,7 @@
         n_steps, num_rows = hidden_in.shape[:2]
         num_slots, head_dim = k_heads.shape[1], k_heads.shape[3]
         my_pos = lax.dynamic_slice_in_dim(start_pos, me * num_rows, num_rows)
-        scalars = jnp.concatenate([start_pos, me[None].astype(jnp.int32)])
+        scalars = start_pos, me[None].astype(jnp.int32)
         xor_heads = me ^ jnp.arange(N_DEV)
         own = tuple(c.reshape(N_DEV * num_rows, num_slots, head_dim) for c in (k_heads, v_heads))
 
@@ -284,8 +286,10 @@
             merged = {k: v for part in parts for k, v in part.items()}
             return [merged[k] for k in range(1, N_DEV)]
 
-        blocks = packed(own, 0, FIRST, far)
-        far_first = exchange(blocks, 0)
+        far_first = {}
+        for k in far:
+            blocks = packed(own, 0, FIRST, (k,))
+            far_first.update(exchange(blocks, 0))
         positions = my_pos[None, :] + jnp.arange(n_steps)[:, None]
         queries, keys_new, values_new = project(hidden_in, positions, attn_norm, w_q, w_k, w_v, q_norm, k_norm)
         q_rows = jnp.transpose(queries.reshape(n_steps, num_rows, N_DEV, -1, head_dim), (1, 2, 0, 3, 4)).reshape(num_rows, N_DEV, -1, head_dim)

time: 475 us -> 523 us (1.10)
  starting transfers between devices: 82.8 us -> 109 us
  Pallas kernels: 102 us -> 111 us
  waiting for transfers between devices: 189 us -> 198 us
  local copies, waits for them, and re-layouts: 6.18 us -> 12.2 us
    ppermute x40, starting transfers between devices: 82.8 us -> 109 us  [swap(): return lax.ppermute(value, 'x', [(i, i ^ k) for i in range(N_DEV)])]
    pallas_call x7 -> x10, Pallas kernels: 35.2 us -> 44.6 us  [pack_blocks(): pl.pallas_call(body, grid_spec=pltpu.PrefetchScalarGridSpec(num_scalar_pr...]
    ppermute x40, waiting for transfers between devices: 189 us -> 198 us  [swap(): return lax.ppermute(value, 'x', [(i, i ^ k) for i in range(N_DEV)])]
  transfers between devices with their start and end apart: 40 -> 40, of which waited for: 16 -> 16; matrix products, arithmetic and copies ran while one was open for 19% -> 18% of each run, Pallas kernels for 20% -> 20%
where the time goes in v3:
time: 523 us; the launch traced here: 516 us
  waiting for transfers between devices  198 us (38%)
  Pallas kernels  111 us (21%)
  starting transfers between devices  109 us (21%)
  matrix products  79.6 us (15%)
  local copies, waits for them, and re-layouts  12.2 us (2%)
    ppermute x40, waiting for transfers between devices, swap(): return lax.ppermute(value, 'x', [(i, i ^ k) for i in range(N_DEV)])  198 us
    ppermute x40, starting transfers between devices, swap(): return lax.ppermute(value, 'x', [(i, i ^ k) for i in range(N_DEV)])  109 us
    pallas_call x5, Pallas kernels, settle(): pl.pallas_call(body, grid_spec=pltpu.PrefetchScalarGridSpec(num_scalar_pr...  51.7 us
    pallas_call x10, Pallas kernels, pack_blocks(): pl.pallas_call(body, grid_spec=pltpu.PrefetchScalarGridSpec(num_scalar_pr...  44.6 us
    dot_general x1, matrix products, finish(): jnp.einsum('sbf,fd->sbd', activated, w_down, preferred_element_type=jnp.f...  34.9 us
    dot_general x1, matrix products, finish(): jnp.einsum('sbd,df->sbf', normed, w_gate, preferred_element_type=jnp.floa...  19.6 us
    pallas_call x1, Pallas kernels, remote_attend(): pl.pallas_call(body, grid_spec=pltpu.PrefetchScalarGridSpec(num_scalar_pr...  14.9 us
  transfers between devices with their start and end apart: 40, of which 16 were waited for; matrix products, arithmetic and copies ran while one was open for 18% of the time, Pallas kernels for 20%

profile of v3, /device:TPU:17, one launch (start us, length us, event | category | flops | bytes accessed | tf_op | source)
XLA Modules:
  0.0 515.6 jit_solution(11097976568843018020)
XLA Ops:
  13.4 9.0 %fusion.8 = f32[4,16,4096]{2,1,0:T(8,128)S(1)} fusion(bf16[2560,4096]{1,0:T(8,128)(2,1)} %param.20, bf16[4,16,2560]{2,1,0:T(8,128)(2,1)S(1)} %copy-done.3, f32[2560]{0:T(1024)S(1)} %convert_element_type.53, f32[4,16]{1,0:T(4,128)S(1)} %add_rsqrt_fusion.3), kind=kOutput, calls=%fused_computation.10 | convolution fusion | flops 1342832640 | bytes 22358272 | tf_op jit(solution)/shard_map/sbd,de->sbe/dot_general | solution.py:41
  44.2 33.9 %collective-permute-done.20.refs_22_ = bf16[5,24,128]{2,1,0:T(8,128)(2,1)S(1)} collective-permute-done((bf16[5,24,128]{2,1,0:T(8,128)(2,1)S(1)}, bf16[5,24,128]{2,1,0:T(8,128)(2,1)S(1)}, u32[]{:S(2)}, u32[]{:S(2)}) %collective-permute-start.20) | collective-permute-done | bytes 30752 | tf_op jit(solution)/shard_map/ppermute | solution.py:264
  79.3 14.9 %remote_attend.1 = (bf16[5,16,128]{2,1,0:T(8,128)(2,1)}, bf16[5,16,128]{2,1,0:T(8,128)(2,1)}, bf16[5,16,128]{2,1,0:T(8,128)(2,1)}, bf16[5,16,128]{2,1,0:T(8,128)...) custom-call(s32[128]{0:T(128)} %scal_ref.31, ...), custom_call_target="tpu_custom_call" | custom-call | flops 200000000 | bytes 5500000 | tf_op jit(solution)/shard_map/remote_attend/pallas_call | solution.py:156
  115.7 5.1 pack_blocks.17
  120.8 4.7 pack_blocks.19
  125.5 5.7 %pack_blocks.15 = (bf16[5,504,128]{2,1,0:T(8,128)(2,1)}, bf16[5,504,128]{2,1,0:T(8,128)(2,1)}, bf16[5,504,128]{2,1,0:T(8,128)(2,1)}, bf16[5,504,128]{2,1,0:T(8,128)(2,1)}) custom-call(s32[128]{0:T(128)} %scal_ref.31, s32[1]{0:T(128)} %bitcast.me_ref, bf16[128,256,128]{2,1,0:T(8,128)(2,1)} %bitcast.168, bf16[128,256,128]{2,1,0:T(8,128)(2,1)} %bitcast.169, ...), custom_call_target="tpu_custom_call" | custom-call | flops 20000000 | bytes 5200000 | tf_op jit(solution)/shard_map/pack_blocks/pallas_call | solution.py:128
  131.2 8.8 %pack_blocks.10 = (bf16[11,504,128]{2,1,0:T(8,128)(2,1)}, bf16[11,504,128]{2,1,0:T(8,128)(2,1)}, bf16[11,504,128]{2,1,0:T(8,128)(2,1)}) custom-call(s32[128]{0:T(128)} %scal_ref.31, s32[1]{0:T(128)} %bitcast.me_ref, bf16[128,256,128]{2,1,0:T(8,128)(2,1)} %bitcast.172, bf16[128,256,128]{2,1,0:T(8,128)(2,1)} %bitcast.173, bf16[128,256,128]{2,1,0:T(8,128)(2,1)} %bitcast.174, ...), custom_call_target="tpu_custom_call" | custom-call | flops 33000000 | bytes 8580000 | tf_op jit(solution)/shard_map/pack_blocks/pallas_call | solution.py:128
  146.1 8.8 %collective-permute-done.6.refs_8_ = bf16[3,504,128]{2,1,0:T(8,128)(2,1)S(1)} collective-permute-done((bf16[3,504,128]{2,1,0:T(8,128)(2,1)}, bf16[3,504,128]{2,1,0:T(8,128)(2,1)S(1)}, u32[]{:S(2)}, u32[]{:S(2)}) %collective-permute-start.6) | collective-permute-done | bytes 387104 | tf_op jit(solution)/shard_map/ppermute | solution.py:264
  155.7 60.5 %collective-permute-start.7 = (bf16[5,504,128]{2,1,0:T(8,128)(2,1)}, bf16[5,504,128]{2,1,0:T(8,128)(2,1)S(1)}, u32[]{:S(2)}, u32[]{:S(2)}) collective-permute-start(bf16[5,504,128]{2,1,0:T(8,128)(2,1)} %get-tuple-element.50), channel_id=1, source_target_pairs={{0,4},{1,5},{2,6},{3,7},{4,0},{5,1},{6,2},{7,3},{8,12},{9,13},{10,... | collective-permute-start | bytes 1935368 | tf_op jit(solution)/shard_map/ppermute | solution.py:264
  216.8 11.6 %collective-permute-start.8 = (bf16[5,504,128]{2,1,0:T(8,128)(2,1)}, bf16[5,504,128]{2,1,0:T(8,128)(2,1)S(1)}, u32[]{:S(2)}, u32[]{:S(2)}) collective-permute-start(bf16[5,504,128]{2,1,0:T(8,128)(2,1)} %get-tuple-element.51), channel_id=1, source_target_pairs={{0,5},{1,4},{2,7},{3,6},{4,1},{5,0},{6,3},{7,2},{8,13},{9,12},{10,... | collective-permute-start | bytes 1935368 | tf_op jit(solution)/shard_map/ppermute | solution.py:264
  229.7 37.5 %collective-permute-done.7.refs_5_ = bf16[5,504,128]{2,1,0:T(8,128)(2,1)S(1)} collective-permute-done((bf16[5,504,128]{2,1,0:T(8,128)(2,1)}, bf16[5,504,128]{2,1,0:T(8,128)(2,1)S(1)}, u32[]{:S(2)}, u32[]{:S(2)}) %collective-permute-start.7) | collective-permute-done | bytes 645152 | tf_op jit(solution)/shard_map/ppermute | solution.py:264
  268.4 26.4 %collective-permute-done.8.refs_6_ = bf16[5,504,128]{2,1,0:T(8,128)(2,1)S(1)} collective-permute-done((bf16[5,504,128]{2,1,0:T(8,128)(2,1)}, bf16[5,504,128]{2,1,0:T(8,128)(2,1)S(1)}, u32[]{:S(2)}, u32[]{:S(2)}) %collective-permute-start.8) | collective-permute-done | bytes 645152 | tf_op jit(solution)/shard_map/ppermute | solution.py:264
  302.6 11.7 %settle.5 = (bf16[16,256,8,128]{3,2,1,0:T(8,128)(2,1)}, bf16[16,256,8,128]{3,2,1,0:T(8,128)(2,1)}, bf16[3,8,16,128]{3,2,1,0:T(8,128)(2,1)}) custom-call(s32[128]{0:T(128)} %scal_ref.31, s32[1]{0:T(128)} %bitcast.me_ref, bf16[128,256,128]{2,1,0:T(8,128)(2,1)} %bitcast.175, bf16[128,256,128]{2,1,0:T(8,128)(2,1)} %bitcast.214, bf16[11,504,128]{2,1,0:T(8,128)(2,1)} %copy-done.1, ...), custom_call_target="tpu_custom_call" | custom-call | flops 180000000 | bytes 6600000 | tf_op jit(solution)/shard_map/settle/pallas_call | solution.py:241
  314.3 28.7 %collective-permute-done.9.refs_7_ = bf16[5,504,128]{2,1,0:T(8,128)(2,1)} collective-permute-done((bf16[5,504,128]{2,1,0:T(8,128)(2,1)}, bf16[5,504,128]{2,1,0:T(8,128)(2,1)}, u32[]{:S(2)}, u32[]{:S(2)}) %collective-permute-start.9) | collective-permute-done | bytes 645152 | tf_op jit(solution)/shard_map/ppermute | solution.py:264
  343.4 17.8 %settle.6 = (bf16[16,256,8,128]{3,2,1,0:T(8,128)(2,1)}, bf16[16,256,8,128]{3,2,1,0:T(8,128)(2,1)}, bf16[5,8,16,128]{3,2,1,0:T(8,128)(2,1)}) custom-call(s32[128]{0:T(128)} %scal_ref.31, s32[1]{0:T(128)} %bitcast.me_ref, bf16[128,256,128]{2,1,0:T(8,128)(2,1)} %bitcast.176, ...), custom_call_target="tpu_custom_call", output_to_operand_aliasing={{0}: (14, {}), {1}: (15, {})} | custom-call | flops 300000000 | bytes 11000000 | tf_op jit(solution)/shard_map/settle/pallas_call | solution.py:241
  368.1 8.1 %collective-permute-done.14.refs_8_ = bf16[3,504,128]{2,1,0:T(8,128)(2,1)} collective-permute-done((bf16[3,504,128]{2,1,0:T(8,128)(2,1)}, bf16[3,504,128]{2,1,0:T(8,128)(2,1)}, u32[]{:S(2)}, u32[]{:S(2)}) %collective-permute-start.14) | collective-permute-done | bytes 387104 | tf_op jit(solution)/shard_map/ppermute | solution.py:264
  377.2 11.8 %settle.7 = (bf16[16,256,8,128]{3,2,1,0:T(8,128)(2,1)}, bf16[16,256,8,128]{3,2,1,0:T(8,128)(2,1)}, bf16[3,8,16,128]{3,2,1,0:T(8,128)(2,1)}) custom-call(s32[128]{0:T(128)} %scal_ref.31, s32[1]{0:T(128)} %bitcast.me_ref, bf16[128,256,128]{2,1,0:T(8,128)(2,1)} %bitcast.177, ...), custom_call_target="tpu_custom_call", output_to_operand_aliasing={{0}: (14, {}), {1}: (15, {})} | custom-call | flops 180000000 | bytes 6600000 | tf_op jit(solution)/shard_map/settle/pallas_call | solution.py:241
  390.6 9.0 %multiply_reduce_fusion = (f32[4,16]{1,0:T(4,128)S(1)}, f32[4,16,2560]{2,1,0:T(8,128)S(1)}) fusion(bf16[4,16,4096]{2,1,0:T(8,128)(2,1)S(1)} %reshape.132, bf16[4096,2560]{1,0:T(8,128)(2,1)} %param.25, bf16[4,16,2560]{2,1,0:T(8,128)(2,1)S(1)} %copy-done.4), kind=kOutput, calls=%fused_computation.43 | convolution fusion | flops 1343160320 | bytes 22479104 | tf_op jit(solution)/shard_map/sbe,ed->sbd/dot_general | solution.py:52
  399.6 19.6 %collective-permute-done.36.refs_5_ = bf16[4,504,128]{2,1,0:T(8,128)(2,1)S(1)} collective-permute-done((bf16[4,504,128]{2,1,0:T(8,128)(2,1)S(1)}, bf16[4,504,128]{2,1,0:T(8,128)(2,1)S(1)}, u32[]{:S(2)}, u32[]{:S(2)}) %collective-permute-start.36) | collective-permute-done | bytes 516128 | tf_op jit(solution)/shard_map/ppermute | solution.py:264
  420.0 19.6 %fusion.4 = f32[4,16,9728]{2,1,0:T(8,128)S(1)} fusion(bf16[2560,9728]{1,0:T(8,128)(2,1)} %param.27, f32[4,16,2560]{2,1,0:T(8,128)S(1)} %get-tuple-element.106, f32[2560]{0:T(1024)S(1)} %convert_element_type.62, f32[4,16]{1,0:T(4,128)S(1)} %add_rsqrt_fusion.2), kind=kOutput, calls=%fused_computation.6 | convolution fusion | flops 3188162560 | bytes 52963584 | tf_op jit(solution)/shard_map/sbd,df->sbf/dot_general | solution.py:55
  444.3 9.6 %collective-permute-done.38.refs_7_ = bf16[4,504,128]{2,1,0:T(8,128)(2,1)} collective-permute-done((bf16[4,504,128]{2,1,0:T(8,128)(2,1)}, bf16[4,504,128]{2,1,0:T(8,128)(2,1)}, u32[]{:S(2)}, u32[]{:S(2)}) %collective-permute-start.38) | collective-permute-done | bytes 516128 | tf_op jit(solution)/shard_map/ppermute | solution.py:264
  453.9 13.7 %collective-permute-done.39.refs_8_ = bf16[4,504,128]{2,1,0:T(8,128)(2,1)} collective-permute-done((bf16[4,504,128]{2,1,0:T(8,128)(2,1)}, bf16[4,504,128]{2,1,0:T(8,128)(2,1)}, u32[]{:S(2)}, u32[]{:S(2)}) %collective-permute-start.39) | collective-permute-done | bytes 516128 | tf_op jit(solution)/shard_map/ppermute | solution.py:264
  469.7 34.9 %fusion.30 = bf16[4,16,2560]{2,1,0:T(8,128)(2,1)} fusion(f32[4,16,2560]{2,1,0:T(8,128)S(1)} %get-tuple-element.106, bf16[9728,2560]{1,0:T(8,128)(2,1)} %param.29, bf16[2560,9728]{1,0:T(8,128)(2,1)} %param.28, f32[4,16,9728]{2,1,0:T(8,128)S(1)} %fusion.4, f32[2560]{0:T(1024)S(1)} %convert_element_type.62, f32[4,16]{1,0:T(4,128)S(1)} %add_rsqrt_fusion.2), kind=kOutput, calls=%fused_computation.20 | convolution fusion | flops 6379896832 | bytes 103098624 | tf_op jit(solution)/shard_map/sbf,fd->sbd/dot_general | solution.py:58
  504.6 6.7 %settle.8 = (bf16[16,256,8,128]{3,2,1,0:T(8,128)(2,1)}, bf16[16,256,8,128]{3,2,1,0:T(8,128)(2,1)}) custom-call(s32[128]{0:T(128)} %scal_ref.31, s32[1]{0:T(128)} %bitcast.me_ref, bf16[128,256,128]{2,1,0:T(8,128)(2,1)} %bitcast.178, bf16[128,256,128]{2,1,0:T(8,128)(2,1)} %bitcast.217, ...), custom_call_target="tpu_custom_call", output_to_operand_aliasing={{0}: (13, {}), {1}: (14, {})} | custom-call | flops 240000000 | bytes 8800000 | tf_op jit(solution)/shard_map/settle/pallas_call | solution.py:241
  (196 shorter events, 96.1 us)
Async XLA Ops:
  4.1 138.1 %collective-permute-start.3 = (bf16[3,504,128]{2,1,0:T(8,128)(2,1)}, bf16[3,504,128]{2,1,0:T(8,128)(2,1)}, u32[]{:S(2)}, u32[]{:S(2)}) collective-permute-start(bf16[3,504,128]{2,1,0:T(8,128)(2,1)} %pack_blocks.11), channel_id=1, source_target_pairs={{0,4},{1,5},{2,6},{3,7},{4,0},{5,1},{6,2},{7,3},{8,12},{9,13},{10,... | collective-permute-start | bytes 1161224 | tf_op jit(solution)/shard_map/ppermute | solution.py:264
  39.2 104.0 %collective-permute-start.4 = (bf16[3,504,128]{2,1,0:T(8,128)(2,1)S(1)}, bf16[3,504,128]{2,1,0:T(8,128)(2,1)}, u32[]{:S(2)}, u32[]{:S(2)}) collective-permute-start(bf16[3,504,128]{2,1,0:T(8,128)(2,1)S(1)} %copy-done.9), channel_id=1, source_target_pairs={{0,5},{1,4},{2,7},{3,6},{4,1},{5,0},{6,3},{7,2},{8,13},{9,12},{10,... | collective-permute-start | bytes 1161224 | tf_op jit(solution)/shard_map/ppermute | solution.py:264
  41.6 102.3 %collective-permute-start.5 = (bf16[3,504,128]{2,1,0:T(8,128)(2,1)}, bf16[3,504,128]{2,1,0:T(8,128)(2,1)}, u32[]{:S(2)}, u32[]{:S(2)}) collective-permute-start(bf16[3,504,128]{2,1,0:T(8,128)(2,1)} %pack_blocks.13), channel_id=1, source_target_pairs={{0,6},{1,7},{2,4},{3,5},{4,2},{5,3},{6,0},{7,1},{8,14},{9,15},{10,... | collective-permute-start | bytes 1161224 | tf_op jit(solution)/shard_map/ppermute | solution.py:264
  140.0 157.7 %collective-permute-start = (bf16[11,504,128]{2,1,0:T(8,128)(2,1)}, bf16[11,504,128]{2,1,0:T(8,128)(2,1)S(1)}, u32[]{:S(2)}, u32[]{:S(2)}) collective-permute-start(bf16[11,504,128]{2,1,0:T(8,128)(2,1)} %get-tuple-element.46), channel_id=1, source_target_pairs={{0,1},{1,0},{2,3},{3,2},{4,5},{5,4},{6,7},{7,6},{8,9},{9,8},{10,11... | collective-permute-start | bytes 4257800 | tf_op jit(solution)/shard_map/ppermute | solution.py:264
  140.1 158.1 %collective-permute-start.1 = (bf16[11,504,128]{2,1,0:T(8,128)(2,1)}, bf16[11,504,128]{2,1,0:T(8,128)(2,1)S(1)}, u32[]{:S(2)}, u32[]{:S(2)}) collective-permute-start(bf16[11,504,128]{2,1,0:T(8,128)(2,1)} %get-tuple-element.47), channel_id=1, source_target_pairs={{0,2},{1,3},{2,0},{3,1},{4,6},{5,7},{6,4},{7,5},{8,10},{9,11},{10,... | collective-permute-start | bytes 4257800 | tf_op jit(solution)/shard_map/ppermute | solution.py:264
  142.2 156.7 %collective-permute-start.2 = (bf16[11,504,128]{2,1,0:T(8,128)(2,1)}, bf16[11,504,128]{2,1,0:T(8,128)(2,1)}, u32[]{:S(2)}, u32[]{:S(2)}) collective-permute-start(bf16[11,504,128]{2,1,0:T(8,128)(2,1)} %get-tuple-element.48), channel_id=1, source_target_pairs={{0,3},{1,2},{2,1},{3,0},{4,7},{5,6},{6,5},{7,4},{8,11},{9,10},{10,... | collective-permute-start | bytes 4257800 | tf_op jit(solution)/shard_map/ppermute | solution.py:264
  143.9 72.9 %collective-permute-start.10 = (bf16[5,504,128]{2,1,0:T(8,128)(2,1)}, bf16[5,504,128]{2,1,0:T(8,128)(2,1)S(1)}, u32[]{:S(2)}, u32[]{:S(2)}) collective-permute-start(bf16[5,504,128]{2,1,0:T(8,128)(2,1)} %get-tuple-element.53), channel_id=1, source_target_pairs={{0,7},{1,6},{2,5},{3,4},{4,3},{5,2},{6,1},{7,0},{8,15},{9,14},{10,... | collective-permute-start | bytes 1935368 | tf_op jit(solution)/shard_map/ppermute | solution.py:264
  155.7 111.4 %collective-permute-start.7 = (bf16[5,504,128]{2,1,0:T(8,128)(2,1)}, bf16[5,504,128]{2,1,0:T(8,128)(2,1)S(1)}, u32[]{:S(2)}, u32[]{:S(2)}) collective-permute-start(bf16[5,504,128]{2,1,0:T(8,128)(2,1)} %get-tuple-element.50), channel_id=1, source_target_pairs={{0,4},{1,5},{2,6},{3,7},{4,0},{5,1},{6,2},{7,3},{8,12},{9,13},{10,... | collective-permute-start | bytes 1935368 | tf_op jit(solution)/shard_map/ppermute | solution.py:264
  216.8 78.0 %collective-permute-start.8 = (bf16[5,504,128]{2,1,0:T(8,128)(2,1)}, bf16[5,504,128]{2,1,0:T(8,128)(2,1)S(1)}, u32[]{:S(2)}, u32[]{:S(2)}) collective-permute-start(bf16[5,504,128]{2,1,0:T(8,128)(2,1)} %get-tuple-element.51), channel_id=1, source_target_pairs={{0,5},{1,4},{2,7},{3,6},{4,1},{5,0},{6,3},{7,2},{8,13},{9,12},{10,... | collective-permute-start | bytes 1935368 | tf_op jit(solution)/shard_map/ppermute | solution.py:264
  267.2 75.9 %collective-permute-start.9 = (bf16[5,504,128]{2,1,0:T(8,128)(2,1)}, bf16[5,504,128]{2,1,0:T(8,128)(2,1)}, u32[]{:S(2)}, u32[]{:S(2)}) collective-permute-start(bf16[5,504,128]{2,1,0:T(8,128)(2,1)} %get-tuple-element.52), channel_id=1, source_target_pairs={{0,6},{1,7},{2,4},{3,5},{4,2},{5,3},{6,0},{7,1},{8,14},{9,15},{10,... | collective-permute-start | bytes 1935368 | tf_op jit(solution)/shard_map/ppermute | solution.py:264
  294.8 66.5 %collective-permute-start.11 = (bf16[3,504,128]{2,1,0:T(8,128)(2,1)}, bf16[3,504,128]{2,1,0:T(8,128)(2,1)}, u32[]{:S(2)}, u32[]{:S(2)}) collective-permute-start(bf16[3,504,128]{2,1,0:T(8,128)(2,1)} %get-tuple-element.57), channel_id=1, source_target_pairs={{0,4},{1,5},{2,6},{3,7},{4,0},{5,1},{6,2},{7,3},{8,12},{9,13},{10,... | collective-permute-start | bytes 1161224 | tf_op jit(solution)/shard_map/ppermute | solution.py:264
  297.8 63.6 %collective-permute-start.12 = (bf16[3,504,128]{2,1,0:T(8,128)(2,1)}, bf16[3,504,128]{2,1,0:T(8,128)(2,1)}, u32[]{:S(2)}, u32[]{:S(2)}) collective-permute-start(bf16[3,504,128]{2,1,0:T(8,128)(2,1)} %get-tuple-element.58), channel_id=1, source_target_pairs={{0,5},{1,4},{2,7},{3,6},{4,1},{5,0},{6,3},{7,2},{8,13},{9,12},{10,... | collective-permute-start | bytes 1161224 | tf_op jit(solution)/shard_map/ppermute | solution.py:264
  298.2 69.9 %collective-permute-start.13 = (bf16[3,504,128]{2,1,0:T(8,128)(2,1)}, bf16[3,504,128]{2,1,0:T(8,128)(2,1)}, u32[]{:S(2)}, u32[]{:S(2)}) collective-permute-start(bf16[3,504,128]{2,1,0:T(8,128)(2,1)} %get-tuple-element.59), channel_id=1, source_target_pairs={{0,6},{1,7},{2,4},{3,5},{4,2},{5,3},{6,0},{7,1},{8,14},{9,15},{10,... | collective-permute-start | bytes 1161224 | tf_op jit(solution)/shard_map/ppermute | solution.py:264
  298.8 77.4 %collective-permute-start.14 = (bf16[3,504,128]{2,1,0:T(8,128)(2,1)}, bf16[3,504,128]{2,1,0:T(8,128)(2,1)}, u32[]{:S(2)}, u32[]{:S(2)}) collective-permute-start(bf16[3,504,128]{2,1,0:T(8,128)(2,1)} %get-tuple-element.60), channel_id=1, source_target_pairs={{0,7},{1,6},{2,5},{3,4},{4,3},{5,2},{6,1},{7,0},{8,15},{9,14},{10,... | collective-permute-start | bytes 1161224 | tf_op jit(solution)/shard_map/ppermute | solution.py:264
  343.0 124.5 %collective-permute-start.29 = (bf16[5,504,128]{2,1,0:T(8,128)(2,1)}, bf16[5,504,128]{2,1,0:T(8,128)(2,1)}, u32[]{:S(2)}, u32[]{:S(2)}) collective-permute-start(bf16[5,504,128]{2,1,0:T(8,128)(2,1)} %get-tuple-element.72), channel_id=1, source_target_pairs={{0,1},{1,0},{2,3},{3,2},{4,5},{5,4},{6,7},{7,6},{8,9},{9,8},{10,11... | collective-permute-start | bytes 1935368 | tf_op jit(solution)/shard_map/ppermute | solution.py:264
  361.3 107.2 %collective-permute-start.30 = (bf16[5,504,128]{2,1,0:T(8,128)(2,1)}, bf16[5,504,128]{2,1,0:T(8,128)(2,1)}, u32[]{:S(2)}, u32[]{:S(2)}) collective-permute-start(bf16[5,504,128]{2,1,0:T(8,128)(2,1)} %get-tuple-element.73), channel_id=1, source_target_pairs={{0,2},{1,3},{2,0},{3,1},{4,6},{5,7},{6,4},{7,5},{8,10},{9,11},{10,... | collective-permute-start | bytes 1935368 | tf_op jit(solution)/shard_map/ppermute | solution.py:264
  361.4 57.8 %collective-permute-start.36 = (bf16[4,504,128]{2,1,0:T(8,128)(2,1)S(1)}, bf16[4,504,128]{2,1,0:T(8,128)(2,1)S(1)}, u32[]{:S(2)}, u32[]{:S(2)}) collective-permute-start(bf16[4,504,128]{2,1,0:T(8,128)(2,1)S(1)} %copy-done.30), channel_id=1, source_target_pairs={{0,4},{1,5},{2,6},{3,7},{4,0},{5,1},{6,2},{7,3},{8,12},{9,13},{10,... | collective-permute-start | bytes 1548296 | tf_op jit(solution)/shard_map/ppermute | solution.py:264
  368.1 73.3 %collective-permute-start.37 = (bf16[4,504,128]{2,1,0:T(8,128)(2,1)}, bf16[4,504,128]{2,1,0:T(8,128)(2,1)}, u32[]{:S(2)}, u32[]{:S(2)}) collective-permute-start(bf16[4,504,128]{2,1,0:T(8,128)(2,1)} %get-tuple-element.80), channel_id=1, source_target_pairs={{0,5},{1,4},{2,7},{3,6},{4,1},{5,0},{6,3},{7,2},{8,13},{9,12},{10,... | collective-permute-start | bytes 1548296 | tf_op jit(solution)/shard_map/ppermute | solution.py:264
  376.2 77.6 %collective-permute-start.38 = (bf16[4,504,128]{2,1,0:T(8,128)(2,1)}, bf16[4,504,128]{2,1,0:T(8,128)(2,1)}, u32[]{:S(2)}, u32[]{:S(2)}) collective-permute-start(bf16[4,504,128]{2,1,0:T(8,128)(2,1)} %get-tuple-element.81), channel_id=1, source_target_pairs={{0,6},{1,7},{2,4},{3,5},{4,2},{5,3},{6,0},{7,1},{8,14},{9,15},{10,... | collective-permute-start | bytes 1548296 | tf_op jit(solution)/shard_map/ppermute | solution.py:264
  419.2 48.3 %collective-permute-start.39 = (bf16[4,504,128]{2,1,0:T(8,128)(2,1)}, bf16[4,504,128]{2,1,0:T(8,128)(2,1)}, u32[]{:S(2)}, u32[]{:S(2)}) collective-permute-start(bf16[4,504,128]{2,1,0:T(8,128)(2,1)} %get-tuple-element.82), channel_id=1, source_target_pairs={{0,7},{1,6},{2,5},{3,4},{4,3},{5,2},{6,1},{7,0},{8,15},{9,14},{10,... | collective-permute-start | bytes 1548296 | tf_op jit(solution)/shard_map/ppermute | solution.py:264
  441.4 63.2 %collective-permute-start.31 = (bf16[5,504,128]{2,1,0:T(8,128)(2,1)}, bf16[5,504,128]{2,1,0:T(8,128)(2,1)}, u32[]{:S(2)}, u32[]{:S(2)}) collective-permute-start(bf16[5,504,128]{2,1,0:T(8,128)(2,1)} %get-tuple-element.74), channel_id=1, source_target_pairs={{0,3},{1,2},{2,1},{3,0},{4,7},{5,6},{6,5},{7,4},{8,11},{9,10},{10,... | collective-permute-start | bytes 1935368 | tf_op jit(solution)/shard_map/ppermute | solution.py:264
  453.8 57.5 %collective-permute-start.32 = (bf16[1,504,128]{2,1,0:T(8,128)(2,1)}, bf16[1,504,128]{2,1,0:T(8,128)(2,1)S(1)}, u32[]{:S(2)}, u32[]{:S(2)}) collective-permute-start(bf16[1,504,128]{2,1,0:T(8,128)(2,1)} %get-tuple-element.75), channel_id=1, source_target_pairs={{0,4},{1,5},{2,6},{3,7},{4,0},{5,1},{6,2},{7,3},{8,12},{9,13},{10,... | collective-permute-start | bytes 387080 | tf_op jit(solution)/shard_map/ppermute | solution.py:264
  467.5 43.9 %collective-permute-start.33 = (bf16[1,504,128]{2,1,0:T(8,128)(2,1)}, bf16[1,504,128]{2,1,0:T(8,128)(2,1)S(1)}, u32[]{:S(2)}, u32[]{:S(2)}) collective-permute-start(bf16[1,504,128]{2,1,0:T(8,128)(2,1)} %get-tuple-element.76), channel_id=1, source_target_pairs={{0,5},{1,4},{2,7},{3,6},{4,1},{5,0},{6,3},{7,2},{8,13},{9,12},{10,... | collective-permute-start | bytes 387080 | tf_op jit(solution)/shard_map/ppermute | solution.py:264
  467.5 43.9 %collective-permute-start.34 = (bf16[1,504,128]{2,1,0:T(8,128)(2,1)}, bf16[1,504,128]{2,1,0:T(8,128)(2,1)S(1)}, u32[]{:S(2)}, u32[]{:S(2)}) collective-permute-start(bf16[1,504,128]{2,1,0:T(8,128)(2,1)} %get-tuple-element.77), channel_id=1, source_target_pairs={{0,6},{1,7},{2,4},{3,5},{4,2},{5,3},{6,0},{7,1},{8,14},{9,15},{10,... | collective-permute-start | bytes 387080 | tf_op jit(solution)/shard_map/ppermute | solution.py:264
  (49 other events, 886.6 us)

commit v4 on v3

--- a/solution.py
+++ b/solution.py
@@ -9,7 +9,7 @@
 EPS = 1e-6
 THETA = 1000000.0
 N_DEV = 8
-FIRST, MIDDLE, LOCAL, LAST = 3, 8, 11, 15
+FIRST, MIDDLE, LOCAL, LAST = 3, 9, 11, 15
 N_NEW = 4
 
 
@@ -106,37 +106,40 @@
     return pl.BlockSpec((1, num_slots, head_dim), lambda i, s, m: (first_row(m) + i, 0, 0))
 
 
-def pack_blocks(scalars, own, chunk, partners):
+def pack_blocks(scalars, own, chunk, partners, group):
     lo, hi = chunk
     num_slots, head_dim = own[0].shape[1:]
-    count = len(partners)
+    jobs = [(j, k, g) for j, k in enumerate(partners) for g in range(group)]
 
     def body(scal_ref, me_ref, *refs):
-        key_refs, value_refs, out_refs = refs[:count], refs[count:2 * count], refs[2 * count:]
+        key_refs, value_refs, out_refs = refs[:len(jobs)], refs[len(jobs):2 * len(jobs)], refs[2 * len(jobs):]
         me = me_ref[0]
-        for j, k in enumerate(partners):
-            pos = scal_ref[(me ^ k) * 16 + lo + pl.program_id(0)]
-            keys, values = without_new(key_refs[j][0], pos), without_new(value_refs[j][0], pos)
-            out_refs[j][0, :MAIN] = keys[:MAIN].astype(jnp.bfloat16)
-            out_refs[j][0, MAIN:2 * MAIN] = values[:MAIN].astype(jnp.bfloat16)
+        for (j, k, g), key_ref, value_ref in zip(jobs, key_refs, value_refs):
+            pos = scal_ref[(me ^ k) * 16 + lo + pl.program_id(0) * group + g]
+            keys, values = without_new(key_ref[0], pos), without_new(value_ref[0], pos)
+            out_refs[j][g, :MAIN] = keys[:MAIN].astype(jnp.bfloat16)
+            out_refs[j][g, MAIN:2 * MAIN] = values[:MAIN].astype(jnp.bfloat16)
             upper = lax.broadcasted_iota(jnp.int32, (8, head_dim), 0) < N_NEW
             tail = jnp.where(upper, keys[MAIN:], pltpu.roll(values[MAIN:], N_NEW, 0))
-            out_refs[j][0, 2 * MAIN:] = tail.astype(jnp.bfloat16)
-
-    rows = [cache_specs(num_slots, head_dim, lambda m, k=k: (m[0] ^ k) * 16 + lo) for k in partners]
+            out_refs[j][g, 2 * MAIN:] = tail.astype(jnp.bfloat16)
+
+    rows = [
+        pl.BlockSpec((1, num_slots, head_dim), lambda i, s, m, k=k, g=g: ((m[0] ^ k) * 16 + lo + i * group + g, 0, 0))
+        for _, k, g in jobs
+    ]
     size = 2 * (num_slots - N_NEW)
     return pl.pallas_call(
         body,
         grid_spec=pltpu.PrefetchScalarGridSpec(
             num_scalar_prefetch=2,
-            grid=(hi - lo,),
+            grid=((hi - lo) // group,),
             in_specs=rows + rows,
-            out_specs=[pl.BlockSpec((1, size, head_dim), lambda i, s, m: (i, 0, 0))] * count,
+            out_specs=[pl.BlockSpec((group, size, head_dim), lambda i, s, m: (i, 0, 0))] * len(partners),
         ),
-        out_shape=[jax.ShapeDtypeStruct((hi - lo, size, head_dim), jnp.bfloat16)] * count,
-        cost_estimate=pl.CostEstimate(flops=(hi - lo) * count * 1_000_000, bytes_accessed=(hi - lo) * count * 260_000, transcendentals=0),
+        out_shape=[jax.ShapeDtypeStruct((hi - lo, size, head_dim), jnp.bfloat16)] * len(partners),
+        cost_estimate=pl.CostEstimate(flops=(hi - lo) * len(partners) * 1_000_000, bytes_accessed=(hi - lo) * len(partners) * 260_000, transcendentals=0),
         name="pack_blocks",
-    )(*scalars, *[own[0]] * count, *[own[1]] * count)
+    )(*scalars, *[own[0]] * len(jobs), *[own[1]] * len(jobs))
 
 
 def remote_attend(scalars, caches, packs, offset):
@@ -275,8 +278,8 @@
         def exchange(packed, lo):
             return {k: (lo, swap(block, k)) for k, block in packed.items()}
 
-        def packed(caches, lo, hi, partners):
-            return dict(zip(partners, pack_blocks(scalars, caches, (lo, hi), partners)))
+        def packed(caches, lo, hi, partners, group=1):
+            return dict(zip(partners, pack_blocks(scalars, caches, (lo, hi), partners, group)))
 
         def swap_small(values):
             got = {k: swap(values[k], k) for k in near + far}
@@ -288,7 +291,7 @@
 
         far_first = {}
         for k in far:
-            blocks = packed(own, 0, FIRST, (k,))
+            blocks = packed(own, 0, FIRST, (k,), FIRST)
             far_first.update(exchange(blocks, 0))
         positions = my_pos[None, :] + jnp.arange(n_steps)[:, None]
         queries, keys_new, values_new = project(hidden_in, positions, attn_norm, w_q, w_k, w_v, q_norm, k_norm)
@@ -304,14 +307,18 @@
         local_blocks = packed(own, MIDDLE, LOCAL, far)
         near_local = exchange(near_blocks, 0)
         far_middle = exchange(middle_blocks, FIRST)
-        far_local = exchange(local_blocks, MIDDLE)
+        far_local = {}
+        for k in far:
+            far_local.update(exchange({k: local_blocks[k]}, MIDDLE))
         o_r = remote_attend(scalars, own, got_q, LOCAL)
         got_o = swap_small(o_r)
         near_blocks = packed(own, LOCAL, num_rows, near)
         rest_blocks = packed(own, LOCAL, LAST, far)
         last_blocks = packed(own, LAST, num_rows, far)
         near_rest = exchange(near_blocks, LOCAL)
-        far_rest = exchange(rest_blocks, LOCAL)
+        far_rest = {}
+        for k in far:
+            far_rest.update(exchange({k: rest_blocks[k]}, LOCAL))
         far_last = exchange(last_blocks, LAST)
         *caches, o_a = settle(scalars, own, chosen(near_local, far_first), *new, pack, None, (0, FIRST), num_rows)
         *caches, o_b = settle(scalars, own, chosen(near_local, far_middle), *new, pack, caches, (FIRST, MIDDLE), num_rows)

time: 523 us -> 515 us (0.985)
  starting transfers between devices: 109 us -> 57.2 us
  waiting for transfers between devices: 198 us -> 244 us
    ppermute x40, starting transfers between devices: 109 us -> 57.2 us  [swap(): return lax.ppermute(value, 'x', [(i, i ^ k) for i in range(N_DEV)])]
    ppermute x40, waiting for transfers between devices: 198 us -> 244 us  [swap(): return lax.ppermute(value, 'x', [(i, i ^ k) for i in range(N_DEV)])]
  transfers between devices with their start and end apart: 40 -> 40, of which waited for: 16 -> 19; matrix products, arithmetic and copies ran while one was open for 18% -> 14% of each run, Pallas kernels for 20% -> 20%
where the time goes in v4:
time: 515 us; the launch traced here: 507 us
  waiting for transfers between devices  244 us (47%)
  Pallas kernels  108 us (21%)
  matrix products  77.5 us (15%)
  starting transfers between devices  57.2 us (11%)
  local copies, waits for them, and re-layouts  12.5 us (2%)
  other arithmetic  7.39 us (1%)
    ppermute x40, waiting for transfers between devices, swap(): return lax.ppermute(value, 'x', [(i, i ^ k) for i in range(N_DEV)])  244 us
    ppermute x40, starting transfers between devices, swap(): return lax.ppermute(value, 'x', [(i, i ^ k) for i in range(N_DEV)])  57.2 us
    pallas_call x5, Pallas kernels, settle(): pl.pallas_call(body, grid_spec=pltpu.PrefetchScalarGridSpec(num_scalar_pr...  51.9 us
    pallas_call x10, Pallas kernels, pack_blocks(): pl.pallas_call(body, grid_spec=pltpu.PrefetchScalarGridSpec(num_scalar_pr...  40.8 us
    dot_general x1, matrix products, finish(): jnp.einsum('sbf,fd->sbd', activated, w_down, preferred_element_type=jnp.f...  34.9 us
    dot_general x1, matrix products, finish(): jnp.einsum('sbd,df->sbf', normed, w_gate, preferred_element_type=jnp.floa...  19.6 us
    pallas_call x1, Pallas kernels, remote_attend(): pl.pallas_call(body, grid_spec=pltpu.PrefetchScalarGridSpec(num_scalar_pr...  14.8 us
  transfers between devices with their start and end apart: 40, of which 19 were waited for; matrix products, arithmetic and copies ran while one was open for 14% of the time, Pallas kernels for 20%

profile of v4, /device:TPU:17, one launch (start us, length us, event | category | flops | bytes accessed | tf_op | source)
XLA Modules:
  0.0 507.4 jit_solution(5512676168199808795)
XLA Ops:
  11.2 9.2 %fusion.8 = f32[4,16,4096]{2,1,0:T(8,128)S(1)} fusion(bf16[2560,4096]{1,0:T(8,128)(2,1)} %param.20, bf16[4,16,2560]{2,1,0:T(8,128)(2,1)S(1)} %copy-done.3, f32[2560]{0:T(1024)S(1)} %convert_element_type.53, f32[4,16]{1,0:T(4,128)S(1)} %add_rsqrt_fusion.3), kind=kOutput, calls=%fused_computation.10 | convolution fusion | flops 1342832640 | bytes 22358272 | tf_op jit(solution)/shard_map/sbd,de->sbe/dot_general | solution.py:41
  44.2 53.7 %collective-permute-done.18.refs_20_ = bf16[5,24,128]{2,1,0:T(8,128)(2,1)S(1)} collective-permute-done((bf16[5,24,128]{2,1,0:T(8,128)(2,1)S(1)}, bf16[5,24,128]{2,1,0:T(8,128)(2,1)S(1)}, u32[]{:S(2)}, u32[]{:S(2)}) %collective-permute-start.18) | collective-permute-done | bytes 30752 | tf_op jit(solution)/shard_map/ppermute | solution.py:267
  112.1 14.8 %remote_attend.1 = (bf16[5,16,128]{2,1,0:T(8,128)(2,1)}, bf16[5,16,128]{2,1,0:T(8,128)(2,1)}, bf16[5,16,128]{2,1,0:T(8,128)(2,1)}, bf16[5,16,128]{2,1,0:T(8,128)...) custom-call(s32[128]{0:T(128)} %scal_ref.31, ...), custom_call_target="tpu_custom_call" | custom-call | flops 200000000 | bytes 5500000 | tf_op jit(solution)/shard_map/remote_attend/pallas_call | solution.py:159
  128.4 6.5 %collective-permute-start.23 = (bf16[5,16,128]{2,1,0:T(8,128)(2,1)}, bf16[5,16,128]{2,1,0:T(8,128)(2,1)S(1)}, u32[]{:S(2)}, u32[]{:S(2)}) collective-permute-start(bf16[5,16,128]{2,1,0:T(8,128)(2,1)} %get-tuple-element.66), channel_id=1, source_target_pairs={{0,2},{1,3},{2,0},{3,1},{4,6},{5,7},{6,4},{7,5},{8,10},{9,11},{10,... | collective-permute-start | bytes 61448 | tf_op jit(solution)/shard_map/ppermute | solution.py:267
  154.3 6.2 %pack_blocks.15 = (bf16[6,504,128]{2,1,0:T(8,128)(2,1)}, bf16[6,504,128]{2,1,0:T(8,128)(2,1)}, bf16[6,504,128]{2,1,0:T(8,128)(2,1)}, bf16[6,504,128]{2,1,0:T(8,128)(2,1)}) custom-call(s32[128]{0:T(128)} %scal_ref.31, s32[1]{0:T(128)} %bitcast.me_ref, bf16[128,256,128]{2,1,0:T(8,128)(2,1)} %bitcast.166, bf16[128,256,128]{2,1,0:T(8,128)(2,1)} %bitcast.164, ...), custom_call_target="tpu_custom_call" | custom-call | flops 24000000 | bytes 6240000 | tf_op jit(solution)/shard_map/pack_blocks/pallas_call | solution.py:131
  166.4 5.1 %pack_blocks.17 = (bf16[5,504,128]{2,1,0:T(8,128)(2,1)}, bf16[5,504,128]{2,1,0:T(8,128)(2,1)}, bf16[5,504,128]{2,1,0:T(8,128)(2,1)}) custom-call(s32[128]{0:T(128)} %scal_ref.31, s32[1]{0:T(128)} %bitcast.me_ref, bf16[128,256,128]{2,1,0:T(8,128)(2,1)} %bitcast.177, bf16[128,256,128]{2,1,0:T(8,128)(2,1)} %bitcast.176, bf16[128,256,128]{2,1,0:T(8,128)(2,1)} %bitcast.175, ...), custom_call_target="tpu_custom_call" | custom-call | flops 15000000 | bytes 3900000 | tf_op jit(solution)/shard_map/pack_blocks/pallas_call | solution.py:131
  171.5 4.7 pack_blocks.19
  176.3 8.8 %pack_blocks.10 = (bf16[11,504,128]{2,1,0:T(8,128)(2,1)}, bf16[11,504,128]{2,1,0:T(8,128)(2,1)}, bf16[11,504,128]{2,1,0:T(8,128)(2,1)}) custom-call(s32[128]{0:T(128)} %scal_ref.31, s32[1]{0:T(128)} %bitcast.me_ref, bf16[128,256,128]{2,1,0:T(8,128)(2,1)} %bitcast.182, bf16[128,256,128]{2,1,0:T(8,128)(2,1)} %bitcast.183, bf16[128,256,128]{2,1,0:T(8,128)(2,1)} %bitcast.184, ...), custom_call_target="tpu_custom_call" | custom-call | flops 33000000 | bytes 8580000 | tf_op jit(solution)/shard_map/pack_blocks/pallas_call | solution.py:131
  186.6 5.3 %collective-permute-start.1 = (bf16[11,504,128]{2,1,0:T(8,128)(2,1)}, bf16[11,504,128]{2,1,0:T(8,128)(2,1)S(1)}, u32[]{:S(2)}, u32[]{:S(2)}) collective-permute-start(bf16[11,504,128]{2,1,0:T(8,128)(2,1)} %get-tuple-element.47), channel_id=1, source_target_pairs={{0,2},{1,3},{2,0},{3,1},{4,6},{5,7},{6,4},{7,5},{8,10},{9,11},{10,... | collective-permute-start | bytes 4257800 | tf_op jit(solution)/shard_map/ppermute | solution.py:267
  197.5 71.6 %collective-permute-done.7.refs_5_ = bf16[6,504,128]{2,1,0:T(8,128)(2,1)S(1)} collective-permute-done((bf16[6,504,128]{2,1,0:T(8,128)(2,1)}, bf16[6,504,128]{2,1,0:T(8,128)(2,1)S(1)}, u32[]{:S(2)}, u32[]{:S(2)}) %collective-permute-start.7) | collective-permute-done | bytes 774176 | tf_op jit(solution)/shard_map/ppermute | solution.py:267
  273.5 12.9 %collective-permute-done.8.refs_6_ = bf16[6,504,128]{2,1,0:T(8,128)(2,1)S(1)} collective-permute-done((bf16[6,504,128]{2,1,0:T(8,128)(2,1)}, bf16[6,504,128]{2,1,0:T(8,128)(2,1)S(1)}, u32[]{:S(2)}, u32[]{:S(2)}) %collective-permute-start.8) | collective-permute-done | bytes 774176 | tf_op jit(solution)/shard_map/ppermute | solution.py:267
  291.4 11.2 %collective-permute-done.2.refs_4_ = bf16[11,504,128]{2,1,0:T(8,128)(2,1)} collective-permute-done((bf16[11,504,128]{2,1,0:T(8,128)(2,1)}, bf16[11,504,128]{2,1,0:T(8,128)(2,1)}, u32[]{:S(2)}, u32[]{:S(2)}) %collective-permute-start.2) | collective-permute-done | bytes 1419296 | tf_op jit(solution)/shard_map/ppermute | solution.py:267
  304.9 11.7 %settle.5 = (bf16[16,256,8,128]{3,2,1,0:T(8,128)(2,1)}, bf16[16,256,8,128]{3,2,1,0:T(8,128)(2,1)}, bf16[3,8,16,128]{3,2,1,0:T(8,128)(2,1)}) custom-call(s32[128]{0:T(128)} %scal_ref.31, s32[1]{0:T(128)} %bitcast.me_ref, bf16[128,256,128]{2,1,0:T(8,128)(2,1)} %bitcast.185, bf16[128,256,128]{2,1,0:T(8,128)(2,1)} %bitcast.232, bf16[11,504,128]{2,1,0:T(8,128)(2,1)} %copy-done.1, ...), custom_call_target="tpu_custom_call" | custom-call | flops 180000000 | bytes 6600000 | tf_op jit(solution)/shard_map/settle/pallas_call | solution.py:244
  316.6 25.1 %collective-permute-done.9.refs_7_ = bf16[6,504,128]{2,1,0:T(8,128)(2,1)} collective-permute-done((bf16[6,504,128]{2,1,0:T(8,128)(2,1)}, bf16[6,504,128]{2,1,0:T(8,128)(2,1)}, u32[]{:S(2)}, u32[]{:S(2)}) %collective-permute-start.9) | collective-permute-done | bytes 774176 | tf_op jit(solution)/shard_map/ppermute | solution.py:267
  342.2 21.1 %settle.6 = (bf16[16,256,8,128]{3,2,1,0:T(8,128)(2,1)}, bf16[16,256,8,128]{3,2,1,0:T(8,128)(2,1)}, bf16[6,8,16,128]{3,2,1,0:T(8,128)(2,1)}) custom-call(s32[128]{0:T(128)} %scal_ref.31, s32[1]{0:T(128)} %bitcast.me_ref, bf16[128,256,128]{2,1,0:T(8,128)(2,1)} %bitcast.186, ...), custom_call_target="tpu_custom_call", output_to_operand_aliasing={{0}: (14, {}), {1}: (15, {})} | custom-call | flops 360000000 | bytes 13200000 | tf_op jit(solution)/shard_map/settle/pallas_call | solution.py:244
  368.2 8.9 %settle.7 = (bf16[16,256,8,128]{3,2,1,0:T(8,128)(2,1)}, bf16[16,256,8,128]{3,2,1,0:T(8,128)(2,1)}, bf16[2,8,16,128]{3,2,1,0:T(8,128)(2,1)}) custom-call(s32[128]{0:T(128)} %scal_ref.31, s32[1]{0:T(128)} %bitcast.me_ref, bf16[128,256,128]{2,1,0:T(8,128)(2,1)} %bitcast.187, ...), custom_call_target="tpu_custom_call", output_to_operand_aliasing={{0}: (14, {}), {1}: (15, {})} | custom-call | flops 120000000 | bytes 4400000 | tf_op jit(solution)/shard_map/settle/pallas_call | solution.py:244
  378.7 9.0 %multiply_reduce_fusion = (f32[4,16]{1,0:T(4,128)S(1)}, f32[4,16,2560]{2,1,0:T(8,128)S(1)}) fusion(bf16[4,16,4096]{2,1,0:T(8,128)(2,1)S(1)} %reshape.132, bf16[4096,2560]{1,0:T(8,128)(2,1)} %param.25, bf16[4,16,2560]{2,1,0:T(8,128)(2,1)S(1)} %copy-done.4), kind=kOutput, calls=%fused_computation.43 | convolution fusion | flops 1343160320 | bytes 22479104 | tf_op jit(solution)/shard_map/sbe,ed->sbd/dot_general | solution.py:52
  387.7 5.0 collective-permute-done.36.refs_5_
  393.5 19.6 %fusion.4 = f32[4,16,9728]{2,1,0:T(8,128)S(1)} fusion(bf16[2560,9728]{1,0:T(8,128)(2,1)} %param.27, f32[4,16,2560]{2,1,0:T(8,128)S(1)} %get-tuple-element.106, f32[2560]{0:T(1024)S(1)} %convert_element_type.62, f32[4,16]{1,0:T(4,128)S(1)} %add_rsqrt_fusion.2), kind=kOutput, calls=%fused_computation.6 | convolution fusion | flops 3188162560 | bytes 52963584 | tf_op jit(solution)/shard_map/sbd,df->sbf/dot_general | solution.py:55
  413.1 19.9 %collective-permute-done.37.refs_6_ = bf16[4,504,128]{2,1,0:T(8,128)(2,1)} collective-permute-done((bf16[4,504,128]{2,1,0:T(8,128)(2,1)}, bf16[4,504,128]{2,1,0:T(8,128)(2,1)}, u32[]{:S(2)}, u32[]{:S(2)}) %collective-permute-start.37) | collective-permute-done | bytes 516128 | tf_op jit(solution)/shard_map/ppermute | solution.py:267
  434.5 9.6 %collective-permute-done.38.refs_7_ = bf16[4,504,128]{2,1,0:T(8,128)(2,1)} collective-permute-done((bf16[4,504,128]{2,1,0:T(8,128)(2,1)}, bf16[4,504,128]{2,1,0:T(8,128)(2,1)}, u32[]{:S(2)}, u32[]{:S(2)}) %collective-permute-start.38) | collective-permute-done | bytes 516128 | tf_op jit(solution)/shard_map/ppermute | solution.py:267
  444.1 15.0 %collective-permute-done.39.refs_8_ = bf16[4,504,128]{2,1,0:T(8,128)(2,1)} collective-permute-done((bf16[4,504,128]{2,1,0:T(8,128)(2,1)}, bf16[4,504,128]{2,1,0:T(8,128)(2,1)}, u32[]{:S(2)}, u32[]{:S(2)}) %collective-permute-start.39) | collective-permute-done | bytes 516128 | tf_op jit(solution)/shard_map/ppermute | solution.py:267
  461.5 34.9 %fusion.30 = bf16[4,16,2560]{2,1,0:T(8,128)(2,1)} fusion(f32[4,16,2560]{2,1,0:T(8,128)S(1)} %get-tuple-element.106, bf16[9728,2560]{1,0:T(8,128)(2,1)} %param.29, bf16[2560,9728]{1,0:T(8,128)(2,1)} %param.28, f32[4,16,9728]{2,1,0:T(8,128)S(1)} %fusion.4, f32[2560]{0:T(1024)S(1)} %convert_element_type.62, f32[4,16]{1,0:T(4,128)S(1)} %add_rsqrt_fusion.2), kind=kOutput, calls=%fused_computation.20 | convolution fusion | flops 6379896832 | bytes 103098624 | tf_op jit(solution)/shard_map/sbf,fd->sbd/dot_general | solution.py:58
  496.4 6.7 %settle.8 = (bf16[16,256,8,128]{3,2,1,0:T(8,128)(2,1)}, bf16[16,256,8,128]{3,2,1,0:T(8,128)(2,1)}) custom-call(s32[128]{0:T(128)} %scal_ref.31, s32[1]{0:T(128)} %bitcast.me_ref, bf16[128,256,128]{2,1,0:T(8,128)(2,1)} %bitcast.188, bf16[128,256,128]{2,1,0:T(8,128)(2,1)} %bitcast.235, ...), custom_call_target="tpu_custom_call", output_to_operand_aliasing={{0}: (13, {}), {1}: (14, {})} | custom-call | flops 240000000 | bytes 8800000 | tf_op jit(solution)/shard_map/settle/pallas_call | solution.py:244
  (187 shorter events, 109.5 us)
Async XLA Ops:
  30.1 155.0 %collective-permute-start.3 = (bf16[3,504,128]{2,1,0:T(8,128)(2,1)}, bf16[3,504,128]{2,1,0:T(8,128)(2,1)}, u32[]{:S(2)}, u32[]{:S(2)}) collective-permute-start(bf16[3,504,128]{2,1,0:T(8,128)(2,1)} %pack_blocks.11), channel_id=1, source_target_pairs={{0,4},{1,5},{2,6},{3,7},{4,0},{5,1},{6,2},{7,3},{8,12},{9,13},{10,... | collective-permute-start | bytes 1161224 | tf_op jit(solution)/shard_map/ppermute | solution.py:267
  32.7 153.9 %collective-permute-start.4 = (bf16[3,504,128]{2,1,0:T(8,128)(2,1)}, bf16[3,504,128]{2,1,0:T(8,128)(2,1)}, u32[]{:S(2)}, u32[]{:S(2)}) collective-permute-start(bf16[3,504,128]{2,1,0:T(8,128)(2,1)} %pack_blocks.12), channel_id=1, source_target_pairs={{0,5},{1,4},{2,7},{3,6},{4,1},{5,0},{6,3},{7,2},{8,13},{9,12},{10,... | collective-permute-start | bytes 1161224 | tf_op jit(solution)/shard_map/ppermute | solution.py:267
  38.0 153.9 %collective-permute-start.5 = (bf16[3,504,128]{2,1,0:T(8,128)(2,1)}, bf16[3,504,128]{2,1,0:T(8,128)(2,1)}, u32[]{:S(2)}, u32[]{:S(2)}) collective-permute-start(bf16[3,504,128]{2,1,0:T(8,128)(2,1)} %pack_blocks.13), channel_id=1, source_target_pairs={{0,6},{1,7},{2,4},{3,5},{4,2},{5,3},{6,0},{7,1},{8,14},{9,15},{10,... | collective-permute-start | bytes 1161224 | tf_op jit(solution)/shard_map/ppermute | solution.py:267
  40.8 151.2 %collective-permute-start.6 = (bf16[3,504,128]{2,1,0:T(8,128)(2,1)}, bf16[3,504,128]{2,1,0:T(8,128)(2,1)S(1)}, u32[]{:S(2)}, u32[]{:S(2)}) collective-permute-start(bf16[3,504,128]{2,1,0:T(8,128)(2,1)} %pack_blocks.14), channel_id=1, source_target_pairs={{0,7},{1,6},{2,5},{3,4},{4,3},{5,2},{6,1},{7,0},{8,15},{9,14},{10,... | collective-permute-start | bytes 1161224 | tf_op jit(solution)/shard_map/ppermute | solution.py:267
  42.3 55.6 %collective-permute-start.18 = (bf16[5,24,128]{2,1,0:T(8,128)(2,1)S(1)}, bf16[5,24,128]{2,1,0:T(8,128)(2,1)S(1)}, u32[]{:S(2)}, u32[]{:S(2)}) collective-permute-start(bf16[5,24,128]{2,1,0:T(8,128)(2,1)S(1)} %get-tuple-element.98), channel_id=1, source_target_pairs={{0,4},{1,5},{2,6},{3,7},{4,0},{5,1},{6,2},{7,3},{8,12},{9,13},{10,... | collective-permute-start | bytes 92168 | tf_op jit(solution)/shard_map/ppermute | solution.py:267
  185.1 101.4 %collective-permute-start = (bf16[11,504,128]{2,1,0:T(8,128)(2,1)}, bf16[11,504,128]{2,1,0:T(8,128)(2,1)S(1)}, u32[]{:S(2)}, u32[]{:S(2)}) collective-permute-start(bf16[11,504,128]{2,1,0:T(8,128)(2,1)} %get-tuple-element.46), channel_id=1, source_target_pairs={{0,1},{1,0},{2,3},{3,2},{4,5},{5,4},{6,7},{7,6},{8,9},{9,8},{10,11... | collective-permute-start | bytes 4257800 | tf_op jit(solution)/shard_map/ppermute | solution.py:267
  186.6 102.1 %collective-permute-start.1 = (bf16[11,504,128]{2,1,0:T(8,128)(2,1)}, bf16[11,504,128]{2,1,0:T(8,128)(2,1)S(1)}, u32[]{:S(2)}, u32[]{:S(2)}) collective-permute-start(bf16[11,504,128]{2,1,0:T(8,128)(2,1)} %get-tuple-element.47), channel_id=1, source_target_pairs={{0,2},{1,3},{2,0},{3,1},{4,6},{5,7},{6,4},{7,5},{8,10},{9,11},{10,... | collective-permute-start | bytes 4257800 | tf_op jit(solution)/shard_map/ppermute | solution.py:267
  191.9 110.7 %collective-permute-start.2 = (bf16[11,504,128]{2,1,0:T(8,128)(2,1)}, bf16[11,504,128]{2,1,0:T(8,128)(2,1)}, u32[]{:S(2)}, u32[]{:S(2)}) collective-permute-start(bf16[11,504,128]{2,1,0:T(8,128)(2,1)} %get-tuple-element.48), channel_id=1, source_target_pairs={{0,3},{1,2},{2,1},{3,0},{4,7},{5,6},{6,5},{7,4},{8,11},{9,10},{10,... | collective-permute-start | bytes 4257800 | tf_op jit(solution)/shard_map/ppermute | solution.py:267
  192.0 77.1 %collective-permute-start.7 = (bf16[6,504,128]{2,1,0:T(8,128)(2,1)}, bf16[6,504,128]{2,1,0:T(8,128)(2,1)S(1)}, u32[]{:S(2)}, u32[]{:S(2)}) collective-permute-start(bf16[6,504,128]{2,1,0:T(8,128)(2,1)} %get-tuple-element.50), channel_id=1, source_target_pairs={{0,4},{1,5},{2,6},{3,7},{4,0},{5,1},{6,2},{7,3},{8,12},{9,13},{10,... | collective-permute-start | bytes 2322440 | tf_op jit(solution)/shard_map/ppermute | solution.py:267
  196.8 89.6 %collective-permute-start.8 = (bf16[6,504,128]{2,1,0:T(8,128)(2,1)}, bf16[6,504,128]{2,1,0:T(8,128)(2,1)S(1)}, u32[]{:S(2)}, u32[]{:S(2)}) collective-permute-start(bf16[6,504,128]{2,1,0:T(8,128)(2,1)} %get-tuple-element.51), channel_id=1, source_target_pairs={{0,5},{1,4},{2,7},{3,6},{4,1},{5,0},{6,3},{7,2},{8,13},{9,12},{10,... | collective-permute-start | bytes 2322440 | tf_op jit(solution)/shard_map/ppermute | solution.py:267
  269.1 72.6 %collective-permute-start.9 = (bf16[6,504,128]{2,1,0:T(8,128)(2,1)}, bf16[6,504,128]{2,1,0:T(8,128)(2,1)}, u32[]{:S(2)}, u32[]{:S(2)}) collective-permute-start(bf16[6,504,128]{2,1,0:T(8,128)(2,1)} %get-tuple-element.52), channel_id=1, source_target_pairs={{0,6},{1,7},{2,4},{3,5},{4,2},{5,3},{6,0},{7,1},{8,14},{9,15},{10,... | collective-permute-start | bytes 2322440 | tf_op jit(solution)/shard_map/ppermute | solution.py:267
  286.4 76.9 %collective-permute-start.11 = (bf16[2,504,128]{2,1,0:T(8,128)(2,1)}, bf16[2,504,128]{2,1,0:T(8,128)(2,1)}, u32[]{:S(2)}, u32[]{:S(2)}) collective-permute-start(bf16[2,504,128]{2,1,0:T(8,128)(2,1)} %get-tuple-element.57), channel_id=1, source_target_pairs={{0,4},{1,5},{2,6},{3,7},{4,0},{5,1},{6,2},{7,3},{8,12},{9,13},{10,... | collective-permute-start | bytes 774152 | tf_op jit(solution)/shard_map/ppermute | solution.py:267
  286.4 77.0 %collective-permute-start.12 = (bf16[2,504,128]{2,1,0:T(8,128)(2,1)}, bf16[2,504,128]{2,1,0:T(8,128)(2,1)}, u32[]{:S(2)}, u32[]{:S(2)}) collective-permute-start(bf16[2,504,128]{2,1,0:T(8,128)(2,1)} %get-tuple-element.58), channel_id=1, source_target_pairs={{0,5},{1,4},{2,7},{3,6},{4,1},{5,0},{6,3},{7,2},{8,13},{9,12},{10,... | collective-permute-start | bytes 774152 | tf_op jit(solution)/shard_map/ppermute | solution.py:267
  288.7 78.1 %collective-permute-start.13 = (bf16[2,504,128]{2,1,0:T(8,128)(2,1)}, bf16[2,504,128]{2,1,0:T(8,128)(2,1)}, u32[]{:S(2)}, u32[]{:S(2)}) collective-permute-start(bf16[2,504,128]{2,1,0:T(8,128)(2,1)} %get-tuple-element.59), channel_id=1, source_target_pairs={{0,6},{1,7},{2,4},{3,5},{4,2},{5,3},{6,0},{7,1},{8,14},{9,15},{10,... | collective-permute-start | bytes 774152 | tf_op jit(solution)/shard_map/ppermute | solution.py:267
  302.6 64.4 %collective-permute-start.14 = (bf16[2,504,128]{2,1,0:T(8,128)(2,1)}, bf16[2,504,128]{2,1,0:T(8,128)(2,1)}, u32[]{:S(2)}, u32[]{:S(2)}) collective-permute-start(bf16[2,504,128]{2,1,0:T(8,128)(2,1)} %get-tuple-element.60), channel_id=1, source_target_pairs={{0,7},{1,6},{2,5},{3,4},{4,3},{5,2},{6,1},{7,0},{8,15},{9,14},{10,... | collective-permute-start | bytes 774152 | tf_op jit(solution)/shard_map/ppermute | solution.py:267
  341.7 117.5 %collective-permute-start.29 = (bf16[5,504,128]{2,1,0:T(8,128)(2,1)}, bf16[5,504,128]{2,1,0:T(8,128)(2,1)}, u32[]{:S(2)}, u32[]{:S(2)}) collective-permute-start(bf16[5,504,128]{2,1,0:T(8,128)(2,1)} %get-tuple-element.72), channel_id=1, source_target_pairs={{0,1},{1,0},{2,3},{3,2},{4,5},{5,4},{6,7},{7,6},{8,9},{9,8},{10,11... | collective-permute-start | bytes 1935368 | tf_op jit(solution)/shard_map/ppermute | solution.py:267
  363.3 98.0 %collective-permute-start.30 = (bf16[5,504,128]{2,1,0:T(8,128)(2,1)}, bf16[5,504,128]{2,1,0:T(8,128)(2,1)}, u32[]{:S(2)}, u32[]{:S(2)}) collective-permute-start(bf16[5,504,128]{2,1,0:T(8,128)(2,1)} %get-tuple-element.73), channel_id=1, source_target_pairs={{0,2},{1,3},{2,0},{3,1},{4,6},{5,7},{6,4},{7,5},{8,10},{9,11},{10,... | collective-permute-start | bytes 1935368 | tf_op jit(solution)/shard_map/ppermute | solution.py:267
  366.8 66.3 %collective-permute-start.37 = (bf16[4,504,128]{2,1,0:T(8,128)(2,1)}, bf16[4,504,128]{2,1,0:T(8,128)(2,1)}, u32[]{:S(2)}, u32[]{:S(2)}) collective-permute-start(bf16[4,504,128]{2,1,0:T(8,128)(2,1)} %get-tuple-element.80), channel_id=1, source_target_pairs={{0,5},{1,4},{2,7},{3,6},{4,1},{5,0},{6,3},{7,2},{8,13},{9,12},{10,... | collective-permute-start | bytes 1548296 | tf_op jit(solution)/shard_map/ppermute | solution.py:267
  367.0 77.1 %collective-permute-start.38 = (bf16[4,504,128]{2,1,0:T(8,128)(2,1)}, bf16[4,504,128]{2,1,0:T(8,128)(2,1)}, u32[]{:S(2)}, u32[]{:S(2)}) collective-permute-start(bf16[4,504,128]{2,1,0:T(8,128)(2,1)} %get-tuple-element.81), channel_id=1, source_target_pairs={{0,6},{1,7},{2,4},{3,5},{4,2},{5,3},{6,0},{7,1},{8,14},{9,15},{10,... | collective-permute-start | bytes 1548296 | tf_op jit(solution)/shard_map/ppermute | solution.py:267
  392.7 66.4 %collective-permute-start.39 = (bf16[4,504,128]{2,1,0:T(8,128)(2,1)}, bf16[4,504,128]{2,1,0:T(8,128)(2,1)}, u32[]{:S(2)}, u32[]{:S(2)}) collective-permute-start(bf16[4,504,128]{2,1,0:T(8,128)(2,1)} %get-tuple-element.82), channel_id=1, source_target_pairs={{0,7},{1,6},{2,5},{3,4},{4,3},{5,2},{6,1},{7,0},{8,15},{9,14},{10,... | collective-permute-start | bytes 1548296 | tf_op jit(solution)/shard_map/ppermute | solution.py:267
  433.1 63.3 %collective-permute-start.31 = (bf16[5,504,128]{2,1,0:T(8,128)(2,1)}, bf16[5,504,128]{2,1,0:T(8,128)(2,1)}, u32[]{:S(2)}, u32[]{:S(2)}) collective-permute-start(bf16[5,504,128]{2,1,0:T(8,128)(2,1)} %get-tuple-element.74), channel_id=1, source_target_pairs={{0,3},{1,2},{2,1},{3,0},{4,7},{5,6},{6,5},{7,4},{8,11},{9,10},{10,... | collective-permute-start | bytes 1935368 | tf_op jit(solution)/shard_map/ppermute | solution.py:267
  444.1 59.0 %collective-permute-start.32 = (bf16[1,504,128]{2,1,0:T(8,128)(2,1)}, bf16[1,504,128]{2,1,0:T(8,128)(2,1)S(1)}, u32[]{:S(2)}, u32[]{:S(2)}) collective-permute-start(bf16[1,504,128]{2,1,0:T(8,128)(2,1)} %get-tuple-element.75), channel_id=1, source_target_pairs={{0,4},{1,5},{2,6},{3,7},{4,0},{5,1},{6,2},{7,3},{8,12},{9,13},{10,... | collective-permute-start | bytes 387080 | tf_op jit(solution)/shard_map/ppermute | solution.py:267
  459.1 44.0 %collective-permute-start.33 = (bf16[1,504,128]{2,1,0:T(8,128)(2,1)}, bf16[1,504,128]{2,1,0:T(8,128)(2,1)S(1)}, u32[]{:S(2)}, u32[]{:S(2)}) collective-permute-start(bf16[1,504,128]{2,1,0:T(8,128)(2,1)} %get-tuple-element.76), channel_id=1, source_target_pairs={{0,5},{1,4},{2,7},{3,6},{4,1},{5,0},{6,3},{7,2},{8,13},{9,12},{10,... | collective-permute-start | bytes 387080 | tf_op jit(solution)/shard_map/ppermute | solution.py:267
  459.1 44.0 %collective-permute-start.34 = (bf16[1,504,128]{2,1,0:T(8,128)(2,1)}, bf16[1,504,128]{2,1,0:T(8,128)(2,1)S(1)}, u32[]{:S(2)}, u32[]{:S(2)}) collective-permute-start(bf16[1,504,128]{2,1,0:T(8,128)(2,1)} %get-tuple-element.77), channel_id=1, source_target_pairs={{0,6},{1,7},{2,4},{3,5},{4,2},{5,3},{6,0},{7,1},{8,14},{9,15},{10,... | collective-permute-start | bytes 387080 | tf_op jit(solution)/shard_map/ppermute | solution.py:267
  (45 other events, 680.5 us)

commit v5 on v4

--- a/solution.py
+++ b/solution.py
@@ -9,7 +9,7 @@
 EPS = 1e-6
 THETA = 1000000.0
 N_DEV = 8
-FIRST, MIDDLE, LOCAL, LAST = 3, 9, 11, 15
+FIRST, MIDDLE, LOCAL, LAST = 3, 8, 11, 15
 N_NEW = 4
 
 
@@ -257,6 +257,30 @@
     )(*args)
 
 
+def merge(scalars, local, remote):
+    num_rows = sum(part.shape[0] for part in local) + remote[0].shape[0]
+
+    def body(me_ref, *refs):
+        *parts, out_ref = refs
+        row = 0
+        for part in parts[:len(local)]:
+            out_ref[row:row + part.shape[0]] = part[...]
+            row += part.shape[0]
+        for k, part in enumerate(parts[len(local):]):
+            for seq in range(part.shape[0]):
+                out_ref[row + seq, me_ref[0] ^ k] = part[seq]
+
+    return pl.pallas_call(
+        body,
+        in_specs=[pl.BlockSpec(memory_space=pltpu.SMEM)] + [pl.BlockSpec(memory_space=pltpu.VMEM)] * (len(local) + N_DEV),
+        out_specs=pl.BlockSpec(memory_space=pltpu.VMEM),
+        out_shape=jax.ShapeDtypeStruct((num_rows,) + local[0].shape[1:], jnp.bfloat16),
+        compiler_params=pltpu.CompilerParams(vmem_limit_bytes=8 << 20),
+        cost_estimate=pl.CostEstimate(flops=1_000_000, bytes_accessed=1_000_000, transcendentals=0),
+        name="merge",
+    )(scalars[1], *local, *remote)
+
+
 def solution(mesh):
     row_spec = P(None, ('dp', 'x'), None)
     cache_in = P('dp', None, 'x', None)
@@ -316,15 +340,13 @@
         rest_blocks = packed(own, LOCAL, LAST, far)
         last_blocks = packed(own, LAST, num_rows, far)
         near_rest = exchange(near_blocks, LOCAL)
-        far_rest = {}
-        for k in far:
-            far_rest.update(exchange({k: rest_blocks[k]}, LOCAL))
-        far_last = exchange(last_blocks, LAST)
+        far_last = exchange({far[0]: last_blocks[far[0]]}, LAST)
+        far_rest = exchange(rest_blocks, LOCAL)
+        far_last.update(exchange({k: last_blocks[k] for k in far[1:]}, LAST))
         *caches, o_a = settle(scalars, own, chosen(near_local, far_first), *new, pack, None, (0, FIRST), num_rows)
         *caches, o_b = settle(scalars, own, chosen(near_local, far_middle), *new, pack, caches, (FIRST, MIDDLE), num_rows)
         *caches, o_c = settle(scalars, own, chosen(near_local, far_local), *new, pack, caches, (MIDDLE, LOCAL), num_rows)
-        o_r = jnp.swapaxes(jnp.take(jnp.stack(got_o), xor_heads, axis=0), 0, 1)
-        attended = jnp.concatenate([o_a, o_b, o_c, o_r], axis=0).reshape(num_rows, N_DEV, n_steps, -1, head_dim)
+        attended = merge(scalars, (o_a, o_b, o_c), got_o).reshape(num_rows, N_DEV, n_steps, -1, head_dim)
         attended = jnp.transpose(attended, (2, 0, 1, 3, 4)).reshape(n_steps, num_rows, -1)
         out_hidden = finish(hidden_in, attended, w_o, mlp_norm, w_gate, w_up, w_down)
         caches = settle(scalars, own, chosen(near_rest, far_rest), *new, None, caches, (LOCAL, LAST), num_rows)

time: 515 us -> 520 us (level)
  waiting for transfers between devices: 244 us -> 256 us
  starting transfers between devices: 57.2 us -> 51.1 us
    ppermute x40, waiting for transfers between devices: 244 us -> 256 us  [swap(): return lax.ppermute(value, 'x', [(i, i ^ k) for i in range(N_DEV)])]
    ppermute x40, starting transfers between devices: 57.2 us -> 51.1 us  [swap(): return lax.ppermute(value, 'x', [(i, i ^ k) for i in range(N_DEV)])]
  transfers between devices with their start and end apart: 40 -> 40, of which waited for: 19 -> 15; matrix products, arithmetic and copies ran while one was open for 14% -> 18% of each run, Pallas kernels for 20% -> 19%
where the time goes in v5:
time: 520 us; the launch traced here: 511 us
  waiting for transfers between devices  256 us (49%)
  Pallas kernels  108 us (21%)
  matrix products  79.8 us (15%)
  starting transfers between devices  51.1 us (10%)
  local copies, waits for them, and re-layouts  7.99 us (2%)
  other arithmetic  7.01 us (1%)
    ppermute x40, waiting for transfers between devices, swap(): return lax.ppermute(value, 'x', [(i, i ^ k) for i in range(N_DEV)])  256 us
    pallas_call x5, Pallas kernels, settle(): pl.pallas_call(body, grid_spec=pltpu.PrefetchScalarGridSpec(num_scalar_pr...  51.7 us
    ppermute x40, starting transfers between devices, swap(): return lax.ppermute(value, 'x', [(i, i ^ k) for i in range(N_DEV)])  51.1 us
    pallas_call x10, Pallas kernels, pack_blocks(): pl.pallas_call(body, grid_spec=pltpu.PrefetchScalarGridSpec(num_scalar_pr...  41.6 us
    dot_general x1, matrix products, finish(): jnp.einsum('sbf,fd->sbd', activated, w_down, preferred_element_type=jnp.f...  35 us
    dot_general x1, matrix products, finish(): jnp.einsum('sbd,df->sbf', normed, w_gate, preferred_element_type=jnp.floa...  19.7 us
    pallas_call x1, Pallas kernels, remote_attend(): pl.pallas_call(body, grid_spec=pltpu.PrefetchScalarGridSpec(num_scalar_pr...  14.8 us
  transfers between devices with their start and end apart: 40, of which 15 were waited for; matrix products, arithmetic and copies ran while one was open for 18% of the time, Pallas kernels for 19%

profile of v5, /device:TPU:17, one launch (start us, length us, event | category | flops | bytes accessed | tf_op | source)
XLA Modules:
  0.0 510.8 jit_solution(6130211712690132817)
XLA Ops:
  0.6 8.8 %pack_blocks.10 = (bf16[11,504,128]{2,1,0:T(8,128)(2,1)}, bf16[11,504,128]{2,1,0:T(8,128)(2,1)}, bf16[11,504,128]{2,1,0:T(8,128)(2,1)}) custom-call(s32[128]{0:T(128)} %scal_ref.31, s32[1]{0:T(128)} %bitcast.me_ref, bf16[128,256,128]{2,1,0:T(8,128)(2,1)} %bitcast.124, bf16[128,256,128]{2,1,0:T(8,128)(2,1)} %bitcast.125, bf16[128,256,128]{2,1,0:T(8,128)(2,1)} %bitcast.126, ...), custom_call_target="tpu_custom_call" | custom-call | flops 33000000 | bytes 8580000 | tf_op jit(solution)/shard_map/pack_blocks/pallas_call | solution.py:131
  26.2 9.0 %fusion.8 = f32[4,16,4096]{2,1,0:T(8,128)S(1)} fusion(bf16[2560,4096]{1,0:T(8,128)(2,1)} %param.20, bf16[4,16,2560]{2,1,0:T(8,128)(2,1)S(1)} %copy-done.7, f32[2560]{0:T(1024)S(1)} %convert_element_type.53, f32[4,16]{1,0:T(4,128)S(1)} %add_rsqrt_fusion.3), kind=kOutput, calls=%fused_computation.9 | convolution fusion | flops 1342832640 | bytes 22358272 | tf_op jit(solution)/shard_map/sbd,de->sbe/dot_general | solution.py:41
  45.0 7.1 %collective-permute-done.16.refs_18_ = bf16[5,24,128]{2,1,0:T(8,128)(2,1)S(1)} collective-permute-done((bf16[5,24,128]{2,1,0:T(8,128)(2,1)S(1)}, bf16[5,24,128]{2,1,0:T(8,128)(2,1)S(1)}, u32[]{:S(2)}, u32[]{:S(2)}) %collective-permute-start.16) | collective-permute-done | bytes 30752 | tf_op jit(solution)/shard_map/ppermute | solution.py:291
  62.4 14.8 %remote_attend.1 = (bf16[5,16,128]{2,1,0:T(8,128)(2,1)}, bf16[5,16,128]{2,1,0:T(8,128)(2,1)}, bf16[5,16,128]{2,1,0:T(8,128)(2,1)}, bf16[5,16,128]{2,1,0:T(8,128)...) custom-call(s32[128]{0:T(128)} %scal_ref.31, ...), custom_call_target="tpu_custom_call" | custom-call | flops 200000000 | bytes 5500000 | tf_op jit(solution)/shard_map/remote_attend/pallas_call | solution.py:159
  96.9 33.4 %collective-permute-done.4.refs_6_ = bf16[3,504,128]{2,1,0:T(8,128)(2,1)} collective-permute-done((bf16[3,504,128]{2,1,0:T(8,128)(2,1)}, bf16[3,504,128]{2,1,0:T(8,128)(2,1)}, u32[]{:S(2)}, u32[]{:S(2)}) %collective-permute-start.4) | collective-permute-done | bytes 387104 | tf_op jit(solution)/shard_map/ppermute | solution.py:291
  130.3 8.4 %collective-permute-start.11 = (bf16[3,504,128]{2,1,0:T(8,128)(2,1)}, bf16[3,504,128]{2,1,0:T(8,128)(2,1)}, u32[]{:S(2)}, u32[]{:S(2)}) collective-permute-start(bf16[3,504,128]{2,1,0:T(8,128)(2,1)} %get-tuple-element.57), channel_id=1, source_target_pairs={{0,4},{1,5},{2,6},{3,7},{4,0},{5,1},{6,2},{7,3},{8,12},{9,13},{10,... | collective-permute-start | bytes 1161224 | tf_op jit(solution)/shard_map/ppermute | solution.py:291
  138.6 24.7 %collective-permute-done.6.refs_8_ = bf16[3,504,128]{2,1,0:T(8,128)(2,1)} collective-permute-done((bf16[3,504,128]{2,1,0:T(8,128)(2,1)}, bf16[3,504,128]{2,1,0:T(8,128)(2,1)}, u32[]{:S(2)}, u32[]{:S(2)}) %collective-permute-start.6) | collective-permute-done | bytes 387104 | tf_op jit(solution)/shard_map/ppermute | solution.py:291
  163.3 13.9 %collective-permute-done.11.refs_5_ = bf16[3,504,128]{2,1,0:T(8,128)(2,1)} collective-permute-done((bf16[3,504,128]{2,1,0:T(8,128)(2,1)}, bf16[3,504,128]{2,1,0:T(8,128)(2,1)}, u32[]{:S(2)}, u32[]{:S(2)}) %collective-permute-start.11) | collective-permute-done | bytes 387104 | tf_op jit(solution)/shard_map/ppermute | solution.py:291
  179.2 5.6 %pack_blocks.15 = (bf16[5,504,128]{2,1,0:T(8,128)(2,1)}, bf16[5,504,128]{2,1,0:T(8,128)(2,1)}, bf16[5,504,128]{2,1,0:T(8,128)(2,1)}, bf16[5,504,128]{2,1,0:T(8,128)(2,1)}) custom-call(s32[128]{0:T(128)} %scal_ref.31, s32[1]{0:T(128)} %bitcast.me_ref, bf16[128,256,128]{2,1,0:T(8,128)(2,1)} %bitcast.151, bf16[128,256,128]{2,1,0:T(8,128)(2,1)} %bitcast.152, ...), custom_call_target="tpu_custom_call" | custom-call | flops 20000000 | bytes 5200000 | tf_op jit(solution)/shard_map/pack_blocks/pallas_call | solution.py:131
  184.8 9.0 %collective-permute-done.12.refs_6_ = bf16[3,504,128]{2,1,0:T(8,128)(2,1)} collective-permute-done((bf16[3,504,128]{2,1,0:T(8,128)(2,1)}, bf16[3,504,128]{2,1,0:T(8,128)(2,1)}, u32[]{:S(2)}, u32[]{:S(2)}) %collective-permute-start.12) | collective-permute-done | bytes 387104 | tf_op jit(solution)/shard_map/ppermute | solution.py:291
  196.9 21.7 %collective-permute-done.13.refs_7_ = bf16[3,504,128]{2,1,0:T(8,128)(2,1)} collective-permute-done((bf16[3,504,128]{2,1,0:T(8,128)(2,1)}, bf16[3,504,128]{2,1,0:T(8,128)(2,1)}, u32[]{:S(2)}, u32[]{:S(2)}) %collective-permute-start.13) | collective-permute-done | bytes 387104 | tf_op jit(solution)/shard_map/ppermute | solution.py:291
  223.6 5.1 %pack_blocks.17 = (bf16[5,504,128]{2,1,0:T(8,128)(2,1)}, bf16[5,504,128]{2,1,0:T(8,128)(2,1)}, bf16[5,504,128]{2,1,0:T(8,128)(2,1)}) custom-call(s32[128]{0:T(128)} %scal_ref.31, s32[1]{0:T(128)} %bitcast.me_ref, bf16[128,256,128]{2,1,0:T(8,128)(2,1)} %bitcast.159, bf16[128,256,128]{2,1,0:T(8,128)(2,1)} %bitcast.160, bf16[128,256,128]{2,1,0:T(8,128)(2,1)} %bitcast.161, ...), custom_call_target="tpu_custom_call" | custom-call | flops 15000000 | bytes 3900000 | tf_op jit(solution)/shard_map/pack_blocks/pallas_call | solution.py:131
  233.6 11.8 %settle.5 = (bf16[16,256,8,128]{3,2,1,0:T(8,128)(2,1)}, bf16[16,256,8,128]{3,2,1,0:T(8,128)(2,1)}, bf16[3,8,16,128]{3,2,1,0:T(8,128)(2,1)}) custom-call(s32[128]{0:T(128)} %scal_ref.31, s32[1]{0:T(128)} %bitcast.me_ref, bf16[128,256,128]{2,1,0:T(8,128)(2,1)} %bitcast.166, bf16[128,256,128]{2,1,0:T(8,128)(2,1)} %bitcast.213, bf16[11,504,128]{2,1,0:T(8,128)(2,1)} %copy-done.5, ...), custom_call_target="tpu_custom_call" | custom-call | flops 180000000 | bytes 6600000 | tf_op jit(solution)/shard_map/settle/pallas_call | solution.py:244
  245.4 86.6 %collective-permute-done.14.refs_8_ = bf16[3,504,128]{2,1,0:T(8,128)(2,1)} collective-permute-done((bf16[3,504,128]{2,1,0:T(8,128)(2,1)}, bf16[3,504,128]{2,1,0:T(8,128)(2,1)}, u32[]{:S(2)}, u32[]{:S(2)}) %collective-permute-start.14) | collective-permute-done | bytes 387104 | tf_op jit(solution)/shard_map/ppermute | solution.py:291
  336.5 17.7 %settle.6 = (bf16[16,256,8,128]{3,2,1,0:T(8,128)(2,1)}, bf16[16,256,8,128]{3,2,1,0:T(8,128)(2,1)}, bf16[5,8,16,128]{3,2,1,0:T(8,128)(2,1)}) custom-call(s32[128]{0:T(128)} %scal_ref.31, s32[1]{0:T(128)} %bitcast.me_ref, bf16[128,256,128]{2,1,0:T(8,128)(2,1)} %bitcast.167, ...), custom_call_target="tpu_custom_call", output_to_operand_aliasing={{0}: (14, {}), {1}: (15, {})} | custom-call | flops 300000000 | bytes 11000000 | tf_op jit(solution)/shard_map/settle/pallas_call | solution.py:244
  354.3 11.9 %settle.7 = (bf16[16,256,8,128]{3,2,1,0:T(8,128)(2,1)}, bf16[16,256,8,128]{3,2,1,0:T(8,128)(2,1)}, bf16[3,8,16,128]{3,2,1,0:T(8,128)(2,1)}) custom-call(s32[128]{0:T(128)} %scal_ref.31, s32[1]{0:T(128)} %bitcast.me_ref, bf16[128,256,128]{2,1,0:T(8,128)(2,1)} %bitcast.168, ...), custom_call_target="tpu_custom_call", output_to_operand_aliasing={{0}: (14, {}), {1}: (15, {})} | custom-call | flops 180000000 | bytes 6600000 | tf_op jit(solution)/shard_map/settle/pallas_call | solution.py:244
  374.6 9.0 %multiply_reduce_fusion = (f32[4,16]{1,0:T(4,128)S(1)}, f32[4,16,2560]{2,1,0:T(8,128)S(1)}) fusion(bf16[4,16,4096]{2,1,0:T(8,128)(2,1)S(1)} %reshape.132, bf16[4096,2560]{1,0:T(8,128)(2,1)} %param.25, bf16[4,16,2560]{2,1,0:T(8,128)(2,1)S(1)} %copy-done.8), kind=kOutput, calls=%fused_computation.42 | convolution fusion | flops 1343160320 | bytes 22479104 | tf_op jit(solution)/shard_map/sbe,ed->sbd/dot_general | solution.py:52
  383.6 11.2 %collective-permute-done.36.refs_5_ = bf16[4,504,128]{2,1,0:T(8,128)(2,1)S(1)} collective-permute-done((bf16[4,504,128]{2,1,0:T(8,128)(2,1)S(1)}, bf16[4,504,128]{2,1,0:T(8,128)(2,1)S(1)}, u32[]{:S(2)}, u32[]{:S(2)}) %collective-permute-start.36) | collective-permute-done | bytes 516128 | tf_op jit(solution)/shard_map/ppermute | solution.py:291
  398.3 19.7 %fusion.4 = f32[4,16,9728]{2,1,0:T(8,128)S(1)} fusion(bf16[2560,9728]{1,0:T(8,128)(2,1)} %param.27, f32[4,16,2560]{2,1,0:T(8,128)S(1)} %get-tuple-element.106, f32[2560]{0:T(1024)S(1)} %convert_element_type.62, f32[4,16]{1,0:T(4,128)S(1)} %add_rsqrt_fusion.2), kind=kOutput, calls=%fused_computation.5 | convolution fusion | flops 3188162560 | bytes 52963584 | tf_op jit(solution)/shard_map/sbd,df->sbf/dot_general | solution.py:55
  417.9 18.0 %collective-permute-done.37.refs_6_ = bf16[4,504,128]{2,1,0:T(8,128)(2,1)} collective-permute-done((bf16[4,504,128]{2,1,0:T(8,128)(2,1)}, bf16[4,504,128]{2,1,0:T(8,128)(2,1)}, u32[]{:S(2)}, u32[]{:S(2)}) %collective-permute-start.37) | collective-permute-done | bytes 516128 | tf_op jit(solution)/shard_map/ppermute | solution.py:291
  439.4 9.6 %collective-permute-done.38.refs_7_ = bf16[4,504,128]{2,1,0:T(8,128)(2,1)} collective-permute-done((bf16[4,504,128]{2,1,0:T(8,128)(2,1)}, bf16[4,504,128]{2,1,0:T(8,128)(2,1)}, u32[]{:S(2)}, u32[]{:S(2)}) %collective-permute-start.38) | collective-permute-done | bytes 516128 | tf_op jit(solution)/shard_map/ppermute | solution.py:291
  449.0 15.2 %collective-permute-done.39.refs_8_ = bf16[4,504,128]{2,1,0:T(8,128)(2,1)} collective-permute-done((bf16[4,504,128]{2,1,0:T(8,128)(2,1)}, bf16[4,504,128]{2,1,0:T(8,128)(2,1)}, u32[]{:S(2)}, u32[]{:S(2)}) %collective-permute-start.39) | collective-permute-done | bytes 516128 | tf_op jit(solution)/shard_map/ppermute | solution.py:291
  464.9 35.0 %fusion.30 = bf16[4,16,2560]{2,1,0:T(8,128)(2,1)} fusion(f32[4,16,2560]{2,1,0:T(8,128)S(1)} %get-tuple-element.106, bf16[9728,2560]{1,0:T(8,128)(2,1)} %param.29, bf16[2560,9728]{1,0:T(8,128)(2,1)} %param.28, f32[4,16,9728]{2,1,0:T(8,128)S(1)} %fusion.4, f32[2560]{0:T(1024)S(1)} %convert_element_type.62, f32[4,16]{1,0:T(4,128)S(1)} %add_rsqrt_fusion.2), kind=kOutput, calls=%fused_computation.19 | convolution fusion | flops 6379896832 | bytes 103098624 | tf_op jit(solution)/shard_map/sbf,fd->sbd/dot_general | solution.py:58
  499.8 6.7 %settle.8 = (bf16[16,256,8,128]{3,2,1,0:T(8,128)(2,1)}, bf16[16,256,8,128]{3,2,1,0:T(8,128)(2,1)}) custom-call(s32[128]{0:T(128)} %scal_ref.31, s32[1]{0:T(128)} %bitcast.me_ref, bf16[128,256,128]{2,1,0:T(8,128)(2,1)} %bitcast.169, bf16[128,256,128]{2,1,0:T(8,128)(2,1)} %bitcast.216, ...), custom_call_target="tpu_custom_call", output_to_operand_aliasing={{0}: (13, {}), {1}: (14, {})} | custom-call | flops 240000000 | bytes 8800000 | tf_op jit(solution)/shard_map/settle/pallas_call | solution.py:244
  (184 shorter events, 95.6 us)
Async XLA Ops:
  9.4 209.2 %collective-permute-start = (bf16[11,504,128]{2,1,0:T(8,128)(2,1)}, bf16[11,504,128]{2,1,0:T(8,128)(2,1)S(1)}, u32[]{:S(2)}, u32[]{:S(2)}) collective-permute-start(bf16[11,504,128]{2,1,0:T(8,128)(2,1)} %get-tuple-element.46), channel_id=1, source_target_pairs={{0,1},{1,0},{2,3},{3,2},{4,5},{5,4},{6,7},{7,6},{8,9},{9,8},{10,11... | collective-permute-start | bytes 4257800 | tf_op jit(solution)/shard_map/ppermute | solution.py:291
  10.1 208.6 %collective-permute-start.1 = (bf16[11,504,128]{2,1,0:T(8,128)(2,1)}, bf16[11,504,128]{2,1,0:T(8,128)(2,1)S(1)}, u32[]{:S(2)}, u32[]{:S(2)}) collective-permute-start(bf16[11,504,128]{2,1,0:T(8,128)(2,1)} %get-tuple-element.47), channel_id=1, source_target_pairs={{0,2},{1,3},{2,0},{3,1},{4,6},{5,7},{6,4},{7,5},{8,10},{9,11},{10,... | collective-permute-start | bytes 4257800 | tf_op jit(solution)/shard_map/ppermute | solution.py:291
  14.1 75.9 %collective-permute-start.3 = (bf16[3,504,128]{2,1,0:T(8,128)(2,1)}, bf16[3,504,128]{2,1,0:T(8,128)(2,1)}, u32[]{:S(2)}, u32[]{:S(2)}) collective-permute-start(bf16[3,504,128]{2,1,0:T(8,128)(2,1)} %pack_blocks.11), channel_id=1, source_target_pairs={{0,4},{1,5},{2,6},{3,7},{4,0},{5,1},{6,2},{7,3},{8,12},{9,13},{10,... | collective-permute-start | bytes 1161224 | tf_op jit(solution)/shard_map/ppermute | solution.py:291
  86.4 134.4 %collective-permute-start.2 = (bf16[11,504,128]{2,1,0:T(8,128)(2,1)}, bf16[11,504,128]{2,1,0:T(8,128)(2,1)}, u32[]{:S(2)}, u32[]{:S(2)}) collective-permute-start(bf16[11,504,128]{2,1,0:T(8,128)(2,1)} %get-tuple-element.48), channel_id=1, source_target_pairs={{0,3},{1,2},{2,1},{3,0},{4,7},{5,6},{6,5},{7,4},{8,11},{9,10},{10,... | collective-permute-start | bytes 4257800 | tf_op jit(solution)/shard_map/ppermute | solution.py:291
  86.5 43.8 %collective-permute-start.4 = (bf16[3,504,128]{2,1,0:T(8,128)(2,1)}, bf16[3,504,128]{2,1,0:T(8,128)(2,1)}, u32[]{:S(2)}, u32[]{:S(2)}) collective-permute-start(bf16[3,504,128]{2,1,0:T(8,128)(2,1)} %pack_blocks.12), channel_id=1, source_target_pairs={{0,5},{1,4},{2,7},{3,6},{4,1},{5,0},{6,3},{7,2},{8,13},{9,12},{10,... | collective-permute-start | bytes 1161224 | tf_op jit(solution)/shard_map/ppermute | solution.py:291
  90.0 40.3 %collective-permute-start.5 = (bf16[3,504,128]{2,1,0:T(8,128)(2,1)}, bf16[3,504,128]{2,1,0:T(8,128)(2,1)}, u32[]{:S(2)}, u32[]{:S(2)}) collective-permute-start(bf16[3,504,128]{2,1,0:T(8,128)(2,1)} %pack_blocks.13), channel_id=1, source_target_pairs={{0,6},{1,7},{2,4},{3,5},{4,2},{5,3},{6,0},{7,1},{8,14},{9,15},{10,... | collective-permute-start | bytes 1161224 | tf_op jit(solution)/shard_map/ppermute | solution.py:291
  130.3 47.0 %collective-permute-start.11 = (bf16[3,504,128]{2,1,0:T(8,128)(2,1)}, bf16[3,504,128]{2,1,0:T(8,128)(2,1)}, u32[]{:S(2)}, u32[]{:S(2)}) collective-permute-start(bf16[3,504,128]{2,1,0:T(8,128)(2,1)} %get-tuple-element.57), channel_id=1, source_target_pairs={{0,4},{1,5},{2,6},{3,7},{4,0},{5,1},{6,2},{7,3},{8,12},{9,13},{10,... | collective-permute-start | bytes 1161224 | tf_op jit(solution)/shard_map/ppermute | solution.py:291
  177.2 41.4 %collective-permute-start.13 = (bf16[3,504,128]{2,1,0:T(8,128)(2,1)}, bf16[3,504,128]{2,1,0:T(8,128)(2,1)}, u32[]{:S(2)}, u32[]{:S(2)}) collective-permute-start(bf16[3,504,128]{2,1,0:T(8,128)(2,1)} %get-tuple-element.59), channel_id=1, source_target_pairs={{0,6},{1,7},{2,4},{3,5},{4,2},{5,3},{6,0},{7,1},{8,14},{9,15},{10,... | collective-permute-start | bytes 1161224 | tf_op jit(solution)/shard_map/ppermute | solution.py:291
  193.8 138.2 %collective-permute-start.7 = (bf16[5,504,128]{2,1,0:T(8,128)(2,1)}, bf16[5,504,128]{2,1,0:T(8,128)(2,1)}, u32[]{:S(2)}, u32[]{:S(2)}) collective-permute-start(bf16[5,504,128]{2,1,0:T(8,128)(2,1)} %get-tuple-element.50), channel_id=1, source_target_pairs={{0,4},{1,5},{2,6},{3,7},{4,0},{5,1},{6,2},{7,3},{8,12},{9,13},{10,... | collective-permute-start | bytes 1935368 | tf_op jit(solution)/shard_map/ppermute | solution.py:291
  218.6 114.3 %collective-permute-start.8 = (bf16[5,504,128]{2,1,0:T(8,128)(2,1)}, bf16[5,504,128]{2,1,0:T(8,128)(2,1)}, u32[]{:S(2)}, u32[]{:S(2)}) collective-permute-start(bf16[5,504,128]{2,1,0:T(8,128)(2,1)} %get-tuple-element.51), channel_id=1, source_target_pairs={{0,5},{1,4},{2,7},{3,6},{4,1},{5,0},{6,3},{7,2},{8,13},{9,12},{10,... | collective-permute-start | bytes 1935368 | tf_op jit(solution)/shard_map/ppermute | solution.py:291
  218.6 116.4 %collective-permute-start.9 = (bf16[5,504,128]{2,1,0:T(8,128)(2,1)}, bf16[5,504,128]{2,1,0:T(8,128)(2,1)}, u32[]{:S(2)}, u32[]{:S(2)}) collective-permute-start(bf16[5,504,128]{2,1,0:T(8,128)(2,1)} %get-tuple-element.52), channel_id=1, source_target_pairs={{0,6},{1,7},{2,4},{3,5},{4,2},{5,3},{6,0},{7,1},{8,14},{9,15},{10,... | collective-permute-start | bytes 1935368 | tf_op jit(solution)/shard_map/ppermute | solution.py:291
  218.7 116.3 %collective-permute-start.10 = (bf16[5,504,128]{2,1,0:T(8,128)(2,1)}, bf16[5,504,128]{2,1,0:T(8,128)(2,1)}, u32[]{:S(2)}, u32[]{:S(2)}) collective-permute-start(bf16[5,504,128]{2,1,0:T(8,128)(2,1)} %get-tuple-element.53), channel_id=1, source_target_pairs={{0,7},{1,6},{2,5},{3,4},{4,3},{5,2},{6,1},{7,0},{8,15},{9,14},{10,... | collective-permute-start | bytes 1935368 | tf_op jit(solution)/shard_map/ppermute | solution.py:291
  220.9 111.1 %collective-permute-start.14 = (bf16[3,504,128]{2,1,0:T(8,128)(2,1)}, bf16[3,504,128]{2,1,0:T(8,128)(2,1)}, u32[]{:S(2)}, u32[]{:S(2)}) collective-permute-start(bf16[3,504,128]{2,1,0:T(8,128)(2,1)} %get-tuple-element.60), channel_id=1, source_target_pairs={{0,7},{1,6},{2,5},{3,4},{4,3},{5,2},{6,1},{7,0},{8,15},{9,14},{10,... | collective-permute-start | bytes 1161224 | tf_op jit(solution)/shard_map/ppermute | solution.py:291
  335.0 38.0 %collective-permute-start.28 = (bf16[5,16,128]{2,1,0:T(8,128)(2,1)S(1)}, bf16[5,16,128]{2,1,0:T(8,128)(2,1)S(1)}, u32[]{:S(2)}, u32[]{:S(2)}) collective-permute-start(bf16[5,16,128]{2,1,0:T(8,128)(2,1)S(1)} %copy-done.25), channel_id=1, source_target_pairs={{0,7},{1,6},{2,5},{3,4},{4,3},{5,2},{6,1},{7,0},{8,15},{9,14},{10,... | collective-permute-start | bytes 61448 | tf_op jit(solution)/shard_map/ppermute | solution.py:291
  366.1 98.1 %collective-permute-start.29 = (bf16[5,504,128]{2,1,0:T(8,128)(2,1)}, bf16[5,504,128]{2,1,0:T(8,128)(2,1)}, u32[]{:S(2)}, u32[]{:S(2)}) collective-permute-start(bf16[5,504,128]{2,1,0:T(8,128)(2,1)} %get-tuple-element.72), channel_id=1, source_target_pairs={{0,1},{1,0},{2,3},{3,2},{4,5},{5,4},{6,7},{7,6},{8,9},{9,8},{10,11... | collective-permute-start | bytes 1935368 | tf_op jit(solution)/shard_map/ppermute | solution.py:291
  366.6 97.9 %collective-permute-start.30 = (bf16[5,504,128]{2,1,0:T(8,128)(2,1)}, bf16[5,504,128]{2,1,0:T(8,128)(2,1)}, u32[]{:S(2)}, u32[]{:S(2)}) collective-permute-start(bf16[5,504,128]{2,1,0:T(8,128)(2,1)} %get-tuple-element.73), channel_id=1, source_target_pairs={{0,2},{1,3},{2,0},{3,1},{4,6},{5,7},{6,4},{7,5},{8,10},{9,11},{10,... | collective-permute-start | bytes 1935368 | tf_op jit(solution)/shard_map/ppermute | solution.py:291
  369.8 66.2 %collective-permute-start.37 = (bf16[4,504,128]{2,1,0:T(8,128)(2,1)}, bf16[4,504,128]{2,1,0:T(8,128)(2,1)}, u32[]{:S(2)}, u32[]{:S(2)}) collective-permute-start(bf16[4,504,128]{2,1,0:T(8,128)(2,1)} %get-tuple-element.80), channel_id=1, source_target_pairs={{0,5},{1,4},{2,7},{3,6},{4,1},{5,0},{6,3},{7,2},{8,13},{9,12},{10,... | collective-permute-start | bytes 1548296 | tf_op jit(solution)/shard_map/ppermute | solution.py:291
  373.0 76.0 %collective-permute-start.38 = (bf16[4,504,128]{2,1,0:T(8,128)(2,1)}, bf16[4,504,128]{2,1,0:T(8,128)(2,1)}, u32[]{:S(2)}, u32[]{:S(2)}) collective-permute-start(bf16[4,504,128]{2,1,0:T(8,128)(2,1)} %get-tuple-element.81), channel_id=1, source_target_pairs={{0,6},{1,7},{2,4},{3,5},{4,2},{5,3},{6,0},{7,1},{8,14},{9,15},{10,... | collective-permute-start | bytes 1548296 | tf_op jit(solution)/shard_map/ppermute | solution.py:291
  394.8 69.4 %collective-permute-start.39 = (bf16[4,504,128]{2,1,0:T(8,128)(2,1)}, bf16[4,504,128]{2,1,0:T(8,128)(2,1)}, u32[]{:S(2)}, u32[]{:S(2)}) collective-permute-start(bf16[4,504,128]{2,1,0:T(8,128)(2,1)} %get-tuple-element.82), channel_id=1, source_target_pairs={{0,7},{1,6},{2,5},{3,4},{4,3},{5,2},{6,1},{7,0},{8,15},{9,14},{10,... | collective-permute-start | bytes 1548296 | tf_op jit(solution)/shard_map/ppermute | solution.py:291
  436.0 63.9 %collective-permute-start.31 = (bf16[5,504,128]{2,1,0:T(8,128)(2,1)}, bf16[5,504,128]{2,1,0:T(8,128)(2,1)}, u32[]{:S(2)}, u32[]{:S(2)}) collective-permute-start(bf16[5,504,128]{2,1,0:T(8,128)(2,1)} %get-tuple-element.74), channel_id=1, source_target_pairs={{0,3},{1,2},{2,1},{3,0},{4,7},{5,6},{6,5},{7,4},{8,11},{9,10},{10,... | collective-permute-start | bytes 1935368 | tf_op jit(solution)/shard_map/ppermute | solution.py:291
  449.0 57.6 %collective-permute-start.32 = (bf16[1,504,128]{2,1,0:T(8,128)(2,1)}, bf16[1,504,128]{2,1,0:T(8,128)(2,1)S(1)}, u32[]{:S(2)}, u32[]{:S(2)}) collective-permute-start(bf16[1,504,128]{2,1,0:T(8,128)(2,1)} %get-tuple-element.75), channel_id=1, source_target_pairs={{0,4},{1,5},{2,6},{3,7},{4,0},{5,1},{6,2},{7,3},{8,12},{9,13},{10,... | collective-permute-start | bytes 387080 | tf_op jit(solution)/shard_map/ppermute | solution.py:291
  464.2 42.3 %collective-permute-start.33 = (bf16[1,504,128]{2,1,0:T(8,128)(2,1)}, bf16[1,504,128]{2,1,0:T(8,128)(2,1)S(1)}, u32[]{:S(2)}, u32[]{:S(2)}) collective-permute-start(bf16[1,504,128]{2,1,0:T(8,128)(2,1)} %get-tuple-element.76), channel_id=1, source_target_pairs={{0,5},{1,4},{2,7},{3,6},{4,1},{5,0},{6,3},{7,2},{8,13},{9,12},{10,... | collective-permute-start | bytes 387080 | tf_op jit(solution)/shard_map/ppermute | solution.py:291
  464.2 42.4 %collective-permute-start.34 = (bf16[1,504,128]{2,1,0:T(8,128)(2,1)}, bf16[1,504,128]{2,1,0:T(8,128)(2,1)}, u32[]{:S(2)}, u32[]{:S(2)}) collective-permute-start(bf16[1,504,128]{2,1,0:T(8,128)(2,1)} %get-tuple-element.77), channel_id=1, source_target_pairs={{0,6},{1,7},{2,4},{3,5},{4,2},{5,3},{6,0},{7,1},{8,14},{9,15},{10,... | collective-permute-start | bytes 387080 | tf_op jit(solution)/shard_map/ppermute | solution.py:291
  464.5 42.2 %collective-permute-start.35 = (bf16[1,504,128]{2,1,0:T(8,128)(2,1)}, bf16[1,504,128]{2,1,0:T(8,128)(2,1)}, u32[]{:S(2)}, u32[]{:S(2)}) collective-permute-start(bf16[1,504,128]{2,1,0:T(8,128)(2,1)} %get-tuple-element.78), channel_id=1, source_target_pairs={{0,7},{1,6},{2,5},{3,4},{4,3},{5,2},{6,1},{7,0},{8,15},{9,14},{10,... | collective-permute-start | bytes 387080 | tf_op jit(solution)/shard_map/ppermute | solution.py:291
  (48 other events, 1028.7 us)
